TPU v7x, 32 devices: a whole 2x2x4 slice. The times are simulated.
32 devices in a mesh: nest: 4 (over x, core), py: 2 (over y), px: 4 (over z).
Axes of the slice: x: 2, y: 2, z: 4, core: 2. Of those that a mesh axis runs over, the one named last changes fastest.
Arguments:
- initial_state: float32 [4, 4, 256, 256], P('nest', None, 'px', 'py'), may hold values from -6 to 6
- drive_modes: float32 [3, 4, 64, 64], replicated, may hold values from -6 to 6
- relax_rates: float32 [4, 4], P('nest'), may hold values from 0.2 to 0.9
- nest_offsets: int32 [4, 2], replicated, may hold values from 0 to 170
Outputs:
- final_state: float32 [4, 4, 256, 256], P('nest', None, 'px', 'py')
- final_modes: float32 [4, 4, 64, 64], P('nest')
Inputs may be any that keep to these rules, and one draw needn't show every extreme that they name: `nest_offsets`: row 0 is not read.
All inputs are finite; a program needn't handle non-finite values.
Results may differ from a plain program's by a relative error of at most 0.0001.
Values sent between devices are 32-bit elements; how exact they have to be, the bound alone decides.
No kernel may reach another device: no remote copies, remote signals or barrier semaphores. Data moves between devices by JAX's collectives and lax.ppermute only.
A program may use at most 64 MiB of HBM per device.

v0:
```python
import jax
import jax.numpy as jnp
from jax import lax
from jax.sharding import PartitionSpec as P

RATIO = 3


highest = lax.Precision.HIGHEST
diffusion_rate = 0.2


def shifted(block, axis, distance):
    devices = range(lax.axis_size(axis))
    route = [(i - distance, i) for i in devices if i - distance in devices]
    return lax.ppermute(block, axis, route)


def padded_2(value, sides, width):
    for axis, dim in sides:
        devices, length = (lax.axis_size(axis), value.shape[dim])
        up = [(i, (i + 1) % devices) for i in range(devices - 1)]
        down = [(j, i) for i, j in up]
        last = lax.slice_in_dim(value, length - width, length, axis=dim)
        first = lax.slice_in_dim(value, 0, width, axis=dim)
        before = lax.ppermute(last, axis, up)
        after = lax.ppermute(first, axis, down)
        value = jnp.concatenate([before, value, after], axis=dim)
    return value


def cosine_basis(numerator, cell_count, mode_count, refine):
    wavenum = jnp.arange(mode_count, dtype=jnp.int32)
    product = wavenum[None, :] * numerator[:, None] % (4 * refine * cell_count)
    angles = jnp.pi * product.astype(jnp.float32) / (2.0 * refine * cell_count)
    weight = jnp.where(wavenum == 0, 1.0, 2.0).astype(jnp.float32) / cell_count
    return jnp.sqrt(weight)[None, :] * jnp.cos(angles)


def parent_of(coeffs):
    moved = shifted(coeffs, "nest", 1)
    return moved


def advance(
    field_now, parent, drive_now, gain_levels, row_local, col_local, row_map, col_map, is_root
):
    padded = padded_2(field_now, (("py", 3), ("px", 2)), 1)
    beside_all = (
        padded[:, :, 2:, 1:-1]
        + padded[:, :, :-2, 1:-1]
        + padded[:, :, 1:-1, 2:]
        + padded[:, :, 1:-1, :-2]
    )
    stepped = field_now + diffusion_rate * (beside_all - 4.0 * field_now)
    partial_rows = jnp.einsum("lxy,ym->lxm", stepped[0], col_local, precision=highest)
    partial_sum = jnp.einsum("xj,lxm->ljm", row_local, partial_rows, precision=highest)
    interp = jnp.einsum("jp,lpq,mq->ljm", row_map, parent, col_map, precision=highest)
    target = jnp.where(is_root, drive_now, interp)
    own = lax.psum(partial_sum, ("py", "px"))
    change = gain_levels[:, None, None] * (target - own)
    coeffs = own + change
    back_rows = jnp.einsum("ljm,ym->ljy", change, col_local, precision=highest)
    field_new = stepped + jnp.einsum("xj,ljy->lxy", row_local, back_rows, precision=highest)[None]
    return (field_new, coeffs)


def body(initial_state, drive_modes, relax_rates, nest_offsets):
    nest_index = lax.axis_index("nest")
    nest_count = lax.axis_size("nest")
    cells_x = initial_state.shape[2]
    cells_y = initial_state.shape[3]
    levels = initial_state.shape[1]
    mode_count = drive_modes.shape[2]
    window_count = drive_modes.shape[0]
    total_x = cells_x * lax.axis_size("px")
    total_y = cells_y * lax.axis_size("py")
    global_x = jnp.arange(total_x, dtype=jnp.int32)
    global_y = jnp.arange(total_y, dtype=jnp.int32)
    row_full = cosine_basis(2 * global_x + 1, total_x, mode_count, 1)
    col_full = cosine_basis(2 * global_y + 1, total_y, mode_count, 1)
    local_x = lax.axis_index("px") * cells_x + jnp.arange(cells_x, dtype=jnp.int32)
    local_y = lax.axis_index("py") * cells_y + jnp.arange(cells_y, dtype=jnp.int32)
    row_local = cosine_basis(2 * local_x + 1, total_x, mode_count, 1)
    col_local = cosine_basis(2 * local_y + 1, total_y, mode_count, 1)
    offset_x = nest_offsets[nest_index, 0]
    offset_y = nest_offsets[nest_index, 1]
    row_map = jnp.dot(
        row_full.T,
        cosine_basis(2 * RATIO * offset_x + 2 * global_x + 1, total_x, mode_count, RATIO),
        precision=highest,
    )
    col_map = jnp.dot(
        col_full.T,
        cosine_basis(2 * RATIO * offset_y + 2 * global_y + 1, total_y, mode_count, RATIO),
        precision=highest,
    )
    gain_levels = relax_rates[0]
    is_root = nest_index == 0
    field_now = initial_state
    coeffs = jnp.zeros((levels, mode_count, mode_count), jnp.float32)
    for tick_index in range(window_count + nest_count - 1):
        parent = parent_of(coeffs)
        window = tick_index - nest_index
        active = (window >= 0) & (window < window_count)
        drive_now = lax.dynamic_index_in_dim(
            drive_modes, jnp.clip(window, 0, window_count - 1), 0, keepdims=False
        )
        field_new, coeff_new = advance(
            field_now,
            parent,
            drive_now,
            gain_levels,
            row_local,
            col_local,
            row_map,
            col_map,
            is_root,
        )
        field_now = jnp.where(active, field_new, field_now)
        coeffs = jnp.where(active, coeff_new, coeffs)
    return (field_now, coeffs[None])


def solution(mesh):
    placed = (P("nest", None, "px", "py"), P(), P("nest", None), P())
    return jax.shard_map(
        body,
        mesh=mesh,
        in_specs=placed,
        out_specs=(P("nest", None, "px", "py"), P("nest", None, None, None)),
        check_vma=False,
    )
```

profile of v0, /device:TPU:0, one launch (start us, length us, event | category | flops | bytes accessed | tf_op | source)
XLA Modules:
  0.0 578.2 jit_solution(15255747016439641226)
XLA Ops:
  7.2 2.4 collective-permute-start.4
  9.8 4.2 collective-permute-start
  14.0 1.3 collective-permute-start.1
  17.9 1.3 convolution_bitcast_fusion.13
  19.2 1.3 convolution_bitcast_fusion.12
  20.6 1.2 collective-permute-done.1
  21.9 1.3 collective-permute-start.2
  23.2 4.5 collective-permute-start.3
  27.7 1.3 collective-permute-done.3
  30.1 1.4 convolution_bitcast_fusion.11
  31.8 72.3 %all-reduce.7.cloned.1.call-done = f32[4,64,64]{2,1,0:T(8,128)} async-done(((f32[4,64,64]{2,1,0:T(8,128)}), f32[4,64,64]{2,1,0:T(8,128)}) %all-reduce.7.cloned.1.call-update) | async-done | bytes 65552 | tf_op jit(solution)/shard_map/psum | solution.py:60
  104.1 1.2 add_select_fusion.7
  106.4 2.5 collective-permute-start.5
  108.9 1.3 collective-permute-start.6
  110.2 1.2 collective-permute-done.5
  111.4 4.4 collective-permute-done.6
  115.9 1.3 collective-permute-start.7
  117.2 4.5 collective-permute-start.8
  121.8 1.3 collective-permute-start.9
  124.2 1.4 convolution_bitcast_fusion.9
  125.9 71.0 %all-reduce.9.cloned.1.call-done = f32[4,64,64]{2,1,0:T(8,128)} async-done(((f32[4,64,64]{2,1,0:T(8,128)}), f32[4,64,64]{2,1,0:T(8,128)}) %all-reduce.9.cloned.1.call-update) | async-done | bytes 65552 | tf_op jit(solution)/shard_map/psum | solution.py:60
  196.9 1.2 add_select_fusion.6
  199.2 2.5 collective-permute-start.10
  201.7 1.3 collective-permute-start.11
  203.0 1.2 collective-permute-done.10
  204.2 4.4 collective-permute-done.11
  208.7 1.3 collective-permute-start.12
  210.0 4.5 collective-permute-start.13
  214.5 1.3 collective-permute-start.14
  216.9 1.4 convolution_bitcast_fusion.7
  218.6 71.0 %all-reduce.11.cloned.1.call-done = f32[4,64,64]{2,1,0:T(8,128)} async-done(((f32[4,64,64]{2,1,0:T(8,128)}), f32[4,64,64]{2,1,0:T(8,128)}) %all-reduce.11.cloned.1.call-update) | async-done | bytes 65552 | tf_op jit(solution)/shard_map/psum | solution.py:60
  289.6 1.2 add_select_fusion.5
  291.9 2.5 collective-permute-start.15
  294.4 1.3 collective-permute-start.16
  295.7 1.2 collective-permute-done.15
  296.9 4.4 collective-permute-done.16
  301.4 1.3 collective-permute-start.17
  302.7 4.5 collective-permute-start.18
  307.3 1.5 collective-permute-start.19
  309.8 1.4 convolution_bitcast_fusion.5
  311.5 70.8 %all-reduce.13.cloned.1.call-done = f32[4,64,64]{2,1,0:T(8,128)} async-done(((f32[4,64,64]{2,1,0:T(8,128)}), f32[4,64,64]{2,1,0:T(8,128)}) %all-reduce.13.cloned.1.call-update) | async-done | bytes 65552 | tf_op jit(solution)/shard_map/psum | solution.py:60
  382.3 1.2 add_select_fusion.4
  384.6 2.5 collective-permute-start.20
  387.2 1.3 collective-permute-start.21
  388.5 1.2 collective-permute-done.20
  389.7 4.4 collective-permute-done.21
  394.1 1.3 collective-permute-start.22
  395.4 4.5 collective-permute-start.23
  400.0 1.3 collective-permute-start.24
  402.4 1.4 convolution_bitcast_fusion.3
  404.1 71.0 %all-reduce.15.cloned.1.call-done = f32[4,64,64]{2,1,0:T(8,128)} async-done(((f32[4,64,64]{2,1,0:T(8,128)}), f32[4,64,64]{2,1,0:T(8,128)}) %all-reduce.15.cloned.1.call-update) | async-done | bytes 65552 | tf_op jit(solution)/shard_map/psum | solution.py:60
  475.1 1.2 add_select_fusion.3
  477.4 2.5 collective-permute-start.25
  479.9 1.3 collective-permute-start.26
  481.2 1.2 collective-permute-done.25
  482.4 4.4 collective-permute-done.26
  486.9 1.3 collective-permute-start.27
  488.2 4.5 collective-permute-start.28
  492.7 1.3 collective-permute-start.29
  494.3 0.8 fusion.75
  495.1 1.4 convolution_bitcast_fusion.1
  496.8 71.0 %all-reduce.17.cloned.1.call-done = f32[4,64,64]{2,1,0:T(8,128)} async-done(((f32[4,64,64]{2,1,0:T(8,128)}), f32[4,64,64]{2,1,0:T(8,128)}) %all-reduce.17.cloned.1.call-update) | async-done | bytes 65552 | tf_op jit(solution)/shard_map/psum | solution.py:60
  567.8 1.2 fusion.11
  569.5 1.1 fusion.23
  (88 shorter events, 16.3 us)
Async XLA Ops:
  7.2 2.5 copy-start
  7.2 96.9 %all-reduce.7.cloned.1.call-start = ((), (), s32[]{:S(2)}) async-start(), calls=%async_computation | async-start | bytes 262144 | tf_op jit(solution)/shard_map/psum | solution.py:60
  7.2 24.3 %collective-permute-start.4 = (f32[4,64,64]{2,1,0:T(8,128)S(1)}, f32[4,64,64]{2,1,0:T(8,128)S(1)}, u32[]{:S(2)}, u32[]{:S(2)}) collective-permute-start(f32[4,64,64]{2,1,0:T(8,128)S(1)} %broadcast_in_dim.60), channel_id=1, source_target_pairs={{0,8},{8,16},{16,24},{1,9},{9,17},{17,25},{2,10},{10,18},{18,26},{... | collective-permute-start | bytes 196616 | tf_op jit(solution)/shard_map/ppermute | solution.py:16
  9.8 10.8 %collective-permute-start = (f32[1,4,64,1]{3,2,1,0:T(8,128)S(1)}, f32[1,4,64,1]{3,2,1,0:T(8,128)S(1)}, u32[]{:S(2)}, u32[]{:S(2)}) collective-permute-start(f32[1,4,64,1]{3,2,1,0:T(8,128)S(1)} %get-tuple-element.25), channel_id=1, source_target_pairs={{0,4},{1,5},{2,6},{3,7},{8,12},{9,13},{10,14},{11,15},{16,20},{17,... | collective-permute-start | bytes 3080 | tf_op jit(solution)/shard_map/ppermute | solution.py:26
  14.0 7.7 %collective-permute-start.1 = (f32[1,4,64,1]{3,2,1,0:T(8,128)S(1)}, f32[1,4,64,1]{3,2,1,0:T(8,128)S(1)}, u32[]{:S(2)}, u32[]{:S(2)}) collective-permute-start(f32[1,4,64,1]{3,2,1,0:T(8,128)S(1)} %get-tuple-element.24), channel_id=1, source_target_pairs={{4,0},{5,1},{6,2},{7,3},{12,8},{13,9},{14,10},{15,11},{20,16},{21,... | collective-permute-start | bytes 3080 | tf_op jit(solution)/shard_map/ppermute | solution.py:27
  15.3 0.7 copy-start.4
  21.9 5.9 %collective-permute-start.2 = (f32[1,4,1,130]{3,2,1,0:T(1,128)S(1)}, f32[1,4,1,130]{3,2,1,0:T(1,128)S(1)}, u32[]{:S(2)}, u32[]{:S(2)}) collective-permute-start(f32[1,4,1,130]{3,2,1,0:T(1,128)S(1)} %get-tuple-element.12), channel_id=1, source_target_pairs={{1,0},{2,1},{3,2},{5,4},{6,5},{7,6},{9,8},{10,9},{11,10},{13,12},{... | collective-permute-start | bytes 6248 | tf_op jit(solution)/shard_map/ppermute | solution.py:27
  23.2 5.9 %collective-permute-start.3 = (f32[1,4,1,130]{3,2,1,0:T(1,128)S(1)}, f32[1,4,1,130]{3,2,1,0:T(1,128)S(1)}, u32[]{:S(2)}, u32[]{:S(2)}) collective-permute-start(f32[1,4,1,130]{3,2,1,0:T(1,128)S(1)} %get-tuple-element.13), channel_id=1, source_target_pairs={{0,1},{1,2},{2,3},{4,5},{5,6},{6,7},{8,9},{9,10},{10,11},{12,13},{... | collective-permute-start | bytes 6248 | tf_op jit(solution)/shard_map/ppermute | solution.py:26
  30.1 74.0 %copy-start.1 = (f32[3,4,64,64]{3,2,1,0:T(8,128)S(1)}, f32[3,4,64,64]{3,2,1,0:T(8,128)}, u32[]{:S(2)}) copy-start(f32[3,4,64,64]{3,2,1,0:T(8,128)} %param.5) | copy-start | bytes 589828
  31.5 165.4 %all-reduce.9.cloned.1.call-start = ((), (), s32[]{:S(2)}) async-start(), calls=%async_computation.1 | async-start | bytes 262144 | tf_op jit(solution)/shard_map/psum | solution.py:60
  31.8 72.3 %copy-start.3 = (f32[1,4]{1,0:T(1,128)S(1)}, f32[1,4]{1,0:T(1,128)}, u32[]{:S(2)}) copy-start(f32[1,4]{1,0:T(1,128)} %param.6) | copy-start | bytes 52
  106.4 5.0 collective-permute-start.5
  108.9 6.9 %collective-permute-start.6 = (f32[1,4,64,1]{3,2,1,0:T(8,128)S(1)}, f32[1,4,64,1]{3,2,1,0:T(8,128)S(1)}, u32[]{:S(2)}, u32[]{:S(2)}) collective-permute-start(f32[1,4,64,1]{3,2,1,0:T(8,128)S(1)} %get-tuple-element.22), channel_id=1, source_target_pairs={{4,0},{5,1},{6,2},{7,3},{12,8},{13,9},{14,10},{15,11},{20,16},{21,... | collective-permute-start | bytes 3080 | tf_op jit(solution)/shard_map/ppermute | solution.py:27
  115.9 7.2 %collective-permute-start.7 = (f32[1,4,1,130]{3,2,1,0:T(1,128)S(1)}, f32[1,4,1,130]{3,2,1,0:T(1,128)S(1)}, u32[]{:S(2)}, u32[]{:S(2)}) collective-permute-start(f32[1,4,1,130]{3,2,1,0:T(1,128)S(1)} %get-tuple-element.10), channel_id=1, source_target_pairs={{1,0},{2,1},{3,2},{5,4},{6,5},{7,6},{9,8},{10,9},{11,10},{13,12},{... | collective-permute-start | bytes 6248 | tf_op jit(solution)/shard_map/ppermute | solution.py:27
  117.2 5.9 %collective-permute-start.8 = (f32[1,4,1,130]{3,2,1,0:T(1,128)S(1)}, f32[1,4,1,130]{3,2,1,0:T(1,128)S(1)}, u32[]{:S(2)}, u32[]{:S(2)}) collective-permute-start(f32[1,4,1,130]{3,2,1,0:T(1,128)S(1)} %get-tuple-element.11), channel_id=1, source_target_pairs={{0,1},{1,2},{2,3},{4,5},{5,6},{6,7},{8,9},{9,10},{10,11},{12,13},{... | collective-permute-start | bytes 6248 | tf_op jit(solution)/shard_map/ppermute | solution.py:26
  121.8 3.8 collective-permute-start.9
  125.5 164.0 %all-reduce.11.cloned.1.call-start = ((), (), s32[]{:S(2)}) async-start(), calls=%async_computation.2 | async-start | bytes 262144 | tf_op jit(solution)/shard_map/psum | solution.py:60
  199.2 5.0 collective-permute-start.10
  201.7 6.9 %collective-permute-start.11 = (f32[1,4,64,1]{3,2,1,0:T(8,128)S(1)}, f32[1,4,64,1]{3,2,1,0:T(8,128)S(1)}, u32[]{:S(2)}, u32[]{:S(2)}) collective-permute-start(f32[1,4,64,1]{3,2,1,0:T(8,128)S(1)} %get-tuple-element.20), channel_id=1, source_target_pairs={{4,0},{5,1},{6,2},{7,3},{12,8},{13,9},{14,10},{15,11},{20,16},{21,... | collective-permute-start | bytes 3080 | tf_op jit(solution)/shard_map/ppermute | solution.py:27
  208.7 7.2 %collective-permute-start.12 = (f32[1,4,1,130]{3,2,1,0:T(1,128)S(1)}, f32[1,4,1,130]{3,2,1,0:T(1,128)S(1)}, u32[]{:S(2)}, u32[]{:S(2)}) collective-permute-start(f32[1,4,1,130]{3,2,1,0:T(1,128)S(1)} %get-tuple-element.8), channel_id=1, source_target_pairs={{1,0},{2,1},{3,2},{5,4},{6,5},{7,6},{9,8},{10,9},{11,10},{13,12},{... | collective-permute-start | bytes 6248 | tf_op jit(solution)/shard_map/ppermute | solution.py:27
  210.0 5.9 %collective-permute-start.13 = (f32[1,4,1,130]{3,2,1,0:T(1,128)S(1)}, f32[1,4,1,130]{3,2,1,0:T(1,128)S(1)}, u32[]{:S(2)}, u32[]{:S(2)}) collective-permute-start(f32[1,4,1,130]{3,2,1,0:T(1,128)S(1)} %get-tuple-element.9), channel_id=1, source_target_pairs={{0,1},{1,2},{2,3},{4,5},{5,6},{6,7},{8,9},{9,10},{10,11},{12,13},{... | collective-permute-start | bytes 6248 | tf_op jit(solution)/shard_map/ppermute | solution.py:26
  214.5 3.8 collective-permute-start.14
  218.3 164.0 %all-reduce.13.cloned.1.call-start = ((), (), s32[]{:S(2)}) async-start(), calls=%async_computation.3 | async-start | bytes 262144 | tf_op jit(solution)/shard_map/psum | solution.py:60
  291.9 5.0 collective-permute-start.15
  294.4 6.9 %collective-permute-start.16 = (f32[1,4,64,1]{3,2,1,0:T(8,128)S(1)}, f32[1,4,64,1]{3,2,1,0:T(8,128)S(1)}, u32[]{:S(2)}, u32[]{:S(2)}) collective-permute-start(f32[1,4,64,1]{3,2,1,0:T(8,128)S(1)} %get-tuple-element.18), channel_id=1, source_target_pairs={{4,0},{5,1},{6,2},{7,3},{12,8},{13,9},{14,10},{15,11},{20,16},{21,... | collective-permute-start | bytes 3080 | tf_op jit(solution)/shard_map/ppermute | solution.py:27
  301.4 7.4 %collective-permute-start.17 = (f32[1,4,1,130]{3,2,1,0:T(1,128)S(1)}, f32[1,4,1,130]{3,2,1,0:T(1,128)S(1)}, u32[]{:S(2)}, u32[]{:S(2)}) collective-permute-start(f32[1,4,1,130]{3,2,1,0:T(1,128)S(1)} %get-tuple-element.6), channel_id=1, source_target_pairs={{1,0},{2,1},{3,2},{5,4},{6,5},{7,6},{9,8},{10,9},{11,10},{13,12},{... | collective-permute-start | bytes 6248 | tf_op jit(solution)/shard_map/ppermute | solution.py:27
  302.7 6.1 %collective-permute-start.18 = (f32[1,4,1,130]{3,2,1,0:T(1,128)S(1)}, f32[1,4,1,130]{3,2,1,0:T(1,128)S(1)}, u32[]{:S(2)}, u32[]{:S(2)}) collective-permute-start(f32[1,4,1,130]{3,2,1,0:T(1,128)S(1)} %get-tuple-element.7), channel_id=1, source_target_pairs={{0,1},{1,2},{2,3},{4,5},{5,6},{6,7},{8,9},{9,10},{10,11},{12,13},{... | collective-permute-start | bytes 6248 | tf_op jit(solution)/shard_map/ppermute | solution.py:26
  307.3 4.0 collective-permute-start.19
  311.2 163.8 %all-reduce.15.cloned.1.call-start = ((), (), s32[]{:S(2)}) async-start(), calls=%async_computation.4 | async-start | bytes 262144 | tf_op jit(solution)/shard_map/psum | solution.py:60
  384.6 5.0 collective-permute-start.20
  387.2 6.9 %collective-permute-start.21 = (f32[1,4,64,1]{3,2,1,0:T(8,128)S(1)}, f32[1,4,64,1]{3,2,1,0:T(8,128)S(1)}, u32[]{:S(2)}, u32[]{:S(2)}) collective-permute-start(f32[1,4,64,1]{3,2,1,0:T(8,128)S(1)} %get-tuple-element.16), channel_id=1, source_target_pairs={{4,0},{5,1},{6,2},{7,3},{12,8},{13,9},{14,10},{15,11},{20,16},{21,... | collective-permute-start | bytes 3080 | tf_op jit(solution)/shard_map/ppermute | solution.py:27
  394.1 7.2 %collective-permute-start.22 = (f32[1,4,1,130]{3,2,1,0:T(1,128)S(1)}, f32[1,4,1,130]{3,2,1,0:T(1,128)S(1)}, u32[]{:S(2)}, u32[]{:S(2)}) collective-permute-start(f32[1,4,1,130]{3,2,1,0:T(1,128)S(1)} %get-tuple-element.4), channel_id=1, source_target_pairs={{1,0},{2,1},{3,2},{5,4},{6,5},{7,6},{9,8},{10,9},{11,10},{13,12},{... | collective-permute-start | bytes 6248 | tf_op jit(solution)/shard_map/ppermute | solution.py:27
  395.4 5.9 %collective-permute-start.23 = (f32[1,4,1,130]{3,2,1,0:T(1,128)S(1)}, f32[1,4,1,130]{3,2,1,0:T(1,128)S(1)}, u32[]{:S(2)}, u32[]{:S(2)}) collective-permute-start(f32[1,4,1,130]{3,2,1,0:T(1,128)S(1)} %get-tuple-element.5), channel_id=1, source_target_pairs={{0,1},{1,2},{2,3},{4,5},{5,6},{6,7},{8,9},{9,10},{10,11},{12,13},{... | collective-permute-start | bytes 6248 | tf_op jit(solution)/shard_map/ppermute | solution.py:26
  400.0 3.8 collective-permute-start.24
  403.8 164.0 %all-reduce.17.cloned.1.call-start = ((), (), s32[]{:S(2)}) async-start(), calls=%async_computation.5 | async-start | bytes 262144 | tf_op jit(solution)/shard_map/psum | solution.py:60
  477.4 5.0 collective-permute-start.25
  479.9 6.9 %collective-permute-start.26 = (f32[1,4,64,1]{3,2,1,0:T(8,128)S(1)}, f32[1,4,64,1]{3,2,1,0:T(8,128)S(1)}, u32[]{:S(2)}, u32[]{:S(2)}) collective-permute-start(f32[1,4,64,1]{3,2,1,0:T(8,128)S(1)} %get-tuple-element.14), channel_id=1, source_target_pairs={{4,0},{5,1},{6,2},{7,3},{12,8},{13,9},{14,10},{15,11},{20,16},{21,... | collective-permute-start | bytes 3080 | tf_op jit(solution)/shard_map/ppermute | solution.py:27
  486.9 7.2 %collective-permute-start.27 = (f32[1,4,1,130]{3,2,1,0:T(1,128)S(1)}, f32[1,4,1,130]{3,2,1,0:T(1,128)S(1)}, u32[]{:S(2)}, u32[]{:S(2)}) collective-permute-start(f32[1,4,1,130]{3,2,1,0:T(1,128)S(1)} %get-tuple-element.2), channel_id=1, source_target_pairs={{1,0},{2,1},{3,2},{5,4},{6,5},{7,6},{9,8},{10,9},{11,10},{13,12},{... | collective-permute-start | bytes 6248 | tf_op jit(solution)/shard_map/ppermute | solution.py:27
  488.2 5.9 %collective-permute-start.28 = (f32[1,4,1,130]{3,2,1,0:T(1,128)S(1)}, f32[1,4,1,130]{3,2,1,0:T(1,128)S(1)}, u32[]{:S(2)}, u32[]{:S(2)}) collective-permute-start(f32[1,4,1,130]{3,2,1,0:T(1,128)S(1)} %get-tuple-element.3), channel_id=1, source_target_pairs={{0,1},{1,2},{2,3},{4,5},{5,6},{6,7},{8,9},{9,10},{10,11},{12,13},{... | collective-permute-start | bytes 6248 | tf_op jit(solution)/shard_map/ppermute | solution.py:26
  492.7 3.8 collective-permute-start.29
  569.5 1.1 copy-start.2
Sparse Core Ops, SparseCore 0:
  31.6 72.4 all-reduce.6
  125.7 71.1 all-reduce.8
  218.4 71.1 all-reduce.10
  311.3 70.9 all-reduce.12
  403.9 71.1 all-reduce.14
  496.6 71.1 all-reduce.16
where the time goes:
time: 579 us; the launch traced here: 578 us
  waiting for transfers between devices  457 us (79%)
  starting transfers between devices  68.9 us (12%)
  matrix products  31 us (5%)
  between operations  16.3 us (3%)
    psum x6, waiting for transfers between devices, advance(): own = lax.psum(partial_sum, ('py', 'px'))  427 us
    ppermute x12, starting transfers between devices, padded_2(): before = lax.ppermute(last, axis, up)  44.1 us
    ppermute x12, waiting for transfers between devices, padded_2(): after = lax.ppermute(first, axis, down)  23 us
    ppermute x12, starting transfers between devices, padded_2(): after = lax.ppermute(first, axis, down)  15.5 us
  transfers between devices with their start and end apart: 36, of which 18 were waited for; matrix products, arithmetic and copies ran while one was open for 3% of the time, Pallas kernels for 0%

commit v1 on v0

v1 whole, which is shorter than its diff:
```python
import functools
import math

import jax
import jax.numpy as jnp
import numpy as np
from jax import lax
from jax.experimental import pallas as pl
from jax.experimental.pallas import tpu as pltpu
from jax.sharding import PartitionSpec as P

RATIO = 3
RATE = 0.2
EDGE = 8
INTERPRET = False

highest = lax.Precision.HIGHEST


def multinomial(n, i, j):
    return math.factorial(n) // (math.factorial(i) * math.factorial(j) * math.factorial(n - i - j))


@functools.lru_cache(maxsize=None)
def tables(cells, modes, order):
    cell = np.arange(cells)
    mode = np.arange(modes)
    weight = np.sqrt(np.where(mode == 0, 1.0, 2.0) / cells)
    product = mode[None] * (2 * cell[:, None] + 1)
    coarse = np.pi * (product % (4 * cells)) / (2 * cells)
    fine = np.pi * (product % (4 * RATIO * cells)) / (2 * RATIO * cells)
    base = weight * np.cos(coarse)
    second = RATE * (np.eye(cells, k=1) + np.eye(cells, k=-1) - 2 * np.eye(cells))
    powers = [base]
    for _ in range(order):
        powers.append(second @ powers[-1])
    factor = RATE * (2 * np.cos(np.pi * mode / cells) - 2)
    places = list(range(order)) + list(range(cells - order, cells))
    edges = np.zeros((cells, EDGE))
    edges[places, range(2 * order)] = 1
    spill = [(powers[i] - base * factor**i).T @ edges for i in range(order + 1)]
    return {
        "base": base,
        "edges": edges,
        "powers": powers,
        "factor": factor,
        "spill": spill,
        "within": [base.T @ power for power in powers],
        "cos_map": base.T @ (weight * np.cos(fine)),
        "sin_map": base.T @ (weight * np.sin(fine)),
    }


def kron(count, block):
    return np.kron(np.eye(count), block)


def f32(value):
    return jnp.asarray(np.asarray(value, np.float32))


def mm(a, b, dims=((1,), (0,))):
    return lax.dot_general(a, b, (dims, ((), ())), precision=highest, preferred_element_type=jnp.float32)


def call(kernel, shapes, *args):
    specs = [pl.BlockSpec(memory_space=pltpu.SMEM) if a.ndim == 2 and a.size <= 16 else pl.BlockSpec(memory_space=pltpu.VMEM) for a in args]
    return pl.pallas_call(
        kernel,
        in_specs=specs,
        out_specs=jax.tree.map(lambda _: pl.BlockSpec(memory_space=pltpu.VMEM), shapes),
        out_shape=shapes,
        interpret=INTERPRET,
    )(*args)


def shape_of(*dims):
    return jax.ShapeDtypeStruct(dims, jnp.float32)


class Plan:
    def __init__(self, initial_state, drive_modes):
        _, self.levels, self.nx, self.ny = initial_state.shape
        self.windows, _, self.modes, _ = drive_modes.shape
        self.px = lax.axis_size("px")
        self.py = lax.axis_size("py")
        self.nest = lax.axis_size("nest")
        self.lanes = self.levels * self.modes
        self.half = self.levels // 2
        self.low = self.modes + EDGE
        self.sums = self.low + self.half * EDGE
        self.x = tables(self.nx * self.px, self.modes, self.windows)
        self.y = tables(self.ny * self.py, self.modes, self.windows)
        assert self.levels % 4 == 0 and self.modes * 2 == self.ny and self.nx == self.modes
        assert 2 * self.windows <= EDGE and self.half * self.windows <= EDGE


def project(plan, state):
    low, half, lanes = plan.low, plan.half, plan.lanes
    bases = np.concatenate([plan.x["base"], plan.x["edges"]], 1)
    left = np.zeros((plan.px, 2 * plan.modes, plan.nx))
    left[:, :low] = bases.T.reshape(low, plan.px, plan.nx).transpose(1, 0, 2)
    right = plan.y["base"].reshape(plan.py, plan.ny, plan.modes)
    right = np.stack([kron(2, block) for block in right])
    edge = plan.y["edges"].T.reshape(EDGE, plan.py, plan.ny).transpose(1, 0, 2)
    pick = np.zeros((EDGE, plan.ny))
    for i in range(plan.windows):
        pick[i, i] = 1
        pick[plan.windows + i, plan.ny - plan.windows + i] = 1

    def kernel(state_ref, left_ref, right_ref, edge_ref, pick_ref, out_ref):
        px, py = lax.axis_index("px"), lax.axis_index("py")
        basis = left_ref[px]
        rights = right_ref[py]
        edges = edge_ref[py]
        rows = [mm(basis, state_ref[0, level]) for level in range(plan.levels)]
        for pair in range(half):
            both = jnp.concatenate([rows[2 * pair][:low], rows[2 * pair + 1][:low]], 1)
            out_ref[:low, pair * plan.ny : (pair + 1) * plan.ny] = mm(both, rights)
            patch = jnp.concatenate([state_ref[0, 2 * pair], state_ref[0, 2 * pair + 1]], 0)
            out_ref[plan.sums :, pair * plan.ny : (pair + 1) * plan.ny] = mm(pick_ref[...], patch, ((1,), (1,)))
        for level in range(plan.levels):
            at = low + EDGE * (level % half)
            lane = level // half * plan.ny
            out_ref[at : at + EDGE, lane : lane + plan.ny] = mm(edges, rows[level], ((1,), (1,)))

    return call(
        kernel, shape_of(plan.sums + EDGE, lanes), state, f32(left), f32(right), f32(edge), f32(pick)
    )


def facing_rows(plan, state_ref, bottom):
    rows = []
    for group in range(2):
        pair = [state_ref[0, 2 * group + i] for i in range(2)]
        top = jnp.concatenate([p[: plan.windows] for p in pair], 1)
        end = jnp.concatenate([p[plan.nx - plan.windows :] for p in pair], 1)
        rows.append(jnp.where(bottom, end, top))
    rows.append(jnp.zeros((EDGE - 2 * plan.windows, plan.lanes), jnp.float32))
    return jnp.concatenate(rows, 0)


def join_first(plan, own, other, state, columns):
    sums = plan.sums

    def kernel(own_ref, other_ref, state_ref, columns_ref, out_ref):
        out_ref[:sums] = own_ref[:sums] + other_ref[:sums]
        out_ref[sums : sums + EDGE] = facing_rows(plan, state_ref, lax.axis_index("px") % 2 == 0)
        out_ref[sums + EDGE :] = columns_ref[sums:]

    return call(kernel, shape_of(sums + 2 * EDGE, plan.lanes), own, other, state, columns)


def join_second(plan, own, other, state):
    sums = plan.sums

    def kernel(own_ref, other_ref, state_ref, out_ref):
        out_ref[:sums] = own_ref[:sums] + other_ref[:sums]
        out_ref[sums : sums + EDGE] = facing_rows(plan, state_ref, lax.axis_index("px") % 2 == 1)
        out_ref[sums + EDGE :] = own_ref[sums + EDGE :]

    return call(kernel, shape_of(sums + 2 * EDGE, plan.lanes), own, other, state)


def join_last(plan, own, other, rates):
    sums, low, modes = plan.sums, plan.low, plan.modes

    def kernel(own_ref, other_ref, rates_ref, out_ref):
        out_ref[...] = own_ref[:sums] + other_ref[:sums]
        level = lax.broadcasted_iota(jnp.int32, (1, plan.lanes), 1) // modes
        row = jnp.zeros((1, plan.lanes), jnp.float32)
        for i in range(plan.levels):
            row = jnp.where(level == i, rates_ref[0, i], row)
        out_ref[low - 1 : low] = row

    return call(kernel, shape_of(sums, plan.lanes), own, other, rates)


def step_patch(plan, state, columns, above, below):
    nx, ny, windows, sums = plan.nx, plan.ny, plan.windows, plan.sums
    place = np.zeros((EDGE, ny))
    for i in range(windows):
        place[i, i] = 1
        place[windows + i, ny - windows + i] = 1
    rows, lanes = nx + 2 * EDGE, 2 * ny

    def kernel(state_ref, columns_ref, above_ref, below_ref, place_ref, out_ref):
        px, py = lax.axis_index("px"), lax.axis_index("py")
        row = lax.broadcasted_iota(jnp.int32, (rows, lanes), 0) - EDGE + px * nx
        lane = lax.broadcasted_iota(jnp.int32, (rows, lanes), 1)
        lane = jnp.where(lane >= ny + ny // 2, lane - lanes, lane) + py * ny
        inside = (row >= 0) & (row < nx * plan.px) & (lane >= 0) & (lane < ny * plan.py)
        where = place_ref[...]
        for level in range(plan.levels):
            pair, part = level // 2, level % 2

            def beside(ref):
                block = ref[sums : sums + EDGE] if ref is columns_ref else ref[sums + EDGE :]
                block = block[:, pair * ny : (pair + 1) * ny]
                return mm(block, where, ((0,), (0,)))[part * nx : (part + 1) * nx]

            def line(ref):
                block = ref[sums : sums + EDGE]
                return block[pair * windows : (pair + 1) * windows, part * ny : (part + 1) * ny]

            up = jnp.concatenate([line(above_ref), beside(above_ref)[nx - windows :]], 1)
            down = jnp.concatenate([line(below_ref), beside(below_ref)[:windows]], 1)
            middle = jnp.concatenate([state_ref[0, level], beside(columns_ref)], 1)
            blank = jnp.zeros((EDGE - windows, lanes), jnp.float32)
            field = jnp.concatenate([blank, up, middle, down, blank], 0)
            field = jnp.where(inside, field, 0.0)
            for _ in range(windows):
                around = (
                    pltpu.roll(field, 1, 0)
                    + pltpu.roll(field, rows - 1, 0)
                    + pltpu.roll(field, 1, 1)
                    + pltpu.roll(field, lanes - 1, 1)
                )
                field = jnp.where(inside, field + RATE * (around - 4.0 * field), 0.0)
            out_ref[level] = field[EDGE : EDGE + nx, :ny]

    return call(kernel, shape_of(plan.levels, nx, ny), state, columns, above, below, f32(place))


def nudge(plan, stepped, gathered, drive, angles):
    modes, low, lanes, levels = plan.modes, plan.low, plan.lanes, plan.levels
    windows, half, nx, ny = plan.windows, plan.half, plan.nx, plan.ny
    x, y = plan.x, plan.y

    inward = np.concatenate([kron(levels, y["spill"][j].T) for j in range(1, windows + 1)], 1)
    across = [np.concatenate([x["spill"][i] for i in range(1, n + 1)], 1) for n in range(1, windows + 1)]
    width = EDGE * windows
    across = np.concatenate([np.pad(a, ((0, 0), (0, width - a.shape[1]))) for a in across], 0)
    scale_x = np.broadcast_to(x["factor"][:, None], (modes, lanes))
    scale_y = np.broadcast_to(np.tile(y["factor"], levels), (EDGE, lanes))
    maps_x = np.concatenate([x["cos_map"], x["sin_map"]], 0)
    maps_y = np.concatenate([kron(levels, y["cos_map"].T), kron(levels, y["sin_map"].T)], 0)
    again = []
    for p in range(1, windows):
        again.append(
            np.concatenate(
                [
                    sum(multinomial(p, i, j) * x["within"][i] for i in range(p - j + 1))
                    for j in range(p + 1)
                ],
                0,
            )
        )
    again = np.concatenate(again, 0)
    sideways = np.concatenate([kron(levels, y["within"][j]) for j in range(1, windows)], 0)
    rows_x = [p.reshape(plan.px, nx, modes) for p in x["powers"]]
    spread_x = np.zeros((plan.px, windows * nx, windows * modes))
    for j in range(windows):
        for w in range(windows):
            p = windows - 1 - w
            for i in range(p - j + 1):
                spread_x[:, j * nx : (j + 1) * nx, w * modes : (w + 1) * modes] += multinomial(p, i, j) * rows_x[i]
    rows_y = [p.reshape(plan.py, ny, modes) for p in y["powers"]]
    spread_y = np.stack(
        [np.concatenate([kron(2, rows_y[j][d].T) for j in range(windows)], 0) for d in range(plan.py)]
    )

    def kernel(
        stepped_ref, gathered_ref, drive_ref, angles_ref, inward_ref, across_ref, scale_x_ref, scale_y_ref,
        maps_x_ref, maps_y_ref, again_ref, sideways_ref, spread_x_ref, spread_y_ref, state_ref, modes_ref,
    ):
        nest = lax.axis_index("nest")
        px, py = lax.axis_index("px"), lax.axis_index("py")
        scale_x, scale_y = scale_x_ref[...], scale_y_ref[:1]

        def own_modes(domain):
            rows = gathered_ref[domain, :low]
            sides = gathered_ref[domain, low:]
            sides = jnp.concatenate([sides[:, i * ny : (i + 1) * ny] for i in range(2)], 0)
            extra = mm(sides, inward_ref[...], ((0,), (0,)))[:low]
            turned = [rows]
            for j in range(1, windows + 1):
                turned.append(rows * scale_y**j + extra[:, (j - 1) * lanes : j * lanes])
            result = []
            for n in range(1, windows + 1):
                parts = [
                    sum(multinomial(n, i, j) * turned[j] for j in range(n - i + 1)) for i in range(n + 1)
                ]
                total = parts[n][:modes]
                for i in range(n - 1, -1, -1):
                    total = total * scale_x + parts[i][:modes]
                ends = jnp.concatenate([part[modes:] for part in parts[1:]], 0)
                result.append(
                    total + mm(across_ref[(n - 1) * modes : n * modes, : n * EDGE], ends)
                )
            return result

        def carried(p, change):
            at = modes * sum(range(2, p + 1))
            left = mm(again_ref[at : at + (p + 1) * modes], change)
            pieces = jnp.concatenate([left[j * modes : (j + 1) * modes] for j in range(1, p + 1)], 1)
            return left[:modes] + mm(pieces, sideways_ref[: p * lanes])

        coeffs = [jnp.zeros((modes, lanes), jnp.float32)] * windows
        final_modes = coeffs[0]
        final_changes = coeffs
        for domain in range(plan.nest):
            gain = gathered_ref[domain, low - 1 : low]
            own = own_modes(domain)
            cos_x = angles_ref[4 * domain : 4 * domain + 1, :modes]
            sin_x = angles_ref[4 * domain + 1 : 4 * domain + 2, :modes]
            cos_y = angles_ref[4 * domain + 2 : 4 * domain + 3]
            sin_y = angles_ref[4 * domain + 3 : 4 * domain + 4]
            row_map = maps_x_ref[:modes] * cos_x - maps_x_ref[modes:] * sin_x
            new, changes = [], []
            for w in range(windows):
                if domain == 0:
                    target = drive_ref[w]
                else:
                    parent = jnp.concatenate([coeffs[w] * cos_y, coeffs[w] * -sin_y], 1)
                    target = mm(row_map, mm(parent, maps_y_ref[...]))
                before = own[w]
                for v in range(w):
                    before = before + carried(w - v, changes[v])
                change = gain * (target - before)
                changes.append(change)
                new.append(before + change)
            coeffs = new
            mine = nest == domain
            final_modes = jnp.where(mine, new[-1], final_modes)
            final_changes = [jnp.where(mine, a, b) for a, b in zip(changes, final_changes)]
        for level in range(levels):
            modes_ref[0, level] = final_modes[:, level * modes : (level + 1) * modes]
        spread = mm(spread_x_ref[px], jnp.concatenate(final_changes, 0))
        for pair in range(half):
            lane = pair * 2 * modes
            pieces = [spread[j * nx : (j + 1) * nx, lane : lane + 2 * modes] for j in range(windows)]
            field = mm(jnp.concatenate(pieces, 1), spread_y_ref[py])
            for part in range(2):
                level = 2 * pair + part
                state_ref[0, level] = stepped_ref[level] + field[:, part * ny : (part + 1) * ny]

    return call(
        kernel,
        (shape_of(1, levels, nx, ny), shape_of(1, levels, modes, modes)),
        stepped, gathered, drive, angles, f32(inward), f32(across), f32(scale_x), f32(scale_y),
        f32(maps_x), f32(maps_y), f32(again), f32(sideways), f32(spread_x), f32(spread_y),
    )


def map_angles(plan, nest_offsets):
    mode = jnp.tile(jnp.arange(plan.modes, dtype=jnp.int32), plan.levels)
    cells = jnp.array([plan.nx * plan.px, plan.ny * plan.py], jnp.int32)
    turn = nest_offsets[:, :, None] * mode % (2 * cells[None, :, None])
    angle = jnp.pi * turn.astype(jnp.float32) / cells[None, :, None].astype(jnp.float32)
    both = jnp.stack([jnp.cos(angle), jnp.sin(angle)], 2)
    return both.reshape(plan.nest * 4, plan.lanes)


def swap(value, axis, partner):
    size = lax.axis_size(axis)
    return lax.ppermute(value, axis, [(i, partner(i)) for i in range(size) if 0 <= partner(i) < size])


def body(initial_state, drive_modes, relax_rates, nest_offsets):
    plan = Plan(initial_state, drive_modes)
    sums = plan.sums
    angles = map_angles(plan, nest_offsets)
    drive = drive_modes.transpose(0, 2, 1, 3).reshape(plan.windows, plan.modes, plan.lanes)
    share = project(plan, initial_state)
    if plan.py == 2 and plan.px == 4:
        columns = swap(share, "py", lambda i: i ^ 1)
        first = join_first(plan, share, columns, initial_state, columns)
        got_first = swap(first, "px", lambda i: i ^ 1)
        second = join_second(plan, first, got_first, initial_state)
        got_second = swap(second, "px", lambda i: i ^ 3)
        last = join_last(plan, second, got_second, relax_rates)
        even = lax.axis_index("px") % 2 == 0
        above = jnp.where(even, got_second, got_first)
        below = jnp.where(even, got_first, got_second)
    else:
        edge = jnp.arange(sums + EDGE)[:, None] < sums + plan.windows
        right = swap(share, "py", lambda i: i - 1)
        left = swap(share, "py", lambda i: i + 1)
        columns = jnp.where(edge, right, left)
        blank = jnp.zeros_like(share)
        first = join_first(plan, share, blank, initial_state, columns)
        second = join_second(plan, first, jnp.zeros_like(first), initial_state)
        even = lax.axis_index("px") % 2 == 0
        above = swap(jnp.where(even, first, second), "px", lambda i: i + 1)
        below = swap(jnp.where(even, second, first), "px", lambda i: i - 1)
        total = lax.psum(share[:sums], ("py", "px"))
        last = join_last(plan, total, jnp.zeros_like(total), relax_rates)
    gathered = lax.all_gather(last, "nest")
    stepped = step_patch(plan, initial_state, columns, above, below)
    return nudge(plan, stepped, gathered, drive, angles)


def solution(mesh):
    return jax.shard_map(
        body,
        mesh=mesh,
        in_specs=(P("nest", None, "px", "py"), P(), P("nest", None), P()),
        out_specs=(P("nest", None, "px", "py"), P("nest", None, None, None)),
        check_vma=False,
    )
```

time: 579 us -> 55.2 us (0.10)
  waiting for transfers between devices: 457 us -> 6.93 us
  starting transfers between devices: 68.9 us -> 8.77 us
  matrix products: 31 us -> 0 us
  Pallas kernels: 0 us -> 25.8 us
  between operations: 16.3 us -> 0.67 us
  blocking collectives: 0 us -> 8.02 us
    psum x6 -> x0, waiting for transfers between devices: 427 us -> none  [advance(): own = lax.psum(partial_sum, ('py', 'px'))]
    ppermute x30 -> x3, starting transfers between devices: 68.7 us -> 8.77 us  [swap(): lax.ppermute(value, axis, [(i, partner(i)) for i in range(size) if 0 <= p...]
    dot_general x38 -> x0, matrix products: 31 us -> none  [the longest x12 8.61 us: advance(): jnp.einsum('jp,lpq,mq->ljm', row_map, parent, col_map, precision=highest)]
    pallas_call x0 -> x6, Pallas kernels: none -> 25.8 us  [call(): pl.pallas_call(kernel, in_specs=specs, out_specs=jax.tree.map(lambda _: p...]
    ppermute x30 -> x3, waiting for transfers between devices: 30.3 us -> 6.93 us  [swap(): lax.ppermute(value, axis, [(i, partner(i)) for i in range(size) if 0 <= p...]
    all_gather x0 -> x1, blocking collectives: none -> 8.02 us  [body(): gathered = lax.all_gather(last, 'nest')]
  transfers between devices with their start and end apart: 36 -> 3, of which waited for: 18 -> 3; matrix products, arithmetic and copies ran while one was open for 3% -> 4% of each run, Pallas kernels for 0% -> 0%
where the time goes in v1:
time: 55.2 us; the launch traced here: 54.9 us
  Pallas kernels  25.8 us (47%)
  starting transfers between devices  8.77 us (16%)
  blocking collectives  8.02 us (15%)
  waiting for transfers between devices  6.93 us (13%)
  local copies, waits for them, and re-layouts  3.84 us (7%)
  other arithmetic  0.85 us (2%)
  between operations  0.67 us (1%)
    pallas_call x6, Pallas kernels, call(): pl.pallas_call(kernel, in_specs=specs, out_specs=jax.tree.map(lambda _: p...  25.8 us
    ppermute x3, starting transfers between devices, swap(): lax.ppermute(value, axis, [(i, partner(i)) for i in range(size) if 0 <= p...  8.77 us
    all_gather x1, blocking collectives, body(): gathered = lax.all_gather(last, 'nest')  8.02 us
    ppermute x3, waiting for transfers between devices, swap(): lax.ppermute(value, axis, [(i, partner(i)) for i in range(size) if 0 <= p...  6.93 us
    unnamed x14, local copies, waits for them, and re-layouts  1.93 us
  transfers between devices with their start and end apart: 3, of which 3 were waited for; matrix products, arithmetic and copies ran while one was open for 4% of the time, Pallas kernels for 0%

profile of v1, /device:TPU:0, one launch (start us, length us, event | category | flops | bytes accessed | tf_op | source)
XLA Modules:
  0.0 54.9 jit_solution(462331258192754804)
XLA Ops:
  0.6 2.9 %shard_map.203.own_ref = f32[96,256]{1,0:T(8,128)} custom-call(f32[1,4,64,128]{3,2,1,0:T(8,128)} %state_ref.7, f32[4,128,64]{2,1,0:T(8,128)} %constant.58.clone.left_ref, f32[2,256,128]{2,1,0:T(8,128)} %constant.59.clone.right_ref, f32[2,8,128]{2,1,0:T(8,128)} %constant.60.clone.edge_ref, f32[8,128]{1,0:T(8,128)} %constant.61.clone.pick_ref.place_ref), custom_call_target="tpu_custom_call" | custom-call | tf_op jit(solution)/shard_map/pallas_call | solution.py:68
  3.5 0.0 copy-start.5
  3.5 3.0 %collective-permute-start = (f32[96,256]{1,0:T(8,128)}, f32[96,256]{1,0:T(8,128)S(1)}, u32[]{:S(2)}, u32[]{:S(2)}) collective-permute-start(f32[96,256]{1,0:T(8,128)} %shard_map.203.own_ref), channel_id=1, source_target_pairs={{0,4},{4,0},{1,5},{5,1},{2,6},{6,2},{3,7},{7,3},{8,12},{12,8},{9,1... | collective-permute-start | bytes 294920 | tf_op jit(solution)/shard_map/ppermute | solution.py:357
  6.5 0.1 mul.48
  6.6 0.0 copy-start.6
  6.6 2.9 %collective-permute-done.other_ref.columns_ref = f32[96,256]{1,0:T(8,128)S(1)} collective-permute-done((f32[96,256]{1,0:T(8,128)}, f32[96,256]{1,0:T(8,128)S(1)}, u32[]{:S(2)}, u32[]{:S(2)}) %collective-permute-start) | collective-permute-done | bytes 98336 | tf_op jit(solution)/shard_map/ppermute | solution.py:357
  9.5 0.0 copy-start
  9.5 0.6 %copy-done = f32[96,256]{1,0:T(8,128)} copy-done((f32[96,256]{1,0:T(8,128)}, f32[96,256]{1,0:T(8,128)S(1)}, u32[]{:S(2)}) %copy-start) | copy-done | bytes 98328
  10.2 1.7 %shard_map.204.own_ref = f32[104,256]{1,0:T(8,128)} custom-call(f32[96,256]{1,0:T(8,128)} %shard_map.203.own_ref, f32[96,256]{1,0:T(8,128)} %copy-done, f32[1,4,64,128]{3,2,1,0:T(8,128)} %state_ref.7, f32[96,256]{1,0:T(8,128)} %copy-done), custom_call_target="tpu_custom_call" | custom-call | tf_op jit(solution)/shard_map/pallas_call | solution.py:68
  11.9 1.9 %collective-permute-start.1 = (f32[104,256]{1,0:T(8,128)}, f32[104,256]{1,0:T(8,128)S(1)}, u32[]{:S(2)}, u32[]{:S(2)}) collective-permute-start(f32[104,256]{1,0:T(8,128)} %shard_map.204.own_ref), channel_id=1, source_target_pairs={{0,1},{1,0},{2,3},{3,2},{4,5},{5,4},{6,7},{7,6},{8,9},{9,8},{10,11... | collective-permute-start | bytes 319496 | tf_op jit(solution)/shard_map/ppermute | solution.py:357
  13.8 0.0 copy-done.6
  13.8 0.2 fusion.4
  13.9 0.0 copy-done.5
  13.9 0.3 copy.24
  14.2 0.9 %reshape.59.drive_ref = f32[3,64,256]{2,1,0:T(8,128)} reshape(f32[3,64,4,64]{3,2,1,0:T(4,128)S(1)} %copy.24) | data formatting | bytes 393216 | tf_op jit(solution)/shard_map/reshape | solution.py:364
  15.1 1.7 %collective-permute-done.1.other_ref = f32[104,256]{1,0:T(8,128)S(1)} collective-permute-done((f32[104,256]{1,0:T(8,128)}, f32[104,256]{1,0:T(8,128)S(1)}, u32[]{:S(2)}, u32[]{:S(2)}) %collective-permute-start.1) | collective-permute-done | bytes 106528 | tf_op jit(solution)/shard_map/ppermute | solution.py:357
  16.8 0.0 copy-start.1
  16.8 0.6 %copy-done.1 = f32[104,256]{1,0:T(8,128)} copy-done((f32[104,256]{1,0:T(8,128)}, f32[104,256]{1,0:T(8,128)S(1)}, u32[]{:S(2)}) %copy-start.1) | copy-done | bytes 106520
  17.4 1.7 %shard_map.205.own_ref = f32[104,256]{1,0:T(8,128)} custom-call(f32[104,256]{1,0:T(8,128)} %shard_map.204.own_ref, f32[104,256]{1,0:T(8,128)} %copy-done.1, f32[1,4,64,128]{3,2,1,0:T(8,128)} %state_ref.7), custom_call_target="tpu_custom_call" | custom-call | tf_op jit(solution)/shard_map/pallas_call | solution.py:68
  19.1 3.9 %collective-permute-start.2 = (f32[104,256]{1,0:T(8,128)}, f32[104,256]{1,0:T(8,128)S(1)}, u32[]{:S(2)}, u32[]{:S(2)}) collective-permute-start(f32[104,256]{1,0:T(8,128)} %shard_map.205.own_ref), channel_id=1, source_target_pairs={{0,3},{1,2},{2,1},{3,0},{4,7},{5,6},{6,5},{7,4},{8,11},{9,10},{10,... | collective-permute-start | bytes 319496 | tf_op jit(solution)/shard_map/ppermute | solution.py:357
  23.0 0.6 %reshape.60.angles_ref = f32[16,256]{1,0:T(8,128)} reshape(f32[4,2,2,256]{3,2,1,0:T(2,128)S(1)} %copy.25) | data formatting | bytes 32768 | tf_op jit(solution)/shard_map/reshape | solution.py:352
  23.6 2.4 %collective-permute-done.2.other_ref = f32[104,256]{1,0:T(8,128)S(1)} collective-permute-done((f32[104,256]{1,0:T(8,128)}, f32[104,256]{1,0:T(8,128)S(1)}, u32[]{:S(2)}, u32[]{:S(2)}) %collective-permute-start.2) | collective-permute-done | bytes 106528 | tf_op jit(solution)/shard_map/ppermute | solution.py:357
  26.0 0.0 copy-start.3
  26.0 0.6 %copy-done.3 = f32[104,256]{1,0:T(8,128)} copy-done((f32[104,256]{1,0:T(8,128)}, f32[104,256]{1,0:T(8,128)S(1)}, u32[]{:S(2)}) %copy-start.3) | copy-done | bytes 106520
  26.6 1.6 %shard_map.207 = f32[88,256]{1,0:T(8,128)} custom-call(f32[104,256]{1,0:T(8,128)} %shard_map.205.own_ref, f32[104,256]{1,0:T(8,128)} %copy-done.3, f32[1,4]{1,0:T(1,128)} %rates_ref.1), custom_call_target="tpu_custom_call" | custom-call | tf_op jit(solution)/shard_map/pallas_call | solution.py:68
  28.2 0.0 copy-start.2
  28.2 0.0 copy-start.4
  28.2 8.0 %all-gather = f32[352,256]{1,0:T(8,128)} all-gather(f32[88,256]{1,0:T(8,128)} %shard_map.207), channel_id=2, replica_groups=mesh['nest'=4,'py'=2,'px'=4] {'nest'}, dimensions={0}, use_global_device_ids=true | all-gather | bytes 450560 | tf_op jit(solution)/shard_map/all_gather | solution.py:389
  36.3 0.0 copy-done.2
  36.3 0.0 copy-done.4
  36.3 0.7 %broadcast_select_fusion = (f32[104,256]{1,0:T(8,128)}, f32[104,256]{1,0:T(8,128)}) fusion(f32[104,256]{1,0:T(8,128)S(1)} %copy-done.2, f32[104,256]{1,0:T(8,128)S(1)} %copy-done.4, pred[]{:T(512)S(6)} %eq.10), kind=kLoop, calls=%fused_computation | loop fusion | flops 53248 | bytes 425985 | tf_op jit(solution)/shard_map/jit(_where)/select_n | solution.py:375
  37.0 2.9 %shard_map.206.stepped_ref = f32[4,64,128]{2,1,0:T(8,128)} custom-call(f32[1,4,64,128]{3,2,1,0:T(8,128)} %state_ref.7, f32[96,256]{1,0:T(8,128)} %copy-done, f32[104,256]{1,0:T(8,128)} %get-tuple-element.3.above_ref, f32[104,256]{1,0:T(8,128)} %get-tuple-element.2.below_ref, f32[8,128]{1,0:T(8,128)} %constant.61.clone.pick_ref.place_ref), custom_call_target="tpu_custom_call" | custom-call | tf_op jit(solution)/shard_map/pallas_call | solution.py:68
  39.9 15.1 %shard_map.208 = (f32[1,4,64,128]{3,2,1,0:T(8,128)}, f32[1,4,64,64]{3,2,1,0:T(8,128)}) custom-call(f32[4,64,128]{2,1,0:T(8,128)} %shard_map.206.stepped_ref, f32[4,88,256]{2,1,0:T(8,128)} %bitcast.2, f32[3,64,256]{2,1,0:T(8,128)} %reshape.59.drive_ref, f32[16,256]{1,0:T(8,128)} %reshape.60.angles_ref, f32[32,768]{1,0:T(8,128)} %constant.62.clone.inward_ref, ...), custom_call_target="tpu_custom_call" | custom-call | tf_op jit(solution)/shard_map/pallas_call | solution.py:68
  (3 shorter events, 0.0 us)
Async XLA Ops:
  3.5 10.4 %copy-start.5 = (f32[3,4,64,64]{3,2,1,0:T(8,128)S(1)}, f32[3,4,64,64]{3,2,1,0:T(8,128)}, u32[]{:S(2)}) copy-start(f32[3,4,64,64]{3,2,1,0:T(8,128)} %param.21) | copy-start | bytes 589828
  3.5 6.0 %collective-permute-start = (f32[96,256]{1,0:T(8,128)}, f32[96,256]{1,0:T(8,128)S(1)}, u32[]{:S(2)}, u32[]{:S(2)}) collective-permute-start(f32[96,256]{1,0:T(8,128)} %shard_map.203.own_ref), channel_id=1, source_target_pairs={{0,4},{4,0},{1,5},{5,1},{2,6},{6,2},{3,7},{7,3},{8,12},{12,8},{9,1... | collective-permute-start | bytes 294920 | tf_op jit(solution)/shard_map/ppermute | solution.py:357
  6.6 7.1 %copy-start.6 = (s32[4,2]{0,1:T(2,128)S(1)}, s32[4,2]{0,1:T(2,128)}, u32[]{:S(2)}) copy-start(s32[4,2]{0,1:T(2,128)} %param.23) | copy-start | bytes 100
  9.5 0.6 %copy-start = (f32[96,256]{1,0:T(8,128)}, f32[96,256]{1,0:T(8,128)S(1)}, u32[]{:S(2)}) copy-start(f32[96,256]{1,0:T(8,128)S(1)} %collective-permute-done.other_ref.columns_ref) | copy-start | bytes 294916
  11.9 4.9 %collective-permute-start.1 = (f32[104,256]{1,0:T(8,128)}, f32[104,256]{1,0:T(8,128)S(1)}, u32[]{:S(2)}, u32[]{:S(2)}) collective-permute-start(f32[104,256]{1,0:T(8,128)} %shard_map.204.own_ref), channel_id=1, source_target_pairs={{0,1},{1,0},{2,3},{3,2},{4,5},{5,4},{6,7},{7,6},{8,9},{9,8},{10,11... | collective-permute-start | bytes 319496 | tf_op jit(solution)/shard_map/ppermute | solution.py:357
  16.8 0.6 %copy-start.1 = (f32[104,256]{1,0:T(8,128)}, f32[104,256]{1,0:T(8,128)S(1)}, u32[]{:S(2)}) copy-start(f32[104,256]{1,0:T(8,128)S(1)} %collective-permute-done.1.other_ref) | copy-start | bytes 319492
  19.1 6.9 %collective-permute-start.2 = (f32[104,256]{1,0:T(8,128)}, f32[104,256]{1,0:T(8,128)S(1)}, u32[]{:S(2)}, u32[]{:S(2)}) collective-permute-start(f32[104,256]{1,0:T(8,128)} %shard_map.205.own_ref), channel_id=1, source_target_pairs={{0,3},{1,2},{2,1},{3,0},{4,7},{5,6},{6,5},{7,4},{8,11},{9,10},{10,... | collective-permute-start | bytes 319496 | tf_op jit(solution)/shard_map/ppermute | solution.py:357
  26.0 0.6 %copy-start.3 = (f32[104,256]{1,0:T(8,128)}, f32[104,256]{1,0:T(8,128)S(1)}, u32[]{:S(2)}) copy-start(f32[104,256]{1,0:T(8,128)S(1)} %collective-permute-done.2.other_ref) | copy-start | bytes 319492
  28.2 8.0 %copy-start.2 = (f32[104,256]{1,0:T(8,128)S(1)}, f32[104,256]{1,0:T(8,128)}, u32[]{:S(2)}) copy-start(f32[104,256]{1,0:T(8,128)} %copy-done.1) | copy-start | bytes 319492
  28.2 8.0 %copy-start.4 = (f32[104,256]{1,0:T(8,128)S(1)}, f32[104,256]{1,0:T(8,128)}, u32[]{:S(2)}) copy-start(f32[104,256]{1,0:T(8,128)} %copy-done.3) | copy-start | bytes 319492

commit v2 on v1

--- a/solution.py
+++ b/solution.py
@@ -63,15 +63,63 @@
     return lax.dot_general(a, b, (dims, ((), ())), precision=highest, preferred_element_type=jnp.float32)
 
 
-def call(kernel, shapes, *args):
-    specs = [pl.BlockSpec(memory_space=pltpu.SMEM) if a.ndim == 2 and a.size <= 16 else pl.BlockSpec(memory_space=pltpu.VMEM) for a in args]
+def bf16(value):
+    return np.asarray(value, jnp.bfloat16)
+
+
+def parts_of(value):
+    high = bf16(value)
+    return high, bf16(value - high.astype(np.float64))
+
+
+def left_table(value):
+    high, low = parts_of(value)
+    return jnp.asarray(np.concatenate([high, low, high], -1))
+
+
+def right_table(value):
+    high, low = parts_of(value)
+    upper = np.concatenate([high, low], -1)
+    lower = np.concatenate([high, np.zeros_like(low)], -1)
+    return jnp.asarray(np.concatenate([upper, lower], -2))
+
+
+def halves(value):
+    high = value.astype(jnp.bfloat16)
+    return high, (value - high.astype(jnp.float32)).astype(jnp.bfloat16)
+
+
+def dot(a, b, dims=((1,), (0,))):
+    return lax.dot_general(a, b, (dims, ((), ())), preferred_element_type=jnp.float32)
+
+
+def stacked(value):
+    high, low = halves(value)
+    return jnp.concatenate([high, high, low], 0)
+
+
+def times_right(value, table):
+    out = dot(jnp.concatenate(halves(value), 1), table)
+    width = out.shape[1] // 2
+    return out[:, :width] + out[:, width:]
+
+
+def in_vmem(value):
+    return value if INTERPRET else pltpu.with_memory_space_constraint(value, pltpu.VMEM)
+
+
+def call(kernel, shapes, *args, first=False, final=False):
+    scalars = [a.ndim == 2 and a.size <= 16 for a in args]
+    specs = [pl.BlockSpec(memory_space=pltpu.SMEM if s else pltpu.VMEM) for s in scalars]
+    if not final and not INTERPRET:
+        shapes = jax.tree.map(lambda s: pltpu.VMEM(s.shape, s.dtype), shapes)
     return pl.pallas_call(
         kernel,
         in_specs=specs,
         out_specs=jax.tree.map(lambda _: pl.BlockSpec(memory_space=pltpu.VMEM), shapes),
         out_shape=shapes,
         interpret=INTERPRET,
-    )(*args)
+    )(*[a if s or first else in_vmem(a) for a, s in zip(args, scalars)])
 
 
 def shape_of(*dims):
@@ -125,7 +173,7 @@
             out_ref[at : at + EDGE, lane : lane + plan.ny] = mm(edges, rows[level], ((1,), (1,)))
 
     return call(
-        kernel, shape_of(plan.sums + EDGE, lanes), state, f32(left), f32(right), f32(edge), f32(pick)
+        kernel, shape_of(plan.sums + EDGE, lanes), state, f32(left), f32(right), f32(edge), f32(pick), first=True
     )
 
 
@@ -222,60 +270,73 @@
     return call(kernel, shape_of(plan.levels, nx, ny), state, columns, above, below, f32(place))
 
 
-def nudge(plan, stepped, gathered, drive, angles):
+def nudge(plan, stepped, gathered, drive, angles, turns):
     modes, low, lanes, levels = plan.modes, plan.low, plan.lanes, plan.levels
     windows, half, nx, ny = plan.windows, plan.half, plan.nx, plan.ny
     x, y = plan.x, plan.y
-
-    inward = np.concatenate([kron(levels, y["spill"][j].T) for j in range(1, windows + 1)], 1)
-    across = [np.concatenate([x["spill"][i] for i in range(1, n + 1)], 1) for n in range(1, windows + 1)]
-    width = EDGE * windows
-    across = np.concatenate([np.pad(a, ((0, 0), (0, width - a.shape[1]))) for a in across], 0)
-    scale_x = np.broadcast_to(x["factor"][:, None], (modes, lanes))
-    scale_y = np.broadcast_to(np.tile(y["factor"], levels), (EDGE, lanes))
-    maps_x = np.concatenate([x["cos_map"], x["sin_map"]], 0)
-    maps_y = np.concatenate([kron(levels, y["cos_map"].T), kron(levels, y["sin_map"].T)], 0)
+    width = EDGE * (windows + 1)
+
+    inward = np.concatenate([kron(2, y["spill"][j].T) for j in range(1, windows + 1)], 1)
+    high, small = parts_of(inward)
+    inward = jnp.asarray(np.concatenate([high, small, high], 0))
+    across = np.zeros((windows, modes, width))
+    for n in range(1, windows + 1):
+        for i in range(1, n + 1):
+            across[n - 1, :, (i - 1) * EDGE : i * EDGE] = x["spill"][i]
+    across = left_table(across)
+    scale_x = f32(np.broadcast_to(x["factor"][:, None], (modes, lanes)))
+    scale_y = f32(np.broadcast_to(np.tile(y["factor"], levels), (EDGE, lanes)))
+    maps_x = f32(np.stack([np.tile(x["cos_map"], (1, 3)), np.tile(x["sin_map"], (1, 3))]))
+    maps_y = f32(np.stack([kron(2, y["cos_map"].T), kron(2, y["sin_map"].T)]))
     again = []
     for p in range(1, windows):
-        again.append(
-            np.concatenate(
-                [
-                    sum(multinomial(p, i, j) * x["within"][i] for i in range(p - j + 1))
-                    for j in range(p + 1)
-                ],
-                0,
-            )
-        )
-    again = np.concatenate(again, 0)
-    sideways = np.concatenate([kron(levels, y["within"][j]) for j in range(1, windows)], 0)
+        again.append(sum(multinomial(p, i, 0) * x["within"][i] for i in range(p + 1)))
+    again = left_table(np.concatenate(again, 0))
+    sideways = jnp.stack([right_table(kron(2, y["within"][j])) for j in range(1, windows)])
     rows_x = [p.reshape(plan.px, nx, modes) for p in x["powers"]]
-    spread_x = np.zeros((plan.px, windows * nx, windows * modes))
+    spread_x = np.zeros((plan.px, windows, windows * nx, modes))
     for j in range(windows):
         for w in range(windows):
             p = windows - 1 - w
             for i in range(p - j + 1):
-                spread_x[:, j * nx : (j + 1) * nx, w * modes : (w + 1) * modes] += multinomial(p, i, j) * rows_x[i]
+                spread_x[:, w, j * nx : (j + 1) * nx] += multinomial(p, i, j) * rows_x[i]
+    spread_x = lax.dynamic_index_in_dim(left_table(spread_x), lax.axis_index("px"), 0, keepdims=False)
     rows_y = [p.reshape(plan.py, ny, modes) for p in y["powers"]]
-    spread_y = np.stack(
-        [np.concatenate([kron(2, rows_y[j][d].T) for j in range(windows)], 0) for d in range(plan.py)]
-    )
+    spread_y = np.stack([[kron(2, rows_y[j][d].T) for j in range(windows)] for d in range(plan.py)])
+    spread_y = lax.dynamic_index_in_dim(right_table(spread_y), lax.axis_index("py"), 0, keepdims=False)
+    assert windows <= 3
+
+    def pairs(value):
+        return jnp.concatenate([value[:, i * ny : (i + 1) * ny] for i in range(half)], 0)
+
+    def unpairs(value):
+        return jnp.concatenate([value[i * modes : (i + 1) * modes] for i in range(half)], 1)
 
     def kernel(
-        stepped_ref, gathered_ref, drive_ref, angles_ref, inward_ref, across_ref, scale_x_ref, scale_y_ref,
-        maps_x_ref, maps_y_ref, again_ref, sideways_ref, spread_x_ref, spread_y_ref, state_ref, modes_ref,
+        stepped_ref, drive_ref, angles_ref, turns_ref, inward_ref, across_ref, scale_x_ref, scale_y_ref,
+        maps_x_ref, maps_y_ref, again_ref, sideways_ref, spread_x_ref, spread_y_ref, *refs,
     ):
+        slots, (state_ref, modes_ref) = refs[:-2], refs[-2:]
+        root = plan.nest - 1
         nest = lax.axis_index("nest")
-        px, py = lax.axis_index("px"), lax.axis_index("py")
         scale_x, scale_y = scale_x_ref[...], scale_y_ref[:1]
-
-        def own_modes(domain):
-            rows = gathered_ref[domain, :low]
-            sides = gathered_ref[domain, low:]
-            sides = jnp.concatenate([sides[:, i * ny : (i + 1) * ny] for i in range(2)], 0)
-            extra = mm(sides, inward_ref[...], ((0,), (0,)))[:low]
+        lane = lax.broadcasted_iota(jnp.int32, (modes, 3 * modes), 1)
+        middle = (lane >= modes) & (lane < 2 * modes)
+
+        def own_modes(ref):
+            rows = ref[:low]
+            extra = []
+            for i in range(half):
+                sides = ref[low:, i * ny : (i + 1) * ny]
+                high = sides.astype(jnp.bfloat16).astype(jnp.float32)
+                sides = jnp.concatenate([high, high, sides - high], 0).astype(jnp.bfloat16)
+                extra.append(dot(sides, inward_ref[...], ((0,), (0,)))[:low])
             turned = [rows]
-            for j in range(1, windows + 1):
-                turned.append(rows * scale_y**j + extra[:, (j - 1) * lanes : j * lanes])
+            scale = scale_y
+            for j in range(windows):
+                add = jnp.concatenate([e[:, j * ny : (j + 1) * ny] for e in extra], 1)
+                turned.append(rows * scale + add)
+                scale = scale * scale_y
             result = []
             for n in range(1, windows + 1):
                 parts = [
@@ -284,72 +345,88 @@
                 total = parts[n][:modes]
                 for i in range(n - 1, -1, -1):
                     total = total * scale_x + parts[i][:modes]
-                ends = jnp.concatenate([part[modes:] for part in parts[1:]], 0)
-                result.append(
-                    total + mm(across_ref[(n - 1) * modes : n * modes, : n * EDGE], ends)
+                ends = [part[modes:] for part in parts[1:]]
+                ends += [jnp.zeros((EDGE, lanes), jnp.float32)] * (windows + 1 - n)
+                ends = jnp.concatenate(ends, 0)
+                result.append(total + dot(across_ref[n - 1], stacked(ends)))
+            return result
+
+        def carried(change, count):
+            left = dot(again_ref[: count * modes], stacked(change))
+            left = [left[i * modes : (i + 1) * modes] for i in range(count)]
+            if count == 1:
+                return [left[0] + unpairs(times_right(pairs(change), sideways_ref[0]))]
+            both = jnp.concatenate([pairs(change), pairs(left[0])], 0)
+            once = times_right(both, sideways_ref[0])
+            twice = times_right(pairs(change), sideways_ref[1])
+            rows = half * modes
+            return [left[0] + unpairs(once[:rows]), left[1] + unpairs(2.0 * once[rows:] + twice)]
+
+        owns = [own_modes(ref) for ref in slots]
+        coeffs = None
+        for slot in range(root, -1, -1):
+            gain = slots[slot][low - 1 : low]
+            own = owns[slot]
+            if slot < root:
+                at = 4 * slot
+                row_map = (
+                    maps_x_ref[0] * angles_ref[at : at + 1, : 3 * modes]
+                    - maps_x_ref[1] * angles_ref[at + 1 : at + 2, : 3 * modes]
                 )
-            return result
-
-        def carried(p, change):
-            at = modes * sum(range(2, p + 1))
-            left = mm(again_ref[at : at + (p + 1) * modes], change)
-            pieces = jnp.concatenate([left[j * modes : (j + 1) * modes] for j in range(1, p + 1)], 1)
-            return left[:modes] + mm(pieces, sideways_ref[: p * lanes])
-
-        coeffs = [jnp.zeros((modes, lanes), jnp.float32)] * windows
-        final_modes = coeffs[0]
-        final_changes = coeffs
-        for domain in range(plan.nest):
-            gain = gathered_ref[domain, low - 1 : low]
-            own = own_modes(domain)
-            cos_x = angles_ref[4 * domain : 4 * domain + 1, :modes]
-            sin_x = angles_ref[4 * domain + 1 : 4 * domain + 2, :modes]
-            cos_y = angles_ref[4 * domain + 2 : 4 * domain + 3]
-            sin_y = angles_ref[4 * domain + 3 : 4 * domain + 4]
-            row_map = maps_x_ref[:modes] * cos_x - maps_x_ref[modes:] * sin_x
-            new, changes = [], []
+                rounded = row_map.astype(jnp.bfloat16).astype(jnp.float32)
+                row_map = jnp.where(middle, row_map - rounded, rounded).astype(jnp.bfloat16)
+                col_map = (
+                    maps_y_ref[0] * turns_ref[:, 2 * slot : 2 * slot + 1]
+                    - maps_y_ref[1] * turns_ref[:, 2 * slot + 1 : 2 * slot + 2]
+                )
+                high, small = halves(col_map)
+                col_map = jnp.concatenate(
+                    [jnp.concatenate([high, small], 1), jnp.concatenate([high, jnp.zeros_like(high)], 1)], 0
+                )
+            new, changes, later = [], [], []
             for w in range(windows):
-                if domain == 0:
-                    target = drive_ref[w]
-                else:
-                    parent = jnp.concatenate([coeffs[w] * cos_y, coeffs[w] * -sin_y], 1)
-                    target = mm(row_map, mm(parent, maps_y_ref[...]))
+                target = drive_ref[w]
+                if slot < root:
+                    inner = dot(row_map, stacked(unpairs(times_right(pairs(coeffs[w]), col_map))))
+                    target = jnp.where(nest <= slot, target, inner)
                 before = own[w]
                 for v in range(w):
-                    before = before + carried(w - v, changes[v])
+                    before = before + later[v][w - v - 1]
                 change = gain * (target - before)
+                if w < windows - 1:
+                    later.append(carried(change, windows - 1 - w))
                 changes.append(change)
                 new.append(before + change)
             coeffs = new
-            mine = nest == domain
-            final_modes = jnp.where(mine, new[-1], final_modes)
-            final_changes = [jnp.where(mine, a, b) for a, b in zip(changes, final_changes)]
         for level in range(levels):
-            modes_ref[0, level] = final_modes[:, level * modes : (level + 1) * modes]
-        spread = mm(spread_x_ref[px], jnp.concatenate(final_changes, 0))
-        for pair in range(half):
-            lane = pair * 2 * modes
-            pieces = [spread[j * nx : (j + 1) * nx, lane : lane + 2 * modes] for j in range(windows)]
-            field = mm(jnp.concatenate(pieces, 1), spread_y_ref[py])
-            for part in range(2):
-                level = 2 * pair + part
-                state_ref[0, level] = stepped_ref[level] + field[:, part * ny : (part + 1) * ny]
+            modes_ref[0, level] = coeffs[-1][:, level * modes : (level + 1) * modes]
+        spread = sum(dot(spread_x_ref[w], stacked(changes[w])) for w in range(windows))
+        field = sum(
+            times_right(pairs(spread[j * nx : (j + 1) * nx]), spread_y_ref[j]) for j in range(windows)
+        )
+        for level in range(levels):
+            row, at = level // 2 * nx, level % 2 * ny
+            state_ref[0, level] = stepped_ref[level] + field[row : row + nx, at : at + ny]
 
     return call(
         kernel,
         (shape_of(1, levels, nx, ny), shape_of(1, levels, modes, modes)),
-        stepped, gathered, drive, angles, f32(inward), f32(across), f32(scale_x), f32(scale_y),
-        f32(maps_x), f32(maps_y), f32(again), f32(sideways), f32(spread_x), f32(spread_y),
+        stepped, drive, angles, turns, inward, across, scale_x, scale_y,
+        maps_x, maps_y, again, sideways, spread_x, spread_y, *gathered,
+        final=True,
     )
 
 
 def map_angles(plan, nest_offsets):
     mode = jnp.tile(jnp.arange(plan.modes, dtype=jnp.int32), plan.levels)
     cells = jnp.array([plan.nx * plan.px, plan.ny * plan.py], jnp.int32)
-    turn = nest_offsets[:, :, None] * mode % (2 * cells[None, :, None])
+    domain = lax.axis_index("nest") - jnp.arange(plan.nest)
+    offsets = nest_offsets[jnp.maximum(domain, 0)]
+    turn = offsets[:, :, None] * mode % (2 * cells[None, :, None])
     angle = jnp.pi * turn.astype(jnp.float32) / cells[None, :, None].astype(jnp.float32)
     both = jnp.stack([jnp.cos(angle), jnp.sin(angle)], 2)
-    return both.reshape(plan.nest * 4, plan.lanes)
+    turns = both[:, 1, :, : 2 * plan.modes].reshape(2 * plan.nest, 2 * plan.modes).T
+    return both.reshape(plan.nest * 4, plan.lanes), turns
 
 
 def swap(value, axis, partner):
@@ -360,7 +437,7 @@
 def body(initial_state, drive_modes, relax_rates, nest_offsets):
     plan = Plan(initial_state, drive_modes)
     sums = plan.sums
-    angles = map_angles(plan, nest_offsets)
+    angles, turns = map_angles(plan, nest_offsets)
     drive = drive_modes.transpose(0, 2, 1, 3).reshape(plan.windows, plan.modes, plan.lanes)
     share = project(plan, initial_state)
     if plan.py == 2 and plan.px == 4:
@@ -386,9 +463,9 @@
         below = swap(jnp.where(even, second, first), "px", lambda i: i - 1)
         total = lax.psum(share[:sums], ("py", "px"))
         last = join_last(plan, total, jnp.zeros_like(total), relax_rates)
-    gathered = lax.all_gather(last, "nest")
+    gathered = [last] + [swap(last, "nest", lambda i, s=s: i + s) for s in range(1, plan.nest)]
     stepped = step_patch(plan, initial_state, columns, above, below)
-    return nudge(plan, stepped, gathered, drive, angles)
+    return nudge(plan, stepped, gathered, drive, angles, turns)
 
 
 def solution(mesh):

time: 55.2 us -> 33.7 us (0.61)
  Pallas kernels: 25.8 us -> 9.16 us
  blocking collectives: 8.02 us -> 0 us
  starting transfers between devices: 8.77 us -> 13.7 us
  waiting for transfers between devices: 6.93 us -> 3.97 us
  local copies, waits for them, and re-layouts: 3.84 us -> 5.38 us
  other arithmetic: 0.85 us -> 0.2 us
    pallas_call x6, Pallas kernels: 25.8 us -> 9.16 us  [call(): pl.pallas_call(kernel, in_specs=specs, out_specs=jax.tree.map(lambda _: p...]
    all_gather x1 -> x0, blocking collectives: 8.02 us -> none  [body(): gathered = lax.all_gather(last, 'nest')]
    ppermute x3 -> x6, starting transfers between devices: 8.77 us -> 13.7 us  [swap(): lax.ppermute(value, axis, [(i, partner(i)) for i in range(size) if 0 <= p...]
    ppermute x3 -> x6, waiting for transfers between devices: 6.93 us -> 3.97 us  [swap(): lax.ppermute(value, axis, [(i, partner(i)) for i in range(size) if 0 <= p...]
    squeeze x0 -> x2, local copies, waits for them, and re-layouts: none -> 2.16 us  [the longest x1 1.18 us: nudge(): lax.dynamic_index_in_dim(right_table(spread_y), lax.axis_index('py'), 0,...]
    unnamed x14 -> x21, local copies, waits for them, and re-layouts: 1.93 us -> 0.83 us
    transpose x1, local copies, waits for them, and re-layouts: 0.26 us -> 1.25 us  [body(): drive_modes.transpose(0, 2, 1, 3)]
    select_n x1, other arithmetic: 0.7 us -> 0.02 us  [body(): below = jnp.where(even, got_first, got_second)]
  transfers between devices with their start and end apart: 3 -> 6, of which waited for: 3 -> 2; matrix products, arithmetic and copies ran while one was open for 4% -> 17% of each run, Pallas kernels for 0% -> 4%
where the time goes in v2:
time: 33.7 us; the launch traced here: 33.3 us
  starting transfers between devices  13.7 us (41%)
  Pallas kernels  9.16 us (27%)
  local copies, waits for them, and re-layouts  5.38 us (16%)
  waiting for transfers between devices  3.97 us (12%)
  between operations  0.92 us (3%)
    ppermute x6, starting transfers between devices, swap(): lax.ppermute(value, axis, [(i, partner(i)) for i in range(size) if 0 <= p...  13.7 us
    pallas_call x6, Pallas kernels, call(): pl.pallas_call(kernel, in_specs=specs, out_specs=jax.tree.map(lambda _: p...  9.16 us
    ppermute x6, waiting for transfers between devices, swap(): lax.ppermute(value, axis, [(i, partner(i)) for i in range(size) if 0 <= p...  3.97 us
    transpose x1, local copies, waits for them, and re-layouts, body(): drive_modes.transpose(0, 2, 1, 3)  1.25 us
    squeeze x1, local copies, waits for them, and re-layouts, nudge(): lax.dynamic_index_in_dim(right_table(spread_y), lax.axis_index('py'), 0,...  1.18 us
    squeeze x1, local copies, waits for them, and re-layouts, nudge(): lax.dynamic_index_in_dim(left_table(spread_x), lax.axis_index('px'), 0, k...  0.98 us
    unnamed x21, local copies, waits for them, and re-layouts  0.83 us
  transfers between devices with their start and end apart: 6, of which 2 were waited for; matrix products, arithmetic and copies ran while one was open for 17% of the time, Pallas kernels for 4%

profile of v2, /device:TPU:0, one launch (start us, length us, event | category | flops | bytes accessed | tf_op | source)
XLA Modules:
  0.0 33.3 jit_solution(7784558800545186446)
XLA Ops:
  0.6 0.0 copy-start
  0.6 2.3 %shard_map.212.own_ref = f32[96,256]{1,0:T(8,128)S(1)} custom-call(f32[1,4,64,128]{3,2,1,0:T(8,128)} %state_ref.7, f32[4,128,64]{2,1,0:T(8,128)} %constant.80.clone.left_ref, f32[2,256,128]{2,1,0:T(8,128)} %constant.81.clone.right_ref, f32[2,8,128]{2,1,0:T(8,128)} %constant.82.clone.edge_ref, f32[8,128]{1,0:T(8,128)} %constant.83.clone.pick_ref.place_ref), custom_call_target="tpu_custom_call" | custom-call | tf_op jit(solution)/shard_map/pallas_call | solution.py:116
  2.9 3.0 %collective-permute-start = (f32[96,256]{1,0:T(8,128)S(1)}, f32[96,256]{1,0:T(8,128)S(1)}, u32[]{:S(2)}, u32[]{:S(2)}) collective-permute-start(f32[96,256]{1,0:T(8,128)S(1)} %shard_map.212.own_ref), channel_id=1, source_target_pairs={{0,4},{4,0},{1,5},{5,1},{2,6},{6,2},{3,7},{7,3},{8,12},{12,8},{9,1... | collective-permute-start | bytes 294920 | tf_op jit(solution)/shard_map/ppermute | solution.py:434
  5.9 0.8 %copy.33 = s32[4,2]{1,0:T(4,128)S(1)} copy(s32[4,2]{0,1:T(2,128)} %param.24) | data formatting | bytes 64 | tf_op args[3]
  6.7 0.1 mul.48
  6.8 0.6 %gather_fusion = s32[4,2]{1,0:T(4,128)S(1)} fusion(s32[4,2]{1,0:T(4,128)S(1)} %copy.33, s32[1024]{0:T(1024)S(1)} %pad_clamp_fusion), kind=kCustom, calls=%fused_computation | custom fusion | bytes 80 | tf_op jit(solution)/shard_map/gather | solution.py:424
  7.4 0.1 copy.34
  7.5 0.2 fusion.5
  7.7 0.1 copy.37
  7.8 1.3 %copy.32 = f32[3,64,4,64]{3,2,1,0:T(4,128)S(1)} copy(f32[3,64,4,64]{3,1,2,0:T(8,128)} %bitcast.10) | data formatting | bytes 393216 | tf_op jit(solution)/shard_map/transpose | solution.py:441
  9.0 0.3 reshape.69.drive_ref
  9.3 0.0 collective-permute-done.other_ref.columns_ref
  9.3 0.0 copy-done
  9.4 0.0 copy-start.8
  9.4 0.0 copy-start.1
  9.4 0.0 copy-start.2
  9.4 0.0 copy-start.3
  9.4 0.0 copy-start.4
  9.4 0.0 copy-start.5
  9.4 0.0 copy-start.6
  9.4 0.0 copy-start.7
  9.5 0.0 copy-start.9
  9.5 1.6 %collective-permute-start.1 = (f32[104,256]{1,0:T(8,128)S(1)}, f32[104,256]{1,0:T(8,128)S(1)}, u32[]{:S(2)}, u32[]{:S(2)}) collective-permute-start(f32[104,256]{1,0:T(8,128)S(1)} %shard_map.213.own_ref), channel_id=1, source_target_pairs={{0,1},{1,0},{2,3},{3,2},{4,5},{5,4},{6,7},{7,6},{8,9},{9,8},{10,11... | collective-permute-start | bytes 319496 | tf_op jit(solution)/shard_map/ppermute | solution.py:434
  11.1 1.2 %dynamic-slice_bitcast_fusion.spread_y_ref = bf16[3,256,512]{2,1,0:T(8,128)(2,1)S(1)} fusion(bf16[2,3,256,512]{3,2,1,0:T(8,128)(2,1)} %constant.94.clone, s32[]{:T(128)S(6)} %select_n.56), kind=kLoop, calls=%fused_computation.1 | loop fusion | bytes 1572868 | tf_op jit(solution)/shard_map/jit(dynamic_index_in_dim)/squeeze | solution.py:306
  12.3 1.9 %collective-permute-done.1.other_ref = f32[104,256]{1,0:T(8,128)S(1)} collective-permute-done((f32[104,256]{1,0:T(8,128)S(1)}, f32[104,256]{1,0:T(8,128)S(1)}, u32[]{:S(2)}, u32[]{:S(2)}) %collective-permute-start.1) | collective-permute-done | bytes 106528 | tf_op jit(solution)/shard_map/ppermute | solution.py:434
  14.3 3.7 %collective-permute-start.2 = (f32[104,256]{1,0:T(8,128)S(1)}, f32[104,256]{1,0:T(8,128)S(1)}, u32[]{:S(2)}, u32[]{:S(2)}) collective-permute-start(f32[104,256]{1,0:T(8,128)S(1)} %shard_map.214.own_ref), channel_id=1, source_target_pairs={{0,3},{1,2},{2,1},{3,0},{4,7},{5,6},{6,5},{7,4},{8,11},{9,10},{10,... | collective-permute-start | bytes 319496 | tf_op jit(solution)/shard_map/ppermute | solution.py:434
  17.9 1.0 %dynamic-slice_bitcast_fusion.1.spread_x_ref = bf16[3,192,192]{2,1,0:T(8,128)(2,1)S(1)} fusion(bf16[4,3,192,192]{3,2,1,0:T(8,128)(2,1)} %constant.93.clone, s32[]{:T(128)S(6)} %select_n.55), kind=kLoop, calls=%fused_computation.2 | loop fusion | bytes 442372 | tf_op jit(solution)/shard_map/jit(dynamic_index_in_dim)/squeeze | solution.py:303
  18.9 2.0 %collective-permute-done.2.other_ref = f32[104,256]{1,0:T(8,128)S(1)} collective-permute-done((f32[104,256]{1,0:T(8,128)S(1)}, f32[104,256]{1,0:T(8,128)S(1)}, u32[]{:S(2)}, u32[]{:S(2)}) %collective-permute-start.2) | collective-permute-done | bytes 106528 | tf_op jit(solution)/shard_map/ppermute | solution.py:434
  20.9 0.7 %shard_map.216.refs_0_ = f32[88,256]{1,0:T(8,128)S(1)} custom-call(f32[104,256]{1,0:T(8,128)S(1)} %shard_map.214.own_ref, f32[104,256]{1,0:T(8,128)S(1)} %collective-permute-done.2.other_ref, f32[1,4]{1,0:T(1,128)} %rates_ref.1), custom_call_target="tpu_custom_call" | custom-call | tf_op jit(solution)/shard_map/pallas_call | solution.py:116
  21.6 1.3 %collective-permute-start.5 = (f32[88,256]{1,0:T(8,128)S(1)}, f32[88,256]{1,0:T(8,128)S(1)}, u32[]{:S(2)}, u32[]{:S(2)}) collective-permute-start(f32[88,256]{1,0:T(8,128)S(1)} %shard_map.216.refs_0_), channel_id=1, source_target_pairs={{0,24},{1,25},{2,26},{3,27},{4,28},{5,29},{6,30},{7,31}} | collective-permute-start | bytes 270344 | tf_op jit(solution)/shard_map/ppermute | solution.py:434
  22.9 2.8 %collective-permute-start.4 = (f32[88,256]{1,0:T(8,128)S(1)}, f32[88,256]{1,0:T(8,128)S(1)}, u32[]{:S(2)}, u32[]{:S(2)}) collective-permute-start(f32[88,256]{1,0:T(8,128)S(1)} %shard_map.216.refs_0_), channel_id=1, source_target_pairs={{0,16},{8,24},{1,17},{9,25},{2,18},{10,26},{3,19},{11,27},{4,20},{... | collective-permute-start | bytes 270344 | tf_op jit(solution)/shard_map/ppermute | solution.py:434
  25.7 1.3 %collective-permute-start.3 = (f32[88,256]{1,0:T(8,128)S(1)}, f32[88,256]{1,0:T(8,128)S(1)}, u32[]{:S(2)}, u32[]{:S(2)}) collective-permute-start(f32[88,256]{1,0:T(8,128)S(1)} %shard_map.216.refs_0_), channel_id=1, source_target_pairs={{0,8},{8,16},{16,24},{1,9},{9,17},{17,25},{2,10},{10,18},{18,26},{... | collective-permute-start | bytes 270344 | tf_op jit(solution)/shard_map/ppermute | solution.py:434
  27.0 0.0 copy-done.8
  27.0 1.2 %shard_map.215.stepped_ref = f32[4,64,128]{2,1,0:T(8,128)S(1)} custom-call(f32[1,4,64,128]{3,2,1,0:T(8,128)S(1)} %copy-done, f32[96,256]{1,0:T(8,128)S(1)} %collective-permute-done.other_ref.columns_ref, f32[104,256]{1,0:T(8,128)S(1)} %get-tuple-element.3.above_ref, f32[104,256]{1,0:T(8,128)S(1)} %get-tuple-element.2.below_ref, f32[8,128]{1,0:T(8,128)S(1)} %copy-done.8), custom_call_target="tpu_custom_call" | custom-call | tf_op jit(solution)/shard_map/pallas_call | solution.py:116
  28.2 0.0 collective-permute-done.5.refs_3_
  28.3 0.0 collective-permute-done.4.refs_2_
  28.3 0.0 collective-permute-done.3.refs_1_
  28.3 0.0 copy-done.1
  28.3 0.0 copy-done.2
  28.3 0.0 copy-done.3
  28.3 0.0 copy-done.4
  28.3 0.0 copy-done.5
  28.3 0.0 copy-done.6
  28.3 0.0 copy-done.7
  28.3 0.0 copy-done.9
  28.4 5.0 %shard_map.217 = (f32[1,4,64,128]{3,2,1,0:T(8,128)}, f32[1,4,64,64]{3,2,1,0:T(8,128)}) custom-call(f32[4,64,128]{2,1,0:T(8,128)S(1)} %shard_map.215.stepped_ref, f32[3,64,256]{2,1,0:T(8,128)S(1)} %reshape.69.drive_ref, f32[16,256]{1,0:T(8,128)S(1)} %reshape.70.angles_ref, f32[128,8]{1,0:T(8,128)S(1)} %bitcast.9, bf16[48,384]{1,0:T(8,128)(2,1)S(1)} %copy-done.7, ...), custom_call_target="tpu_custom_call" | custom-call | tf_op jit(solution)/shard_map/pallas_call | solution.py:116
  (11 shorter events, 0.1 us)
Async XLA Ops:
  0.6 8.7 %copy-start = (f32[1,4,64,128]{3,2,1,0:T(8,128)S(1)}, f32[1,4,64,128]{3,2,1,0:T(8,128)}, u32[]{:S(2)}) copy-start(f32[1,4,64,128]{3,2,1,0:T(8,128)} %state_ref.7) | copy-start | bytes 393220
  2.9 6.4 %collective-permute-start = (f32[96,256]{1,0:T(8,128)S(1)}, f32[96,256]{1,0:T(8,128)S(1)}, u32[]{:S(2)}, u32[]{:S(2)}) collective-permute-start(f32[96,256]{1,0:T(8,128)S(1)} %shard_map.212.own_ref), channel_id=1, source_target_pairs={{0,4},{4,0},{1,5},{5,1},{2,6},{6,2},{3,7},{7,3},{8,12},{12,8},{9,1... | collective-permute-start | bytes 294920 | tf_op jit(solution)/shard_map/ppermute | solution.py:434
  9.4 17.7 %copy-start.8 = (f32[8,128]{1,0:T(8,128)S(1)}, f32[8,128]{1,0:T(8,128)}, u32[]{:S(2)}) copy-start(f32[8,128]{1,0:T(8,128)} %constant.83.clone.pick_ref.place_ref) | copy-start | bytes 12292
  9.4 18.9 %copy-start.1 = (bf16[2,256,256]{2,1,0:T(8,128)(2,1)S(1)}, bf16[2,256,256]{2,1,0:T(8,128)(2,1)}, u32[]{:S(2)}) copy-start(bf16[2,256,256]{2,1,0:T(8,128)(2,1)} %constant.104.sideways_ref) | copy-start | bytes 786436
  9.4 18.9 %copy-start.2 = (f32[2,128,128]{2,1,0:T(8,128)S(1)}, f32[2,128,128]{2,1,0:T(8,128)}, u32[]{:S(2)}) copy-start(f32[2,128,128]{2,1,0:T(8,128)} %constant.89.clone.maps_y_ref) | copy-start | bytes 393220
  9.4 18.9 %copy-start.3 = (f32[2,64,192]{2,1,0:T(8,128)S(1)}, f32[2,64,192]{2,1,0:T(8,128)}, u32[]{:S(2)}) copy-start(f32[2,64,192]{2,1,0:T(8,128)} %constant.88.clone.maps_x_ref) | copy-start | bytes 294916
  9.4 18.9 %copy-start.4 = (bf16[128,192]{1,0:T(8,128)(2,1)S(1)}, bf16[128,192]{1,0:T(8,128)(2,1)}, u32[]{:S(2)}) copy-start(bf16[128,192]{1,0:T(8,128)(2,1)} %constant.90.clone.again_ref) | copy-start | bytes 147460
  9.4 18.9 %copy-start.5 = (f32[64,256]{1,0:T(8,128)S(1)}, f32[64,256]{1,0:T(8,128)}, u32[]{:S(2)}) copy-start(f32[64,256]{1,0:T(8,128)} %constant.86.clone.scale_x_ref) | copy-start | bytes 196612
  9.4 18.9 %copy-start.6 = (bf16[3,64,96]{2,1,0:T(8,128)(2,1)S(1)}, bf16[3,64,96]{2,1,0:T(8,128)(2,1)}, u32[]{:S(2)}) copy-start(bf16[3,64,96]{2,1,0:T(8,128)(2,1)} %constant.85.clone.across_ref) | copy-start | bytes 110596
  9.4 18.9 %copy-start.7 = (bf16[48,384]{1,0:T(8,128)(2,1)S(1)}, bf16[48,384]{1,0:T(8,128)(2,1)}, u32[]{:S(2)}) copy-start(bf16[48,384]{1,0:T(8,128)(2,1)} %constant.84.clone.inward_ref) | copy-start | bytes 110596
  9.5 18.9 %copy-start.9 = (f32[8,256]{1,0:T(8,128)S(1)}, f32[8,256]{1,0:T(8,128)}, u32[]{:S(2)}) copy-start(f32[8,256]{1,0:T(8,128)} %constant.87.clone.scale_y_ref) | copy-start | bytes 24580
  9.5 4.8 %collective-permute-start.1 = (f32[104,256]{1,0:T(8,128)S(1)}, f32[104,256]{1,0:T(8,128)S(1)}, u32[]{:S(2)}, u32[]{:S(2)}) collective-permute-start(f32[104,256]{1,0:T(8,128)S(1)} %shard_map.213.own_ref), channel_id=1, source_target_pairs={{0,1},{1,0},{2,3},{3,2},{4,5},{5,4},{6,7},{7,6},{8,9},{9,8},{10,11... | collective-permute-start | bytes 319496 | tf_op jit(solution)/shard_map/ppermute | solution.py:434
  14.3 6.7 %collective-permute-start.2 = (f32[104,256]{1,0:T(8,128)S(1)}, f32[104,256]{1,0:T(8,128)S(1)}, u32[]{:S(2)}, u32[]{:S(2)}) collective-permute-start(f32[104,256]{1,0:T(8,128)S(1)} %shard_map.214.own_ref), channel_id=1, source_target_pairs={{0,3},{1,2},{2,1},{3,0},{4,7},{5,6},{6,5},{7,4},{8,11},{9,10},{10,... | collective-permute-start | bytes 319496 | tf_op jit(solution)/shard_map/ppermute | solution.py:434
  21.6 6.6 %collective-permute-start.5 = (f32[88,256]{1,0:T(8,128)S(1)}, f32[88,256]{1,0:T(8,128)S(1)}, u32[]{:S(2)}, u32[]{:S(2)}) collective-permute-start(f32[88,256]{1,0:T(8,128)S(1)} %shard_map.216.refs_0_), channel_id=1, source_target_pairs={{0,24},{1,25},{2,26},{3,27},{4,28},{5,29},{6,30},{7,31}} | collective-permute-start | bytes 270344 | tf_op jit(solution)/shard_map/ppermute | solution.py:434
  22.9 5.3 %collective-permute-start.4 = (f32[88,256]{1,0:T(8,128)S(1)}, f32[88,256]{1,0:T(8,128)S(1)}, u32[]{:S(2)}, u32[]{:S(2)}) collective-permute-start(f32[88,256]{1,0:T(8,128)S(1)} %shard_map.216.refs_0_), channel_id=1, source_target_pairs={{0,16},{8,24},{1,17},{9,25},{2,18},{10,26},{3,19},{11,27},{4,20},{... | collective-permute-start | bytes 270344 | tf_op jit(solution)/shard_map/ppermute | solution.py:434
  25.7 2.6 %collective-permute-start.3 = (f32[88,256]{1,0:T(8,128)S(1)}, f32[88,256]{1,0:T(8,128)S(1)}, u32[]{:S(2)}, u32[]{:S(2)}) collective-permute-start(f32[88,256]{1,0:T(8,128)S(1)} %shard_map.216.refs_0_), channel_id=1, source_target_pairs={{0,8},{8,16},{16,24},{1,9},{9,17},{17,25},{2,10},{10,18},{18,26},{... | collective-permute-start | bytes 270344 | tf_op jit(solution)/shard_map/ppermute | solution.py:434

commit v3 on v2

v3 whole, which is shorter than its diff:
```python
import functools
import math

import jax
import jax.numpy as jnp
import numpy as np
from jax import lax
from jax.experimental import pallas as pl
from jax.experimental.pallas import tpu as pltpu
from jax.sharding import PartitionSpec as P

RATIO = 3
RATE = 0.2
EDGE = 8
INTERPRET = False


def multinomial(n, i, j):
    return math.factorial(n) // (math.factorial(i) * math.factorial(j) * math.factorial(n - i - j))


@functools.lru_cache(maxsize=None)
def tables(cells, modes, order):
    cell = np.arange(cells)
    mode = np.arange(modes)
    weight = np.sqrt(np.where(mode == 0, 1.0, 2.0) / cells)
    product = mode[None] * (2 * cell[:, None] + 1)
    coarse = np.pi * (product % (4 * cells)) / (2 * cells)
    fine = np.pi * (product % (4 * RATIO * cells)) / (2 * RATIO * cells)
    base = weight * np.cos(coarse)
    second = RATE * (np.eye(cells, k=1) + np.eye(cells, k=-1) - 2 * np.eye(cells))
    powers = [base]
    for _ in range(order):
        powers.append(second @ powers[-1])
    factor = RATE * (2 * np.cos(np.pi * mode / cells) - 2)
    places = list(range(order)) + list(range(cells - order, cells))
    edges = np.zeros((cells, EDGE))
    edges[places, range(2 * order)] = 1
    spill = [(powers[i] - base * factor**i).T @ edges for i in range(order + 1)]
    return {
        "base": base,
        "edges": edges,
        "powers": powers,
        "factor": factor,
        "spill": spill,
        "within": [base.T @ power for power in powers],
        "cos_map": base.T @ (weight * np.cos(fine)),
        "sin_map": base.T @ (weight * np.sin(fine)),
    }


def kron(count, block):
    return np.kron(np.eye(count), block)


def f32(value):
    return jnp.asarray(np.asarray(value, np.float32))


def bf16(value):
    return np.asarray(value, jnp.bfloat16)


def parts_of(value):
    high = bf16(value)
    return high, bf16(value - high.astype(np.float64))


def left_table(value):
    high, low = parts_of(value)
    return jnp.asarray(np.concatenate([high, low, high], -1))


def right_table(value):
    high, low = parts_of(value)
    upper = np.concatenate([high, low], -1)
    lower = np.concatenate([high, np.zeros_like(low)], -1)
    return jnp.asarray(np.concatenate([upper, lower], -2))


def halves(value):
    high = value.astype(jnp.bfloat16)
    return high, (value - high.astype(jnp.float32)).astype(jnp.bfloat16)


def dot(a, b, dims=((1,), (0,))):
    return lax.dot_general(a, b, (dims, ((), ())), preferred_element_type=jnp.float32)


def stacked(value):
    high, low = halves(value)
    return jnp.concatenate([high, high, low], 0)


def short_stacked(value, rows):
    high = value.astype(jnp.bfloat16).astype(jnp.float32)
    blank = jnp.zeros((rows - 3 * value.shape[0], value.shape[1]), jnp.float32)
    return jnp.concatenate([high, high, value - high, blank], 0).astype(jnp.bfloat16)


def times_right(value, table):
    out = dot(jnp.concatenate(halves(value), 1), table)
    width = out.shape[1] // 2
    return out[:, :width] + out[:, width:]


def in_vmem(value):
    return value if INTERPRET else pltpu.with_memory_space_constraint(value, pltpu.VMEM)


def call(kernel, shapes, *args, first=False, final=False):
    scalars = [a.ndim == 2 and a.size <= 16 for a in args]
    specs = [pl.BlockSpec(memory_space=pltpu.SMEM if s else pltpu.VMEM) for s in scalars]
    if not final and not INTERPRET:
        shapes = jax.tree.map(lambda s: pltpu.VMEM(s.shape, s.dtype), shapes)
    return pl.pallas_call(
        kernel,
        in_specs=specs,
        out_specs=jax.tree.map(lambda _: pl.BlockSpec(memory_space=pltpu.VMEM), shapes),
        out_shape=shapes,
        interpret=INTERPRET,
    )(*[a if s or first else in_vmem(a) for a, s in zip(args, scalars)])


def shape_of(*dims, kind=jnp.float32):
    return jax.ShapeDtypeStruct(dims, kind)


class Plan:
    def __init__(self, initial_state, drive_modes):
        _, self.levels, self.nx, self.ny = initial_state.shape
        self.windows, _, self.modes, _ = drive_modes.shape
        self.px = lax.axis_size("px")
        self.py = lax.axis_size("py")
        self.nest = lax.axis_size("nest")
        self.lanes = self.levels * self.modes
        self.half = self.levels // 2
        self.low = self.modes + EDGE
        self.sums = self.low + EDGE
        self.rows = self.sums + EDGE
        self.x = tables(self.nx * self.px, self.modes, self.windows)
        self.y = tables(self.ny * self.py, self.modes, self.windows)
        assert self.levels % 4 == 0 and self.modes * 2 == self.ny and self.nx == self.modes
        assert self.windows == 3 and self.half == 2 and EDGE * EDGE == self.modes

    def pairs(self, value):
        width = 2 * self.modes
        return jnp.concatenate([value[:, i * width : (i + 1) * width] for i in range(self.half)], 0)

    def unpairs(self, value):
        rows = value.shape[0] // self.half
        return jnp.concatenate([value[i * rows : (i + 1) * rows] for i in range(self.half)], 1)


def project(plan, state, rates):
    low, half, lanes, levels = plan.low, plan.half, plan.lanes, plan.levels
    modes, nx, ny, windows = plan.modes, plan.nx, plan.ny, plan.windows
    bases = np.concatenate([plan.x["base"], plan.x["edges"], np.zeros((nx * plan.px, EDGE))], 1)
    left = left_table(bases.T.reshape(low + EDGE, plan.px, nx).transpose(1, 0, 2))
    base_y = plan.y["base"].reshape(plan.py, ny, modes)
    edge_y = plan.y["edges"].reshape(plan.py, ny, EDGE)
    right, corner, edge = [], [], []
    for at in range(plan.py):
        high, small = parts_of(kron(2, base_y[at]))
        right.append(np.concatenate([high, small], 1))
        corner.append(bf16(kron(2, np.repeat(edge_y[at], EDGE, 1))))
        edge.append(bf16(np.pad(np.tile(edge_y[at].T, (1, 2)), ((0, EDGE), (0, 0)))))
    pick = np.zeros((2 * EDGE, 2 * ny))
    for i in range(windows):
        pick[i, [i, ny + i]] = 1
        pick[windows + i, [ny - windows + i, 2 * ny - windows + i]] = 1

    def kernel(state_ref, left_ref, right_ref, corner_ref, edge_ref, pick_ref, rates_ref, out_ref):
        px, py = lax.axis_index("px"), lax.axis_index("py")
        field = jnp.concatenate([state_ref[0, level] for level in range(levels)], 1)
        rows = dot(left_ref[px], stacked(field))
        width = 2 * ny
        both = jnp.concatenate([rows[:low, i * width : (i + 1) * width] for i in range(half)], 0)
        high, small = halves(both)
        table = right_ref[py]
        found = dot(high, table)
        found = found[:, :ny] + found[:, ny:] + dot(small, table[:, :ny])
        out_ref[:modes] = jnp.concatenate([found[i * low : i * low + modes] for i in range(half)], 1)
        ends = jnp.concatenate([found[i * low + modes : (i + 1) * low] for i in range(half)], 1)
        cells = jnp.concatenate([rows[modes:low, i * width : (i + 1) * width] for i in range(half)], 0)
        cells = dot(jnp.concatenate(halves(cells), 0), corner_ref[py])
        cells = cells[: half * EDGE] + cells[half * EDGE :]
        cells = jnp.concatenate([cells[i * EDGE : (i + 1) * EDGE] for i in range(half)], 1)
        row = lax.broadcasted_iota(jnp.int32, (EDGE, lanes), 0)
        lane = lax.broadcasted_iota(jnp.int32, (EDGE, lanes), 1)
        cells = jnp.sum(jnp.where(lane % EDGE == row, cells, 0.0), 0, keepdims=True)
        gain = jnp.zeros((EDGE, lanes), jnp.float32)
        for i in range(levels):
            gain = jnp.where(lane // modes == i, rates_ref[0, i], gain)
        gain = jnp.where((px == 0) & (py == 0), gain, 0.0)
        ends = jnp.where(row == EDGE - 1, gain, jnp.where(row == EDGE - 2, cells, ends))
        out_ref[modes:low] = ends
        upright = jnp.concatenate([rows[:modes, i * ny : (i + 1) * ny] for i in range(levels)], 0)
        upright = jnp.concatenate(halves(upright), 1)
        out_ref[low : plan.sums] = dot(edge_ref[py], upright, ((1,), (1,)))[:EDGE]
        patch = jnp.concatenate([state_ref[0, level] for level in range(levels)], 0)
        patch = jnp.concatenate(halves(patch), 1)
        out_ref[plan.sums :] = dot(pick_ref[...], patch, ((1,), (1,)))[:EDGE]

    return call(
        kernel,
        shape_of(plan.rows, lanes),
        state, left, jnp.asarray(np.stack(right)), jnp.asarray(np.stack(corner)), jnp.asarray(np.stack(edge)),
        jnp.asarray(bf16(pick)), rates,
        first=True,
    )


def facing(plan, state_ref, columns, bottom):
    rows = []
    for group in range(plan.half):
        pair = [state_ref[0, 2 * group + i] for i in range(2)]
        top = jnp.concatenate([p[: plan.windows] for p in pair], 1)
        end = jnp.concatenate([p[plan.nx - plan.windows :] for p in pair], 1)
        rows.append(jnp.where(bottom, end, top))
    lane = lax.broadcasted_iota(jnp.int32, (EDGE, plan.lanes), 1)
    moved = pltpu.roll(columns, plan.lanes - (plan.nx - plan.windows), 1)
    near = jnp.where(lane % plan.nx < plan.windows, jnp.where(bottom, moved, columns), 0.0)
    packed = near[:1]
    for i in range(1, 2 * plan.windows):
        packed = packed + pltpu.roll(near, EDGE * i, 1)[i : i + 1]
    return jnp.concatenate(rows + [packed, jnp.zeros((1, plan.lanes), jnp.float32)], 0)


def join_first(plan, own, other, state, columns):
    sums = plan.sums

    def kernel(own_ref, other_ref, state_ref, columns_ref, out_ref, next_ref):
        odd = lax.axis_index("px") % 2 == 1
        out_ref[:sums] = own_ref[:sums] + other_ref[:sums]
        out_ref[sums:] = facing(plan, state_ref, columns_ref[sums:], jnp.logical_not(odd))
        next_ref[...] = facing(plan, state_ref, columns_ref[sums:], odd)

    shapes = shape_of(plan.rows, plan.lanes), shape_of(EDGE, plan.lanes)
    return call(kernel, shapes, own, other, state, columns)


def join_second(plan, own, other, halo):
    sums = plan.sums

    def kernel(own_ref, other_ref, halo_ref, out_ref):
        out_ref[:sums] = own_ref[:sums] + other_ref[:sums]
        out_ref[sums:] = halo_ref[...]

    return call(kernel, shape_of(plan.rows, plan.lanes), own, other, halo)


def join_last(plan, own, other):
    sums = plan.sums

    def kernel(own_ref, other_ref, out_ref):
        out_ref[...] = own_ref[:sums] + other_ref[:sums]

    return call(kernel, shape_of(sums, plan.lanes), own, other)


def step_patch(plan, state, columns, got_first, got_second):
    nx, ny, windows, sums, levels = plan.nx, plan.ny, plan.windows, plan.sums, plan.levels
    place = np.zeros((4 * EDGE, ny))
    for i in range(windows):
        for part in range(3):
            place[part * EDGE + i, i] = 1
            place[part * EDGE + windows + i, ny - windows + i] = 1
    rows, lanes = nx + 2 * EDGE, 2 * ny

    def kernel(state_ref, columns_ref, first_ref, second_ref, place_ref, out_ref):
        px, py = lax.axis_index("px"), lax.axis_index("py")
        row = lax.broadcasted_iota(jnp.int32, (rows, lanes), 0) - EDGE + px * nx
        lane = lax.broadcasted_iota(jnp.int32, (rows, lanes), 1)
        lane = jnp.where(lane >= ny + ny // 2, lane - lanes, lane) + py * ny
        inside = (row >= 0) & (row < nx * plan.px) & (lane >= 0) & (lane < ny * plan.py)
        where = place_ref[...]

        def spread(block):
            high = block.astype(jnp.bfloat16).astype(jnp.float32)
            rest = block - high
            middle = rest.astype(jnp.bfloat16).astype(jnp.float32)
            parts = [high, middle, rest - middle, jnp.zeros_like(high)]
            return dot(jnp.concatenate(parts, 0).astype(jnp.bfloat16), where, ((0,), (0,)))

        small_row = lax.broadcasted_iota(jnp.int32, (EDGE, plan.lanes), 0)
        small_lane = lax.broadcasted_iota(jnp.int32, (EDGE, plan.lanes), 1)
        mine = small_lane % nx // EDGE == small_row

        def corners(block):
            line = jnp.broadcast_to(block[2 * windows : 2 * windows + 1], (EDGE, plan.lanes))
            cells = spread(jnp.where(mine, line, 0.0))
            return [
                sum(cells[level * nx + EDGE * i : level * nx + EDGE * (i + 1)] for i in range(2 * windows))
                for level in range(levels)
            ]

        even = px % 2 == 0
        one, two = first_ref[sums:], second_ref[sums:]
        above, below = jnp.where(even, two, one), jnp.where(even, one, two)
        beside = spread(columns_ref[sums:])
        beside_above, beside_below = corners(above), corners(below)
        blank = jnp.zeros((EDGE - windows, lanes), jnp.float32)
        for level in range(levels):
            pair, part = level // 2, level % 2

            def line(block):
                return block[pair * windows : (pair + 1) * windows, part * ny : (part + 1) * ny]

            up = jnp.concatenate([line(above), beside_above[level][:windows]], 1)
            down = jnp.concatenate([line(below), beside_below[level][:windows]], 1)
            middle = jnp.concatenate([state_ref[0, level], beside[level * nx : (level + 1) * nx]], 1)
            field = jnp.concatenate([blank, up, middle, down, blank], 0)
            field = jnp.where(inside, field, 0.0)
            for _ in range(windows):
                around = (
                    pltpu.roll(field, 1, 0)
                    + pltpu.roll(field, rows - 1, 0)
                    + pltpu.roll(field, 1, 1)
                    + pltpu.roll(field, lanes - 1, 1)
                )
                field = jnp.where(inside, field + RATE * (around - 4.0 * field), 0.0)
            out_ref[level] = field[EDGE : EDGE + nx, :ny]

    return call(
        kernel, shape_of(levels, nx, ny), state, columns, got_first, got_second, jnp.asarray(bf16(place))
    )


def prepare(plan, drive, nest_offsets):
    modes, lanes, levels, windows = plan.modes, plan.lanes, plan.levels, plan.windows
    nx, ny, x, y = plan.nx, plan.ny, plan.x, plan.y
    steps = plan.nest - 1
    maps_x = f32(np.stack([np.tile(x[name], (1, 2)) for name in ("cos_map", "sin_map")]))
    maps_y = f32(np.stack([kron(2, y[name].T) for name in ("cos_map", "sin_map")]))
    rows_x = np.stack([np.tile(p, (1, 2)).reshape(plan.px, nx, 2 * modes) for p in x["powers"][:windows]], 1)
    rows_y = np.stack(
        [p.reshape(plan.py, ny, modes).transpose(0, 2, 1) for p in y["powers"][:windows]], 1
    )

    def kernel(
        drive_ref, maps_x_ref, maps_y_ref, rows_x_ref, rows_y_ref, offsets_ref,
        drive_out, row_out, col_out, spread_x_out, spread_y_out,
    ):
        nest, px, py = lax.axis_index("nest"), lax.axis_index("px"), lax.axis_index("py")
        for w in range(windows):
            drive_out[w] = jnp.concatenate([drive_ref[w, level] for level in range(levels)], 1)
        lane = lax.broadcasted_iota(jnp.int32, (modes, 2 * modes), 1)

        def as_left(twice):
            rounded = twice.astype(jnp.bfloat16).astype(jnp.float32)
            pair = jnp.where(lane >= modes, twice - rounded, rounded)
            return jnp.concatenate([pair, rounded], 1)[:, : 3 * modes].astype(jnp.bfloat16)

        def angle(mode, offset, cells):
            turn = (mode * offset).astype(jnp.float32)
            turn = turn - jnp.floor(turn / (2.0 * cells)) * (2.0 * cells)
            return turn * (math.pi / cells)

        mode = lax.broadcasted_iota(jnp.int32, (EDGE, 2 * modes), 1) % modes
        row = lax.broadcasted_iota(jnp.int32, (EDGE, 2 * modes), 0)
        upright = lax.broadcasted_iota(jnp.int32, (2 * modes, 2 * modes), 0) % modes
        place = lax.broadcasted_iota(jnp.int32, (2 * modes, 2 * modes), 1)
        along, down = jnp.zeros_like(mode), jnp.zeros_like(upright)
        for slot in range(steps):
            domain = jnp.maximum(nest - slot, 0)
            along = jnp.where(row == slot, offsets_ref[domain, 0], along)
            down = jnp.where(place == slot, offsets_ref[domain, 1], down)
        along = angle(mode, along, nx * plan.px)
        down = angle(upright, down, ny * plan.py)
        cos_x, sin_x = jnp.cos(along), jnp.sin(along)
        cos_y, sin_y = jnp.cos(down), jnp.sin(down)
        for slot in range(steps):
            at = slice(slot, slot + 1)
            row_out[slot] = as_left(maps_x_ref[0] * cos_x[at] - maps_x_ref[1] * sin_x[at])
            col_map = maps_y_ref[0] * cos_y[:, at] - maps_y_ref[1] * sin_y[:, at]
            high, small = halves(col_map)
            upper = jnp.concatenate([high, small], 1)
            lower = jnp.concatenate([high, jnp.zeros_like(high)], 1)
            col_out[slot] = jnp.concatenate([upper, lower], 0)
        for w in range(windows):
            p = windows - 1 - w
            for j in range(windows):
                if j <= p:
                    combined = sum(multinomial(p, i, j) * rows_x_ref[px, i] for i in range(p - j + 1))
                    spread_x_out[w, j * nx : (j + 1) * nx] = as_left(combined)
                else:
                    spread_x_out[w, j * nx : (j + 1) * nx] = jnp.zeros((nx, 3 * modes), jnp.bfloat16)
        for j in range(windows):
            table = rows_y_ref[py, j]
            blank = jnp.zeros_like(table)
            table = jnp.concatenate(
                [jnp.concatenate([table, blank], 1), jnp.concatenate([blank, table], 1)], 0
            )
            high, small = halves(table)
            spread_y_out[j] = jnp.concatenate([high, high, small], 0)

    shapes = (
        shape_of(windows, modes, lanes),
        shape_of(steps, modes, 3 * modes, kind=jnp.bfloat16),
        shape_of(steps, 4 * modes, 4 * modes, kind=jnp.bfloat16),
        shape_of(windows, windows * nx, 3 * modes, kind=jnp.bfloat16),
        shape_of(windows, 6 * modes, 2 * ny, kind=jnp.bfloat16),
    )
    return call(kernel, shapes, drive, maps_x, maps_y, f32(rows_x), f32(rows_y), nest_offsets, first=True)


def nudge(plan, stepped, gathered, prepared):
    modes, low, lanes, levels = plan.modes, plan.low, plan.lanes, plan.levels
    windows, half, nx, ny = plan.windows, plan.half, plan.nx, plan.ny
    x, y, sums = plan.x, plan.y, plan.sums
    pairs, unpairs = plan.pairs, plan.unpairs

    inward = np.concatenate([np.tile(y["spill"][j].T, (1, 2)) for j in range(1, windows + 1)], 1)
    high, small = parts_of(inward)
    inward = jnp.asarray(np.concatenate([high, small, high, np.zeros_like(high)], 0))
    corner = np.concatenate(
        [kron(2, np.repeat(y["spill"][j].T, EDGE, 0)) for j in range(1, windows + 1)], 1
    )
    high, small = parts_of(corner)
    corner = jnp.asarray(np.concatenate([high, high, small], 0))
    across = np.zeros((windows * modes, windows * EDGE))
    for n in range(1, windows + 1):
        for j in range(n):
            across[(n - 1) * modes : n * modes, j * EDGE : (j + 1) * EDGE] = sum(
                multinomial(n, i, j) * x["spill"][i] for i in range(1, n - j + 1)
            )
    high, small = parts_of(across)
    across = jnp.asarray(np.pad(np.concatenate([high, small, high], 1), ((0, 0), (0, 3 * EDGE))))
    scale_x = f32(np.broadcast_to(1.0 + x["factor"][:, None], (modes, lanes)))
    scale_y = f32(np.broadcast_to(np.tile(y["factor"], levels), (EDGE, lanes)))
    again = []
    for p in range(1, windows):
        again.append(sum(multinomial(p, i, 0) * x["within"][i] for i in range(p + 1)))
    again = left_table(np.concatenate(again, 0))
    sideways = jnp.stack([right_table(kron(2, y["within"][j])) for j in range(1, windows)])
    drive, row_maps, col_maps, spread_x, spread_y = prepared

    def kernel(
        stepped_ref, drive_ref, row_ref, col_ref, spread_x_ref, spread_y_ref, inward_ref, corner_ref,
        across_ref, scale_x_ref, scale_y_ref, again_ref, sideways_ref, *refs,
    ):
        slots, (state_ref, modes_ref) = refs[:-2], refs[-2:]
        root = plan.nest - 1
        nest = lax.axis_index("nest")
        scale_x, scale_y = scale_x_ref[...], scale_y_ref[:1]
        row = lax.broadcasted_iota(jnp.int32, (EDGE, lanes), 0)
        lane = lax.broadcasted_iota(jnp.int32, (EDGE, lanes), 1)
        mine = lane % EDGE == row
        left_lane = lax.broadcasted_iota(jnp.int32, (modes, ny), 1) < modes

        def own_modes(ref):
            rows, ends = ref[:modes], ref[modes:low]
            sides = dot(short_stacked(ref[low:sums], 4 * EDGE), inward_ref[...], ((0,), (0,)))
            cells = jnp.where(mine, jnp.broadcast_to(ends[EDGE - 2 : EDGE - 1], (EDGE, lanes)), 0.0)
            cells = jnp.concatenate([cells[:, i * ny : (i + 1) * ny] for i in range(half)], 0)
            high, small = halves(cells)
            cells = dot(jnp.concatenate([high, small, high], 1), corner_ref[...])
            turned, ends = [rows], [ends]
            for j in range(windows):
                at = slice(j * ny, (j + 1) * ny)
                side = [
                    jnp.where(
                        left_lane,
                        sides[2 * i * modes : (2 * i + 1) * modes, at],
                        sides[(2 * i + 1) * modes : (2 * i + 2) * modes, at],
                    )
                    for i in range(half)
                ]
                cell = [cells[i * EDGE : (i + 1) * EDGE, at] for i in range(half)]
                power = scale_y if j == 0 else power * scale_y
                turned.append(rows * power + jnp.concatenate(side, 1))
                ends.append(ends[0] * power + jnp.concatenate(cell, 1))
            over = dot(across_ref[...], short_stacked(jnp.concatenate(ends[:windows], 0), 12 * EDGE))
            result = []
            for n in range(windows):
                turned = [a * scale_x + b for a, b in zip(turned[:-1], turned[1:])]
                result.append(turned[0] + over[n * modes : (n + 1) * modes])
            return result

        def carried(change, count):
            left = dot(again_ref[: count * modes], stacked(change))
            left = [left[i * modes : (i + 1) * modes] for i in range(count)]
            if count == 1:
                return [left[0] + unpairs(times_right(pairs(change), sideways_ref[0]))]
            both = jnp.concatenate([pairs(change), pairs(left[0])], 0)
            once = times_right(both, sideways_ref[0])
            twice = times_right(pairs(change), sideways_ref[1])
            rows = half * modes
            return [left[0] + unpairs(once[:rows]), left[1] + unpairs(2.0 * once[rows:] + twice)]

        owns = [own_modes(ref) for ref in slots]
        coeffs = None
        for slot in range(root, -1, -1):
            gain = slots[slot][low - 1 : low]
            own = owns[slot]
            new, changes, later = [], [], []
            for w in range(windows):
                target = drive_ref[w]
                if slot < root:
                    inner = unpairs(times_right(pairs(coeffs[w]), col_ref[slot]))
                    target = jnp.where(nest <= slot, target, dot(row_ref[slot], stacked(inner)))
                before = own[w]
                for v in range(w):
                    before = before + later[v][w - v - 1]
                change = gain * (target - before)
                if w < windows - 1:
                    later.append(carried(change, windows - 1 - w))
                changes.append(change)
                new.append(before + change)
            coeffs = new
        for level in range(levels):
            modes_ref[0, level] = coeffs[-1][:, level * modes : (level + 1) * modes]
        spread = sum(dot(spread_x_ref[w], stacked(changes[w])) for w in range(windows))
        field = 0.0
        for j in range(windows):
            high, small = halves(pairs(spread[j * nx : (j + 1) * nx]))
            field = field + dot(jnp.concatenate([high, small, high], 1), spread_y_ref[j])
        for level in range(levels):
            at_row, at = level // 2 * nx, level % 2 * ny
            state_ref[0, level] = stepped_ref[level] + field[at_row : at_row + nx, at : at + ny]

    return call(
        kernel,
        (shape_of(1, levels, nx, ny), shape_of(1, levels, modes, modes)),
        stepped, drive, row_maps, col_maps, spread_x, spread_y, inward, corner, across, scale_x, scale_y,
        again, sideways, *gathered,
        final=True,
    )


def swap(value, axis, partner):
    size = lax.axis_size(axis)
    return lax.ppermute(value, axis, [(i, partner(i)) for i in range(size) if 0 <= partner(i) < size])


def body(initial_state, drive_modes, relax_rates, nest_offsets):
    plan = Plan(initial_state, drive_modes)
    share = project(plan, initial_state, relax_rates)
    if plan.py == 2 and plan.px == 4:
        columns = swap(share, "py", lambda i: i ^ 1)
        first, halo = join_first(plan, share, columns, initial_state, columns)
        got_first = swap(first, "px", lambda i: i ^ 1)
        second = join_second(plan, first, got_first, halo)
        second, drive_modes, nest_offsets = lax.optimization_barrier((second, drive_modes, nest_offsets))
        got_second = swap(second, "px", lambda i: i ^ 3)
        prepared = prepare(plan, drive_modes, nest_offsets)
        got_second, prepared = lax.optimization_barrier((got_second, prepared))
        last = join_last(plan, second, got_second)
    else:
        from_right = jnp.arange(plan.rows)[:, None] < plan.sums + plan.windows
        right = swap(share, "py", lambda i: i - 1)
        left = swap(share, "py", lambda i: i + 1)
        columns = jnp.where(from_right, right, left)
        blank = jnp.zeros_like(share)
        first, halo = join_first(plan, share, blank, initial_state, columns)
        second = join_second(plan, first, blank, halo)
        even = lax.axis_index("px") % 2 == 0
        above = swap(jnp.where(even, first, second), "px", lambda i: i + 1)
        below = swap(jnp.where(even, second, first), "px", lambda i: i - 1)
        got_first, got_second = jnp.where(even, below, above), jnp.where(even, above, below)
        total = lax.psum(share[: plan.sums], ("py", "px"))
        last = join_last(plan, total, jnp.zeros_like(total))
        prepared = prepare(plan, drive_modes, nest_offsets)
    gathered = [last] + [swap(last, "nest", lambda i, s=s: i + s) for s in range(1, plan.nest)]
    stepped = step_patch(plan, initial_state, columns, got_first, got_second)
    return nudge(plan, stepped, gathered, prepared)


def solution(mesh):
    return jax.shard_map(
        body,
        mesh=mesh,
        in_specs=(P("nest", None, "px", "py"), P(), P("nest", None), P()),
        out_specs=(P("nest", None, "px", "py"), P("nest", None, None, None)),
        check_vma=False,
    )
```

time: 33.7 us -> 31.2 us (0.926)
  local copies, waits for them, and re-layouts: 5.38 us -> 0.72 us
  waiting for transfers between devices: 3.97 us -> 5.25 us
  starting transfers between devices: 13.7 us -> 14.8 us
    squeeze x2 -> x0, local copies, waits for them, and re-layouts: 2.16 us -> none  [the longest x1 1.18 us: nudge(): lax.dynamic_index_in_dim(right_table(spread_y), lax.axis_index('py'), 0,...]
    ppermute x6, waiting for transfers between devices: 3.97 us -> 5.25 us  [swap(): lax.ppermute(value, axis, [(i, partner(i)) for i in range(size) if 0 <= p...]
    transpose x1 -> x0, local copies, waits for them, and re-layouts: 1.25 us -> none  [body(): drive_modes.transpose(0, 2, 1, 3)]
    ppermute x6, starting transfers between devices: 13.7 us -> 14.8 us  [swap(): lax.ppermute(value, axis, [(i, partner(i)) for i in range(size) if 0 <= p...]
    unnamed x21 -> x24, local copies, waits for them, and re-layouts: 0.83 us -> 0.06 us
    optimization_barrier x0 -> x1, local copies, waits for them, and re-layouts: none -> 0.66 us  [body(): lax.optimization_barrier((second, drive_modes, nest_offsets))]
    gather x2 -> x0, local copies, waits for them, and re-layouts: 0.65 us -> none  [map_angles(): offsets = nest_offsets[jnp.maximum(domain, 0)]]
    pallas_call x6 -> x7, Pallas kernels: 9.16 us -> 9.24 us  [call(): pl.pallas_call(kernel, in_specs=specs, out_specs=jax.tree.map(lambda _: p...]
  transfers between devices with their start and end apart: 6 -> 6, of which waited for: 2 -> 3; matrix products, arithmetic and copies ran while one was open for 17% -> 2% of each run, Pallas kernels for 4% -> 9%
where the time goes in v3:
time: 31.2 us; the launch traced here: 30.9 us
  starting transfers between devices  14.8 us (47%)
  Pallas kernels  9.24 us (30%)
  waiting for transfers between devices  5.25 us (17%)
  between operations  0.84 us (3%)
  local copies, waits for them, and re-layouts  0.72 us (2%)
    ppermute x6, starting transfers between devices, swap(): lax.ppermute(value, axis, [(i, partner(i)) for i in range(size) if 0 <= p...  14.8 us
    pallas_call x7, Pallas kernels, call(): pl.pallas_call(kernel, in_specs=specs, out_specs=jax.tree.map(lambda _: p...  9.24 us
    ppermute x6, waiting for transfers between devices, swap(): lax.ppermute(value, axis, [(i, partner(i)) for i in range(size) if 0 <= p...  5.25 us
    optimization_barrier x1, local copies, waits for them, and re-layouts, body(): lax.optimization_barrier((second, drive_modes, nest_offsets))  0.66 us
  transfers between devices with their start and end apart: 6, of which 3 were waited for; matrix products, arithmetic and copies ran while one was open for 2% of the time, Pallas kernels for 9%

profile of v3, /device:TPU:0, one launch (start us, length us, event | category | flops | bytes accessed | tf_op | source)
XLA Modules:
  0.0 30.9 jit_solution(12388426450771127578)
XLA Ops:
  0.6 0.0 copy-start
  0.6 1.6 %shard_map.221.own_ref = f32[88,256]{1,0:T(8,128)S(1)} custom-call(f32[1,4,64,128]{3,2,1,0:T(8,128)} %state_ref.5, bf16[4,80,192]{2,1,0:T(8,128)(2,1)} %constant.36.clone.left_ref, bf16[2,256,256]{2,1,0:T(8,128)(2,1)} %constant.37.clone.right_ref, bf16[2,256,128]{2,1,0:T(8,128)(2,1)} %constant.38.clone.corner_ref, ...), custom_call_target="tpu_custom_call" | custom-call | tf_op jit(solution)/shard_map/pallas_call | solution.py:116
  2.2 3.0 %collective-permute-start = (f32[88,256]{1,0:T(8,128)S(1)}, f32[88,256]{1,0:T(8,128)S(1)}, u32[]{:S(2)}, u32[]{:S(2)}) collective-permute-start(f32[88,256]{1,0:T(8,128)S(1)} %shard_map.221.own_ref), channel_id=1, source_target_pairs={{0,4},{4,0},{1,5},{5,1},{2,6},{6,2},{3,7},{7,3},{8,12},{12,8},{9,1... | collective-permute-start | bytes 270344 | tf_op jit(solution)/shard_map/ppermute | solution.py:534
  5.3 2.6 %collective-permute-done.other_ref.columns_ref = f32[88,256]{1,0:T(8,128)S(1)} collective-permute-done((f32[88,256]{1,0:T(8,128)S(1)}, f32[88,256]{1,0:T(8,128)S(1)}, u32[]{:S(2)}, u32[]{:S(2)}) %collective-permute-start) | collective-permute-done | bytes 90144 | tf_op jit(solution)/shard_map/ppermute | solution.py:534
  7.9 0.0 copy-done
  7.9 0.2 shard_map.222
  8.0 2.0 %collective-permute-start.1 = (f32[88,256]{1,0:T(8,128)S(1)}, f32[88,256]{1,0:T(8,128)S(1)}, u32[]{:S(2)}, u32[]{:S(2)}) collective-permute-start(f32[88,256]{1,0:T(8,128)S(1)} %get-tuple-element.18.own_ref), channel_id=1, source_target_pairs={{0,1},{1,0},{2,3},{3,2},{4,5},{5,4},{6,7},{7,6},{8,9},{9,8},{10,11... | collective-permute-start | bytes 270344 | tf_op jit(solution)/shard_map/ppermute | solution.py:534
  10.1 2.6 %collective-permute-done.1.other_ref.first_ref = f32[88,256]{1,0:T(8,128)S(1)} collective-permute-done((f32[88,256]{1,0:T(8,128)S(1)}, f32[88,256]{1,0:T(8,128)S(1)}, u32[]{:S(2)}, u32[]{:S(2)}) %collective-permute-start.1) | collective-permute-done | bytes 90144 | tf_op jit(solution)/shard_map/ppermute | solution.py:534
  12.6 0.0 copy-start.11
  12.7 4.1 %collective-permute-start.2 = (f32[88,256]{1,0:T(8,128)S(1)}, f32[88,256]{1,0:T(8,128)S(1)}, u32[]{:S(2)}, u32[]{:S(2)}) collective-permute-start(f32[88,256]{1,0:T(8,128)S(1)} %shard_map.223.own_ref), channel_id=1, source_target_pairs={{0,3},{1,2},{2,1},{3,0},{4,7},{5,6},{6,5},{7,4},{8,11},{9,10},{10,... | collective-permute-start | bytes 270344 | tf_op jit(solution)/shard_map/ppermute | solution.py:534
  16.7 0.0 copy-done.11
  16.7 0.7 %copy.24.offsets_ref = s32[4,2]{1,0:T(4,128)} copy(s32[4,2]{0,1:T(2,128)S(1)} %copy-done.11) | data formatting | bytes 64 | tf_op jit(solution)/shard_map/optimization_barrier | solution.py:545
  17.4 0.0 copy-start.10
  17.4 0.0 copy-start.5
  17.4 0.0 copy-start.6
  17.4 0.0 copy-start.8
  17.4 0.0 copy-start.9
  17.4 1.8 %shard_map.224 = (f32[3,64,256]{2,1,0:T(8,128)S(1)}, bf16[3,64,192]{2,1,0:T(8,128)(2,1)S(1)}, bf16[3,256,256]{2,1,0:T(8,128)(2,1)S(1)}, bf16[3,192,192]{2,1,0:T(8,128)(2,1)S(1)}, bf16[3,384,256]{2,1,0:T(8,128)(2,1)S(1)}) custom-call(f32[3,4,64,64]{3,2,1,0:T(8,128)} %drive_ref, f32[2,64,128]{2,1,0:T(8,128)} %constant.41.clone.maps_x_ref, ...), custom_call_target="tpu_custom_call" | custom-call | tf_op jit(solution)/shard_map/pallas_call | solution.py:116
  19.2 0.0 copy-start.3
  19.3 0.1 collective-permute-done.2.second_ref.other_ref
  19.3 0.0 copy-start.2
  19.3 0.0 copy-start.1
  19.3 0.0 copy-start.7
  19.4 1.4 %collective-permute-start.5 = (f32[80,256]{1,0:T(8,128)S(1)}, f32[80,256]{1,0:T(8,128)S(1)}, u32[]{:S(2)}, u32[]{:S(2)}) collective-permute-start(f32[80,256]{1,0:T(8,128)S(1)} %shard_map.226.refs_0_), channel_id=1, source_target_pairs={{0,24},{1,25},{2,26},{3,27},{4,28},{5,29},{6,30},{7,31}} | collective-permute-start | bytes 245768 | tf_op jit(solution)/shard_map/ppermute | solution.py:534
  20.8 3.0 %collective-permute-start.4 = (f32[80,256]{1,0:T(8,128)S(1)}, f32[80,256]{1,0:T(8,128)S(1)}, u32[]{:S(2)}, u32[]{:S(2)}) collective-permute-start(f32[80,256]{1,0:T(8,128)S(1)} %shard_map.226.refs_0_), channel_id=1, source_target_pairs={{0,16},{8,24},{1,17},{9,25},{2,18},{10,26},{3,19},{11,27},{4,20},{... | collective-permute-start | bytes 245768 | tf_op jit(solution)/shard_map/ppermute | solution.py:534
  23.8 0.0 copy-done.3
  23.8 1.3 %collective-permute-start.3 = (f32[80,256]{1,0:T(8,128)S(1)}, f32[80,256]{1,0:T(8,128)S(1)}, u32[]{:S(2)}, u32[]{:S(2)}) collective-permute-start(f32[80,256]{1,0:T(8,128)S(1)} %shard_map.226.refs_0_), channel_id=1, source_target_pairs={{0,8},{8,16},{16,24},{1,9},{9,17},{17,25},{2,10},{10,18},{18,26},{... | collective-permute-start | bytes 245768 | tf_op jit(solution)/shard_map/ppermute | solution.py:534
  25.1 0.0 copy-done.10
  25.1 0.0 copy-start.4
  25.1 0.9 %shard_map.225.stepped_ref = f32[4,64,128]{2,1,0:T(8,128)S(1)} custom-call(f32[1,4,64,128]{3,2,1,0:T(8,128)S(1)} %copy-done, f32[88,256]{1,0:T(8,128)S(1)} %collective-permute-done.other_ref.columns_ref, f32[88,256]{1,0:T(8,128)S(1)} %collective-permute-done.1.other_ref.first_ref, f32[88,256]{1,0:T(8,128)S(1)} %collective-permute-done.2.second_ref.other_ref, ...), custom_call_target="tpu_custom_call" | custom-call | tf_op jit(solution)/shard_map/pallas_call | solution.py:116
  26.1 0.0 collective-permute-done.5.refs_3_
  26.1 0.0 collective-permute-done.4.refs_2_
  26.1 0.0 collective-permute-done.3.refs_1_
  26.1 0.0 copy-done.5
  26.1 0.0 copy-done.6
  26.1 0.0 copy-done.8
  26.1 0.0 copy-done.9
  26.1 0.0 copy-done.2
  26.1 0.0 copy-done.1
  26.2 0.0 copy-done.7
  26.2 0.0 copy-done.4
  26.2 4.7 %shard_map.227 = (f32[1,4,64,128]{3,2,1,0:T(8,128)}, f32[1,4,64,64]{3,2,1,0:T(8,128)}) custom-call(f32[4,64,128]{2,1,0:T(8,128)S(1)} %shard_map.225.stepped_ref, f32[3,64,256]{2,1,0:T(8,128)S(1)} %copy-done.4, bf16[3,64,192]{2,1,0:T(8,128)(2,1)S(1)} %get-tuple-element.30.row_ref, bf16[3,256,256]{2,1,0:T(8,128)(2,1)S(1)} %get-tuple-element.31.col_ref, ...), custom_call_target="tpu_custom_call" | custom-call | tf_op jit(solution)/shard_map/pallas_call | solution.py:116
  (2 shorter events, 0.0 us)
Async XLA Ops:
  0.6 7.2 %copy-start = (f32[1,4,64,128]{3,2,1,0:T(8,128)S(1)}, f32[1,4,64,128]{3,2,1,0:T(8,128)}, u32[]{:S(2)}) copy-start(f32[1,4,64,128]{3,2,1,0:T(8,128)} %state_ref.5) | copy-start | bytes 393220
  2.2 5.6 %collective-permute-start = (f32[88,256]{1,0:T(8,128)S(1)}, f32[88,256]{1,0:T(8,128)S(1)}, u32[]{:S(2)}, u32[]{:S(2)}) collective-permute-start(f32[88,256]{1,0:T(8,128)S(1)} %shard_map.221.own_ref), channel_id=1, source_target_pairs={{0,4},{4,0},{1,5},{5,1},{2,6},{6,2},{3,7},{7,3},{8,12},{12,8},{9,1... | collective-permute-start | bytes 270344 | tf_op jit(solution)/shard_map/ppermute | solution.py:534
  8.0 4.6 %collective-permute-start.1 = (f32[88,256]{1,0:T(8,128)S(1)}, f32[88,256]{1,0:T(8,128)S(1)}, u32[]{:S(2)}, u32[]{:S(2)}) collective-permute-start(f32[88,256]{1,0:T(8,128)S(1)} %get-tuple-element.18.own_ref), channel_id=1, source_target_pairs={{0,1},{1,0},{2,3},{3,2},{4,5},{5,4},{6,7},{7,6},{8,9},{9,8},{10,11... | collective-permute-start | bytes 270344 | tf_op jit(solution)/shard_map/ppermute | solution.py:534
  12.6 4.1 %copy-start.11 = (s32[4,2]{0,1:T(2,128)S(1)}, s32[4,2]{0,1:T(2,128)}, u32[]{:S(2)}) copy-start(s32[4,2]{0,1:T(2,128)} %param.25) | copy-start | bytes 100
  12.7 6.7 %collective-permute-start.2 = (f32[88,256]{1,0:T(8,128)S(1)}, f32[88,256]{1,0:T(8,128)S(1)}, u32[]{:S(2)}, u32[]{:S(2)}) collective-permute-start(f32[88,256]{1,0:T(8,128)S(1)} %shard_map.223.own_ref), channel_id=1, source_target_pairs={{0,3},{1,2},{2,1},{3,0},{4,7},{5,6},{6,5},{7,4},{8,11},{9,10},{10,... | collective-permute-start | bytes 270344 | tf_op jit(solution)/shard_map/ppermute | solution.py:534
  17.4 7.7 %copy-start.10 = (bf16[32,128]{1,0:T(8,128)(2,1)S(1)}, bf16[32,128]{1,0:T(8,128)(2,1)}, u32[]{:S(2)}) copy-start(bf16[32,128]{1,0:T(8,128)(2,1)} %constant.45.clone.place_ref) | copy-start | bytes 24580
  17.4 8.7 %copy-start.5 = (bf16[128,192]{1,0:T(8,128)(2,1)S(1)}, bf16[128,192]{1,0:T(8,128)(2,1)}, u32[]{:S(2)}) copy-start(bf16[128,192]{1,0:T(8,128)(2,1)} %constant.51.clone.again_ref) | copy-start | bytes 147460
  17.4 8.7 %copy-start.6 = (f32[64,256]{1,0:T(8,128)S(1)}, f32[64,256]{1,0:T(8,128)}, u32[]{:S(2)}) copy-start(f32[64,256]{1,0:T(8,128)} %constant.49.clone.scale_x_ref) | copy-start | bytes 196612
  17.4 8.7 %copy-start.8 = (bf16[32,384]{1,0:T(8,128)(2,1)S(1)}, bf16[32,384]{1,0:T(8,128)(2,1)}, u32[]{:S(2)}) copy-start(bf16[32,384]{1,0:T(8,128)(2,1)} %constant.46.clone.inward_ref) | copy-start | bytes 73732
  17.4 8.7 %copy-start.9 = (f32[8,256]{1,0:T(8,128)S(1)}, f32[8,256]{1,0:T(8,128)}, u32[]{:S(2)}) copy-start(f32[8,256]{1,0:T(8,128)} %constant.50.clone.scale_y_ref) | copy-start | bytes 24580
  19.2 4.5 %copy-start.3 = (f32[3,64,256]{2,1,0:T(8,128)}, f32[3,64,256]{2,1,0:T(8,128)S(1)}, u32[]{:S(2)}) copy-start(f32[3,64,256]{2,1,0:T(8,128)S(1)} %get-tuple-element.29.drive_ref) | copy-start | bytes 589828
  19.3 6.8 %copy-start.2 = (bf16[2,256,256]{2,1,0:T(8,128)(2,1)S(1)}, bf16[2,256,256]{2,1,0:T(8,128)(2,1)}, u32[]{:S(2)}) copy-start(bf16[2,256,256]{2,1,0:T(8,128)(2,1)} %constant.58.sideways_ref) | copy-start | bytes 786436
  19.3 6.8 %copy-start.1 = (bf16[384,384]{1,0:T(8,128)(2,1)S(1)}, bf16[384,384]{1,0:T(8,128)(2,1)}, u32[]{:S(2)}) copy-start(bf16[384,384]{1,0:T(8,128)(2,1)} %constant.47.clone.corner_ref) | copy-start | bytes 884740
  19.3 6.8 %copy-start.7 = (bf16[192,96]{1,0:T(8,128)(2,1)S(1)}, bf16[192,96]{1,0:T(8,128)(2,1)}, u32[]{:S(2)}) copy-start(bf16[192,96]{1,0:T(8,128)(2,1)} %constant.48.clone.across_ref) | copy-start | bytes 110596
  19.4 6.7 %collective-permute-start.5 = (f32[80,256]{1,0:T(8,128)S(1)}, f32[80,256]{1,0:T(8,128)S(1)}, u32[]{:S(2)}, u32[]{:S(2)}) collective-permute-start(f32[80,256]{1,0:T(8,128)S(1)} %shard_map.226.refs_0_), channel_id=1, source_target_pairs={{0,24},{1,25},{2,26},{3,27},{4,28},{5,29},{6,30},{7,31}} | collective-permute-start | bytes 245768 | tf_op jit(solution)/shard_map/ppermute | solution.py:534
  20.8 5.3 %collective-permute-start.4 = (f32[80,256]{1,0:T(8,128)S(1)}, f32[80,256]{1,0:T(8,128)S(1)}, u32[]{:S(2)}, u32[]{:S(2)}) collective-permute-start(f32[80,256]{1,0:T(8,128)S(1)} %shard_map.226.refs_0_), channel_id=1, source_target_pairs={{0,16},{8,24},{1,17},{9,25},{2,18},{10,26},{3,19},{11,27},{4,20},{... | collective-permute-start | bytes 245768 | tf_op jit(solution)/shard_map/ppermute | solution.py:534
  23.8 2.3 %collective-permute-start.3 = (f32[80,256]{1,0:T(8,128)S(1)}, f32[80,256]{1,0:T(8,128)S(1)}, u32[]{:S(2)}, u32[]{:S(2)}) collective-permute-start(f32[80,256]{1,0:T(8,128)S(1)} %shard_map.226.refs_0_), channel_id=1, source_target_pairs={{0,8},{8,16},{16,24},{1,9},{9,17},{17,25},{2,10},{10,18},{18,26},{... | collective-permute-start | bytes 245768 | tf_op jit(solution)/shard_map/ppermute | solution.py:534
  25.1 1.1 %copy-start.4 = (f32[3,64,256]{2,1,0:T(8,128)S(1)}, f32[3,64,256]{2,1,0:T(8,128)}, u32[]{:S(2)}) copy-start(f32[3,64,256]{2,1,0:T(8,128)} %copy-done.3) | copy-start | bytes 589828

commit v4 on v3

--- a/solution.py
+++ b/solution.py
@@ -104,6 +104,12 @@
     return out[:, :width] + out[:, width:]
 
 
+def by_parts(value, table, rest):
+    high, low = halves(value)
+    out = dot(jnp.concatenate([high, low], 0), table)
+    return out[: value.shape[0]] + out[value.shape[0] :] + dot(high, rest)
+
+
 def in_vmem(value):
     return value if INTERPRET else pltpu.with_memory_space_constraint(value, pltpu.VMEM)
 
@@ -170,7 +176,7 @@
         pick[i, [i, ny + i]] = 1
         pick[windows + i, [ny - windows + i, 2 * ny - windows + i]] = 1
 
-    def kernel(state_ref, left_ref, right_ref, corner_ref, edge_ref, pick_ref, rates_ref, out_ref):
+    def kernel(state_ref, left_ref, right_ref, corner_ref, edge_ref, pick_ref, rates_ref, out_ref, along_ref):
         px, py = lax.axis_index("px"), lax.axis_index("py")
         field = jnp.concatenate([state_ref[0, level] for level in range(levels)], 1)
         rows = dot(left_ref[px], stacked(field))
@@ -201,53 +207,62 @@
         patch = jnp.concatenate([state_ref[0, level] for level in range(levels)], 0)
         patch = jnp.concatenate(halves(patch), 1)
         out_ref[plan.sums :] = dot(pick_ref[...], patch, ((1,), (1,)))[:EDGE]
+        along_ref[: plan.sums] = out_ref[: plan.sums]
+        lines = facing_rows(plan, state_ref, px % 2 == 0)
+        along_ref[plan.sums :] = jnp.concatenate([lines, jnp.zeros((2, lanes), jnp.float32)], 0)
 
     return call(
         kernel,
-        shape_of(plan.rows, lanes),
+        (shape_of(plan.rows, lanes), shape_of(plan.rows, lanes)),
         state, left, jnp.asarray(np.stack(right)), jnp.asarray(np.stack(corner)), jnp.asarray(np.stack(edge)),
         jnp.asarray(bf16(pick)), rates,
         first=True,
     )
 
 
-def facing(plan, state_ref, columns, bottom):
+def facing_rows(plan, state_ref, bottom):
     rows = []
     for group in range(plan.half):
         pair = [state_ref[0, 2 * group + i] for i in range(2)]
         top = jnp.concatenate([p[: plan.windows] for p in pair], 1)
         end = jnp.concatenate([p[plan.nx - plan.windows :] for p in pair], 1)
         rows.append(jnp.where(bottom, end, top))
+    return jnp.concatenate(rows, 0)
+
+
+def facing_corners(plan, columns, bottom):
     lane = lax.broadcasted_iota(jnp.int32, (EDGE, plan.lanes), 1)
     moved = pltpu.roll(columns, plan.lanes - (plan.nx - plan.windows), 1)
     near = jnp.where(lane % plan.nx < plan.windows, jnp.where(bottom, moved, columns), 0.0)
     packed = near[:1]
     for i in range(1, 2 * plan.windows):
         packed = packed + pltpu.roll(near, EDGE * i, 1)[i : i + 1]
-    return jnp.concatenate(rows + [packed, jnp.zeros((1, plan.lanes), jnp.float32)], 0)
-
-
-def join_first(plan, own, other, state, columns):
-    sums = plan.sums
-
-    def kernel(own_ref, other_ref, state_ref, columns_ref, out_ref, next_ref):
+    return jnp.concatenate([packed, jnp.zeros((1, plan.lanes), jnp.float32)], 0)
+
+
+def join_first(plan, own, from_y, from_x, from_both, state):
+    sums, windows = plan.sums, plan.windows
+
+    def kernel(own_ref, y_ref, x_ref, both_ref, state_ref, out_ref, halo_ref):
         odd = lax.axis_index("px") % 2 == 1
-        out_ref[:sums] = own_ref[:sums] + other_ref[:sums]
-        out_ref[sums:] = facing(plan, state_ref, columns_ref[sums:], jnp.logical_not(odd))
-        next_ref[...] = facing(plan, state_ref, columns_ref[sums:], odd)
+        out_ref[:sums] = (own_ref[:sums] + y_ref[:sums]) + (x_ref[:sums] + both_ref[:sums])
+        corners = facing_corners(plan, y_ref[sums:], odd)
+        out_ref[sums:] = jnp.concatenate([facing_rows(plan, state_ref, odd), corners], 0)
+        corners = facing_corners(plan, both_ref[sums:], odd)
+        halo_ref[...] = jnp.concatenate([x_ref[sums : sums + 2 * windows], corners], 0)
 
     shapes = shape_of(plan.rows, plan.lanes), shape_of(EDGE, plan.lanes)
-    return call(kernel, shapes, own, other, state, columns)
-
-
-def join_second(plan, own, other, halo):
-    sums = plan.sums
-
-    def kernel(own_ref, other_ref, halo_ref, out_ref):
-        out_ref[:sums] = own_ref[:sums] + other_ref[:sums]
-        out_ref[sums:] = halo_ref[...]
-
-    return call(kernel, shape_of(plan.rows, plan.lanes), own, other, halo)
+    return call(kernel, shapes, own, from_y, from_x, from_both, state)
+
+
+def both_facing(plan, state, columns):
+    def kernel(state_ref, columns_ref, top_ref, bottom_ref):
+        columns = columns_ref[plan.sums :]
+        for ref, bottom in ((top_ref, False), (bottom_ref, True)):
+            rows = [facing_rows(plan, state_ref, bottom), facing_corners(plan, columns, bottom)]
+            ref[...] = jnp.concatenate(rows, 0)
+
+    return call(kernel, (shape_of(EDGE, plan.lanes),) * 2, state, columns)
 
 
 def join_last(plan, own, other):
@@ -259,7 +274,7 @@
     return call(kernel, shape_of(sums, plan.lanes), own, other)
 
 
-def step_patch(plan, state, columns, got_first, got_second):
+def step_patch(plan, state, columns, first, second):
     nx, ny, windows, sums, levels = plan.nx, plan.ny, plan.windows, plan.sums, plan.levels
     place = np.zeros((4 * EDGE, ny))
     for i in range(windows):
@@ -296,7 +311,7 @@
             ]
 
         even = px % 2 == 0
-        one, two = first_ref[sums:], second_ref[sums:]
+        one, two = first_ref[...], second_ref[second_ref.shape[0] - EDGE :]
         above, below = jnp.where(even, two, one), jnp.where(even, one, two)
         beside = spread(columns_ref[sums:])
         beside_above, beside_below = corners(above), corners(below)
@@ -323,7 +338,7 @@
             out_ref[level] = field[EDGE : EDGE + nx, :ny]
 
     return call(
-        kernel, shape_of(levels, nx, ny), state, columns, got_first, got_second, jnp.asarray(bf16(place))
+        kernel, shape_of(levels, nx, ny), state, columns, first, second, jnp.asarray(bf16(place))
     )
 
 
@@ -364,8 +379,8 @@
         along, down = jnp.zeros_like(mode), jnp.zeros_like(upright)
         for slot in range(steps):
             domain = jnp.maximum(nest - slot, 0)
-            along = jnp.where(row == slot, offsets_ref[domain, 0], along)
-            down = jnp.where(place == slot, offsets_ref[domain, 1], down)
+            along = jnp.where(row == slot, offsets_ref[0, domain], along)
+            down = jnp.where(place == slot, offsets_ref[1, domain], down)
         along = angle(mode, along, nx * plan.px)
         down = angle(upright, down, ny * plan.py)
         cos_x, sin_x = jnp.cos(along), jnp.sin(along)
@@ -393,19 +408,19 @@
                 [jnp.concatenate([table, blank], 1), jnp.concatenate([blank, table], 1)], 0
             )
             high, small = halves(table)
-            spread_y_out[j] = jnp.concatenate([high, high, small], 0)
+            spread_y_out[j] = jnp.concatenate([high, small], 0)
 
     shapes = (
         shape_of(windows, modes, lanes),
         shape_of(steps, modes, 3 * modes, kind=jnp.bfloat16),
         shape_of(steps, 4 * modes, 4 * modes, kind=jnp.bfloat16),
         shape_of(windows, windows * nx, 3 * modes, kind=jnp.bfloat16),
-        shape_of(windows, 6 * modes, 2 * ny, kind=jnp.bfloat16),
-    )
-    return call(kernel, shapes, drive, maps_x, maps_y, f32(rows_x), f32(rows_y), nest_offsets, first=True)
-
-
-def nudge(plan, stepped, gathered, prepared):
+        shape_of(windows, 4 * modes, 2 * ny, kind=jnp.bfloat16),
+    )
+    return call(kernel, shapes, drive, maps_x, maps_y, f32(rows_x), f32(rows_y), nest_offsets.T, first=True)
+
+
+def nudge(plan, stepped, gathered, crossed, prepared):
     modes, low, lanes, levels = plan.modes, plan.low, plan.lanes, plan.levels
     windows, half, nx, ny = plan.windows, plan.half, plan.nx, plan.ny
     x, y, sums = plan.x, plan.y, plan.sums
@@ -418,7 +433,7 @@
         [kron(2, np.repeat(y["spill"][j].T, EDGE, 0)) for j in range(1, windows + 1)], 1
     )
     high, small = parts_of(corner)
-    corner = jnp.asarray(np.concatenate([high, high, small], 0))
+    corner = jnp.asarray(np.concatenate([high, small], 0))
     across = np.zeros((windows * modes, windows * EDGE))
     for n in range(1, windows + 1):
         for j in range(n):
@@ -440,22 +455,24 @@
         stepped_ref, drive_ref, row_ref, col_ref, spread_x_ref, spread_y_ref, inward_ref, corner_ref,
         across_ref, scale_x_ref, scale_y_ref, again_ref, sideways_ref, *refs,
     ):
-        slots, (state_ref, modes_ref) = refs[:-2], refs[-2:]
+        refs, (state_ref, modes_ref) = refs[:-2], refs[-2:]
         root = plan.nest - 1
         nest = lax.axis_index("nest")
+        slots = [ref[...] for ref in refs]
+        if crossed:
+            slots = [slots[0], jnp.where(nest % 2 == 1, slots[2], slots[3]), slots[1], slots[3]]
         scale_x, scale_y = scale_x_ref[...], scale_y_ref[:1]
         row = lax.broadcasted_iota(jnp.int32, (EDGE, lanes), 0)
         lane = lax.broadcasted_iota(jnp.int32, (EDGE, lanes), 1)
         mine = lane % EDGE == row
         left_lane = lax.broadcasted_iota(jnp.int32, (modes, ny), 1) < modes
 
-        def own_modes(ref):
-            rows, ends = ref[:modes], ref[modes:low]
-            sides = dot(short_stacked(ref[low:sums], 4 * EDGE), inward_ref[...], ((0,), (0,)))
+        def own_modes(message):
+            rows, ends = message[:modes], message[modes:low]
+            sides = dot(short_stacked(message[low:sums], 4 * EDGE), inward_ref[...], ((0,), (0,)))
             cells = jnp.where(mine, jnp.broadcast_to(ends[EDGE - 2 : EDGE - 1], (EDGE, lanes)), 0.0)
             cells = jnp.concatenate([cells[:, i * ny : (i + 1) * ny] for i in range(half)], 0)
-            high, small = halves(cells)
-            cells = dot(jnp.concatenate([high, small, high], 1), corner_ref[...])
+            cells = by_parts(cells, corner_ref[:ny], corner_ref[ny:])
             turned, ends = [rows], [ends]
             for j in range(windows):
                 at = slice(j * ny, (j + 1) * ny)
@@ -489,7 +506,7 @@
             rows = half * modes
             return [left[0] + unpairs(once[:rows]), left[1] + unpairs(2.0 * once[rows:] + twice)]
 
-        owns = [own_modes(ref) for ref in slots]
+        owns = [own_modes(slot) for slot in slots]
         coeffs = None
         for slot in range(root, -1, -1):
             gain = slots[slot][low - 1 : low]
@@ -514,8 +531,9 @@
         spread = sum(dot(spread_x_ref[w], stacked(changes[w])) for w in range(windows))
         field = 0.0
         for j in range(windows):
-            high, small = halves(pairs(spread[j * nx : (j + 1) * nx]))
-            field = field + dot(jnp.concatenate([high, small, high], 1), spread_y_ref[j])
+            table = spread_y_ref[j]
+            part = by_parts(pairs(spread[j * nx : (j + 1) * nx]), table[: 2 * modes], table[2 * modes :])
+            field = field + part
         for level in range(levels):
             at_row, at = level // 2 * nx, level % 2 * ny
             state_ref[0, level] = stepped_ref[level] + field[at_row : at_row + nx, at : at + ny]
@@ -530,41 +548,45 @@
 
 
 def swap(value, axis, partner):
-    size = lax.axis_size(axis)
+    size = math.prod(lax.axis_size(name) for name in (axis if isinstance(axis, tuple) else (axis,)))
     return lax.ppermute(value, axis, [(i, partner(i)) for i in range(size) if 0 <= partner(i) < size])
 
 
 def body(initial_state, drive_modes, relax_rates, nest_offsets):
     plan = Plan(initial_state, drive_modes)
-    share = project(plan, initial_state, relax_rates)
+    share, along = project(plan, initial_state, relax_rates)
     if plan.py == 2 and plan.px == 4:
-        columns = swap(share, "py", lambda i: i ^ 1)
-        first, halo = join_first(plan, share, columns, initial_state, columns)
-        got_first = swap(first, "px", lambda i: i ^ 1)
-        second = join_second(plan, first, got_first, halo)
-        second, drive_modes, nest_offsets = lax.optimization_barrier((second, drive_modes, nest_offsets))
-        got_second = swap(second, "px", lambda i: i ^ 3)
+        share, drive_modes, nest_offsets = lax.optimization_barrier((share, drive_modes, nest_offsets))
+        from_y = swap(share, "py", lambda i: i ^ 1)
+        from_x = swap(along, "px", lambda i: i ^ 1)
+        from_both = swap(share, ("py", "px"), lambda i: i ^ (plan.px + 1))
         prepared = prepare(plan, drive_modes, nest_offsets)
-        got_second, prepared = lax.optimization_barrier((got_second, prepared))
-        last = join_last(plan, second, got_second)
+        from_both, prepared = lax.optimization_barrier((from_both, prepared))
+        total, halo = join_first(plan, share, from_y, from_x, from_both, initial_state)
+        columns = from_y
+        across = swap(total, "px", lambda i: i ^ 3)
+        last = join_last(plan, total, across)
     else:
         from_right = jnp.arange(plan.rows)[:, None] < plan.sums + plan.windows
         right = swap(share, "py", lambda i: i - 1)
         left = swap(share, "py", lambda i: i + 1)
         columns = jnp.where(from_right, right, left)
-        blank = jnp.zeros_like(share)
-        first, halo = join_first(plan, share, blank, initial_state, columns)
-        second = join_second(plan, first, blank, halo)
+        top, bottom = both_facing(plan, initial_state, columns)
+        above = swap(bottom, "px", lambda i: i + 1)
+        below = swap(top, "px", lambda i: i - 1)
         even = lax.axis_index("px") % 2 == 0
-        above = swap(jnp.where(even, first, second), "px", lambda i: i + 1)
-        below = swap(jnp.where(even, second, first), "px", lambda i: i - 1)
-        got_first, got_second = jnp.where(even, below, above), jnp.where(even, above, below)
-        total = lax.psum(share[: plan.sums], ("py", "px"))
-        last = join_last(plan, total, jnp.zeros_like(total))
+        halo, across = jnp.where(even, below, above), jnp.where(even, above, below)
+        last = lax.psum(share[: plan.sums], ("py", "px"))
         prepared = prepare(plan, drive_modes, nest_offsets)
-    gathered = [last] + [swap(last, "nest", lambda i, s=s: i + s) for s in range(1, plan.nest)]
-    stepped = step_patch(plan, initial_state, columns, got_first, got_second)
-    return nudge(plan, stepped, gathered, prepared)
+    crossed = plan.nest == 4
+    if crossed:
+        core = swap(last, "nest", lambda i: i ^ 1)
+        chip = swap(last, "nest", lambda i: i ^ 2)
+        gathered = [last, chip, core, swap(chip, "nest", lambda i: i ^ 1)]
+    else:
+        gathered = [last] + [swap(last, "nest", lambda i, s=s: i + s) for s in range(1, plan.nest)]
+    stepped = step_patch(plan, initial_state, columns, halo, across)
+    return nudge(plan, stepped, gathered, crossed, prepared)
 
 
 def solution(mesh):

time: 31.2 us -> 28.6 us (0.917)
  starting transfers between devices: 14.8 us -> 9.58 us
  waiting for transfers between devices: 5.25 us -> 8.87 us
  local copies, waits for them, and re-layouts: 0.72 us -> 0.04 us
    ppermute x6 -> x7, starting transfers between devices: 14.8 us -> 9.58 us  [swap(): lax.ppermute(value, axis, [(i, partner(i)) for i in range(size) if 0 <= p...]
    ppermute x6 -> x7, waiting for transfers between devices: 5.25 us -> 8.87 us  [swap(): lax.ppermute(value, axis, [(i, partner(i)) for i in range(size) if 0 <= p...]
    optimization_barrier x1 -> x0, local copies, waits for them, and re-layouts: 0.66 us -> none  [body(): lax.optimization_barrier((second, drive_modes, nest_offsets))]
    pallas_call x7 -> x6, Pallas kernels: 9.24 us -> 9.24 us  [call(): pl.pallas_call(kernel, in_specs=specs, out_specs=jax.tree.map(lambda _: p...]
  transfers between devices with their start and end apart: 6 -> 7, of which waited for: 3 -> 6; matrix products, arithmetic and copies ran while one was open for 2% -> 0% of each run, Pallas kernels for 9% -> 10%
where the time goes in v4:
time: 28.6 us; the launch traced here: 28.5 us
  starting transfers between devices  9.58 us (33%)
  Pallas kernels  9.24 us (32%)
  waiting for transfers between devices  8.87 us (31%)
  between operations  0.74 us (3%)
    ppermute x7, starting transfers between devices, swap(): lax.ppermute(value, axis, [(i, partner(i)) for i in range(size) if 0 <= p...  9.58 us
    pallas_call x6, Pallas kernels, call(): pl.pallas_call(kernel, in_specs=specs, out_specs=jax.tree.map(lambda _: p...  9.24 us
    ppermute x7, waiting for transfers between devices, swap(): lax.ppermute(value, axis, [(i, partner(i)) for i in range(size) if 0 <= p...  8.87 us
  transfers between devices with their start and end apart: 7, of which 6 were waited for; matrix products, arithmetic and copies ran while one was open for 0% of the time, Pallas kernels for 10%

profile of v4, /device:TPU:0, one launch (start us, length us, event | category | flops | bytes accessed | tf_op | source)
XLA Modules:
  0.0 28.5 jit_solution(1974784737690151004)
XLA Ops:
  0.6 1.6 %shard_map.221 = (f32[88,256]{1,0:T(8,128)S(1)}, f32[88,256]{1,0:T(8,128)S(1)}) custom-call(f32[1,4,64,128]{3,2,1,0:T(8,128)} %state_ref.5, bf16[4,80,192]{2,1,0:T(8,128)(2,1)} %constant.36.clone.left_ref, bf16[2,256,256]{2,1,0:T(8,128)(2,1)} %constant.37.clone.right_ref, bf16[2,256,128]{2,1,0:T(8,128)(2,1)} %constant.38.clone.corner_ref, ...), custom_call_target="tpu_custom_call" | custom-call | tf_op jit(solution)/shard_map/pallas_call | solution.py:122
  2.2 4.0 %collective-permute-start.2 = (f32[88,256]{1,0:T(8,128)S(1)}, f32[88,256]{1,0:T(8,128)S(1)}, u32[]{:S(2)}, u32[]{:S(2)}) collective-permute-start(f32[88,256]{1,0:T(8,128)S(1)} %get-tuple-element.21.own_ref), channel_id=1, source_target_pairs={{0,5},{1,4},{2,7},{3,6},{4,1},{5,0},{6,3},{7,2},{8,13},{9,12},{10,... | collective-permute-start | bytes 270344 | tf_op jit(solution)/shard_map/ppermute | solution.py:552
  6.2 0.5 %collective-permute-start = (f32[88,256]{1,0:T(8,128)S(1)}, f32[88,256]{1,0:T(8,128)S(1)}, u32[]{:S(2)}, u32[]{:S(2)}) collective-permute-start(f32[88,256]{1,0:T(8,128)S(1)} %get-tuple-element.21.own_ref), channel_id=1, source_target_pairs={{0,4},{4,0},{1,5},{5,1},{2,6},{6,2},{3,7},{7,3},{8,12},{12,8},{9,1... | collective-permute-start | bytes 270344 | tf_op jit(solution)/shard_map/ppermute | solution.py:552
  6.7 0.1 collective-permute-start.1
  6.9 0.0 copy-start
  6.9 1.8 %shard_map.222 = (f32[3,64,256]{2,1,0:T(8,128)S(1)}, bf16[3,64,192]{2,1,0:T(8,128)(2,1)S(1)}, bf16[3,256,256]{2,1,0:T(8,128)(2,1)S(1)}, bf16[3,192,192]{2,1,0:T(8,128)(2,1)S(1)}, bf16[3,256,256]{2,1,0:T(8,128)(2,1)S(1)}) custom-call(f32[3,4,64,64]{3,2,1,0:T(8,128)} %drive_ref, f32[2,64,128]{2,1,0:T(8,128)} %constant.41.clone.maps_x_ref, ...), custom_call_target="tpu_custom_call" | custom-call | tf_op jit(solution)/shard_map/pallas_call | solution.py:122
  8.7 0.4 %collective-permute-done.2.both_ref = f32[88,256]{1,0:T(8,128)S(1)} collective-permute-done((f32[88,256]{1,0:T(8,128)S(1)}, f32[88,256]{1,0:T(8,128)S(1)}, u32[]{:S(2)}, u32[]{:S(2)}) %collective-permute-start.2) | collective-permute-done | bytes 90144 | tf_op jit(solution)/shard_map/ppermute | solution.py:552
  9.1 1.7 %collective-permute-done.y_ref.columns_ref = f32[88,256]{1,0:T(8,128)S(1)} collective-permute-done((f32[88,256]{1,0:T(8,128)S(1)}, f32[88,256]{1,0:T(8,128)S(1)}, u32[]{:S(2)}, u32[]{:S(2)}) %collective-permute-start) | collective-permute-done | bytes 90144 | tf_op jit(solution)/shard_map/ppermute | solution.py:552
  10.8 0.5 %collective-permute-done.1.x_ref = f32[88,256]{1,0:T(8,128)S(1)} collective-permute-done((f32[88,256]{1,0:T(8,128)S(1)}, f32[88,256]{1,0:T(8,128)S(1)}, u32[]{:S(2)}, u32[]{:S(2)}) %collective-permute-start.1) | collective-permute-done | bytes 90144 | tf_op jit(solution)/shard_map/ppermute | solution.py:552
  11.3 0.0 copy-done
  11.3 0.2 shard_map.223
  11.4 0.0 copy-start.8
  11.5 3.3 %collective-permute-start.3 = (f32[88,256]{1,0:T(8,128)S(1)}, f32[88,256]{1,0:T(8,128)S(1)}, u32[]{:S(2)}, u32[]{:S(2)}) collective-permute-start(f32[88,256]{1,0:T(8,128)S(1)} %get-tuple-element.32.own_ref), channel_id=1, source_target_pairs={{0,3},{1,2},{2,1},{3,0},{4,7},{5,6},{6,5},{7,4},{8,11},{9,10},{10,... | collective-permute-start | bytes 270344 | tf_op jit(solution)/shard_map/ppermute | solution.py:552
  14.8 3.1 %collective-permute-done.3.second_ref.other_ref = f32[88,256]{1,0:T(8,128)S(1)} collective-permute-done((f32[88,256]{1,0:T(8,128)S(1)}, f32[88,256]{1,0:T(8,128)S(1)}, u32[]{:S(2)}, u32[]{:S(2)}) %collective-permute-start.3) | collective-permute-done | bytes 90144 | tf_op jit(solution)/shard_map/ppermute | solution.py:552
  17.9 0.0 copy-start.3
  17.9 0.0 copy-start.4
  17.9 0.0 copy-start.5
  17.9 0.0 copy-start.6
  17.9 0.0 copy-start.7
  17.9 0.0 copy-start.1
  17.9 1.6 %collective-permute-start.4 = (f32[80,256]{1,0:T(8,128)S(1)}, f32[80,256]{1,0:T(8,128)S(1)}, u32[]{:S(2)}, u32[]{:S(2)}) collective-permute-start(f32[80,256]{1,0:T(8,128)S(1)} %shard_map.225.refs_0_), channel_id=1, source_target_pairs={{0,16},{8,24},{16,0},{24,8},{1,17},{9,25},{17,1},{25,9},{2,18},{10... | collective-permute-start | bytes 245768 | tf_op jit(solution)/shard_map/ppermute | solution.py:552
  19.5 0.0 collective-permute-start.5
  19.5 2.9 %collective-permute-done.4.refs_1_ = f32[80,256]{1,0:T(8,128)S(1)} collective-permute-done((f32[80,256]{1,0:T(8,128)S(1)}, f32[80,256]{1,0:T(8,128)S(1)}, u32[]{:S(2)}, u32[]{:S(2)}) %collective-permute-start.4) | collective-permute-done | bytes 81952 | tf_op jit(solution)/shard_map/ppermute | solution.py:552
  22.4 0.0 collective-permute-start.6
  22.4 0.0 copy-done.8
  22.4 0.0 copy-start.2
  22.4 0.9 %shard_map.224.stepped_ref = f32[4,64,128]{2,1,0:T(8,128)S(1)} custom-call(f32[1,4,64,128]{3,2,1,0:T(8,128)S(1)} %copy-done, f32[88,256]{1,0:T(8,128)S(1)} %collective-permute-done.y_ref.columns_ref, f32[8,256]{1,0:T(8,128)S(1)} %get-tuple-element.31.first_ref, f32[88,256]{1,0:T(8,128)S(1)} %collective-permute-done.3.second_ref.other_ref, ...), custom_call_target="tpu_custom_call" | custom-call | tf_op jit(solution)/shard_map/pallas_call | solution.py:122
  23.4 0.0 collective-permute-done.5.refs_2_
  23.4 0.3 %collective-permute-done.6.refs_3_ = f32[80,256]{1,0:T(8,128)S(1)} collective-permute-done((f32[80,256]{1,0:T(8,128)S(1)}, f32[80,256]{1,0:T(8,128)S(1)}, u32[]{:S(2)}, u32[]{:S(2)}) %collective-permute-start.6) | collective-permute-done | bytes 81952 | tf_op jit(solution)/shard_map/ppermute | solution.py:552
  23.7 0.0 copy-done.3
  23.7 0.0 copy-done.4
  23.7 0.0 copy-done.5
  23.7 0.0 copy-done.6
  23.7 0.0 copy-done.7
  23.7 0.0 copy-done.1
  23.7 0.0 copy-done.2
  23.7 4.7 %shard_map.226 = (f32[1,4,64,128]{3,2,1,0:T(8,128)}, f32[1,4,64,64]{3,2,1,0:T(8,128)}) custom-call(f32[4,64,128]{2,1,0:T(8,128)S(1)} %shard_map.224.stepped_ref, f32[3,64,256]{2,1,0:T(8,128)S(1)} %get-tuple-element.33.drive_ref, bf16[3,64,192]{2,1,0:T(8,128)(2,1)S(1)} %get-tuple-element.34.row_ref, bf16[3,256,256]{2,1,0:T(8,128)(2,1)S(1)} %get-tuple-element.35.col_ref, ...), custom_call_target="tpu_custom_call" | custom-call | tf_op jit(solution)/shard_map/pallas_call | solution.py:122
  (1 shorter events, 0.0 us)
Async XLA Ops:
  2.2 6.9 %collective-permute-start.2 = (f32[88,256]{1,0:T(8,128)S(1)}, f32[88,256]{1,0:T(8,128)S(1)}, u32[]{:S(2)}, u32[]{:S(2)}) collective-permute-start(f32[88,256]{1,0:T(8,128)S(1)} %get-tuple-element.21.own_ref), channel_id=1, source_target_pairs={{0,5},{1,4},{2,7},{3,6},{4,1},{5,0},{6,3},{7,2},{8,13},{9,12},{10,... | collective-permute-start | bytes 270344 | tf_op jit(solution)/shard_map/ppermute | solution.py:552
  6.2 4.5 %collective-permute-start = (f32[88,256]{1,0:T(8,128)S(1)}, f32[88,256]{1,0:T(8,128)S(1)}, u32[]{:S(2)}, u32[]{:S(2)}) collective-permute-start(f32[88,256]{1,0:T(8,128)S(1)} %get-tuple-element.21.own_ref), channel_id=1, source_target_pairs={{0,4},{4,0},{1,5},{5,1},{2,6},{6,2},{3,7},{7,3},{8,12},{12,8},{9,1... | collective-permute-start | bytes 270344 | tf_op jit(solution)/shard_map/ppermute | solution.py:552
  6.7 4.5 %collective-permute-start.1 = (f32[88,256]{1,0:T(8,128)S(1)}, f32[88,256]{1,0:T(8,128)S(1)}, u32[]{:S(2)}, u32[]{:S(2)}) collective-permute-start(f32[88,256]{1,0:T(8,128)S(1)} %get-tuple-element.22), channel_id=1, source_target_pairs={{0,1},{1,0},{2,3},{3,2},{4,5},{5,4},{6,7},{7,6},{8,9},{9,8},{10,11... | collective-permute-start | bytes 270344 | tf_op jit(solution)/shard_map/ppermute | solution.py:552
  6.9 4.4 %copy-start = (f32[1,4,64,128]{3,2,1,0:T(8,128)S(1)}, f32[1,4,64,128]{3,2,1,0:T(8,128)}, u32[]{:S(2)}) copy-start(f32[1,4,64,128]{3,2,1,0:T(8,128)} %state_ref.5) | copy-start | bytes 393220
  11.4 11.0 %copy-start.8 = (bf16[32,128]{1,0:T(8,128)(2,1)S(1)}, bf16[32,128]{1,0:T(8,128)(2,1)}, u32[]{:S(2)}) copy-start(bf16[32,128]{1,0:T(8,128)(2,1)} %constant.45.clone.place_ref) | copy-start | bytes 24580
  11.5 6.4 %collective-permute-start.3 = (f32[88,256]{1,0:T(8,128)S(1)}, f32[88,256]{1,0:T(8,128)S(1)}, u32[]{:S(2)}, u32[]{:S(2)}) collective-permute-start(f32[88,256]{1,0:T(8,128)S(1)} %get-tuple-element.32.own_ref), channel_id=1, source_target_pairs={{0,3},{1,2},{2,1},{3,0},{4,7},{5,6},{6,5},{7,4},{8,11},{9,10},{10,... | collective-permute-start | bytes 270344 | tf_op jit(solution)/shard_map/ppermute | solution.py:552
  17.9 5.8 %copy-start.3 = (bf16[128,192]{1,0:T(8,128)(2,1)S(1)}, bf16[128,192]{1,0:T(8,128)(2,1)}, u32[]{:S(2)}) copy-start(bf16[128,192]{1,0:T(8,128)(2,1)} %constant.51.clone.again_ref) | copy-start | bytes 147460
  17.9 5.8 %copy-start.4 = (f32[64,256]{1,0:T(8,128)S(1)}, f32[64,256]{1,0:T(8,128)}, u32[]{:S(2)}) copy-start(f32[64,256]{1,0:T(8,128)} %constant.49.clone.scale_x_ref) | copy-start | bytes 196612
  17.9 5.8 %copy-start.5 = (bf16[192,96]{1,0:T(8,128)(2,1)S(1)}, bf16[192,96]{1,0:T(8,128)(2,1)}, u32[]{:S(2)}) copy-start(bf16[192,96]{1,0:T(8,128)(2,1)} %constant.48.clone.across_ref) | copy-start | bytes 110596
  17.9 5.8 %copy-start.6 = (bf16[32,384]{1,0:T(8,128)(2,1)S(1)}, bf16[32,384]{1,0:T(8,128)(2,1)}, u32[]{:S(2)}) copy-start(bf16[32,384]{1,0:T(8,128)(2,1)} %constant.46.clone.inward_ref) | copy-start | bytes 73732
  17.9 5.9 %copy-start.7 = (f32[8,256]{1,0:T(8,128)S(1)}, f32[8,256]{1,0:T(8,128)}, u32[]{:S(2)}) copy-start(f32[8,256]{1,0:T(8,128)} %constant.50.clone.scale_y_ref) | copy-start | bytes 24580
  17.9 5.8 %copy-start.1 = (bf16[2,256,256]{2,1,0:T(8,128)(2,1)S(1)}, bf16[2,256,256]{2,1,0:T(8,128)(2,1)}, u32[]{:S(2)}) copy-start(bf16[2,256,256]{2,1,0:T(8,128)(2,1)} %constant.58.sideways_ref) | copy-start | bytes 786436
  17.9 4.5 %collective-permute-start.4 = (f32[80,256]{1,0:T(8,128)S(1)}, f32[80,256]{1,0:T(8,128)S(1)}, u32[]{:S(2)}, u32[]{:S(2)}) collective-permute-start(f32[80,256]{1,0:T(8,128)S(1)} %shard_map.225.refs_0_), channel_id=1, source_target_pairs={{0,16},{8,24},{16,0},{24,8},{1,17},{9,25},{17,1},{25,9},{2,18},{10... | collective-permute-start | bytes 245768 | tf_op jit(solution)/shard_map/ppermute | solution.py:552
  19.5 3.9 %collective-permute-start.5 = (f32[80,256]{1,0:T(8,128)S(1)}, f32[80,256]{1,0:T(8,128)S(1)}, u32[]{:S(2)}, u32[]{:S(2)}) collective-permute-start(f32[80,256]{1,0:T(8,128)S(1)} %shard_map.225.refs_0_), channel_id=1, source_target_pairs={{0,8},{8,0},{16,24},{24,16},{1,9},{9,1},{17,25},{25,17},{2,10},{10... | collective-permute-start | bytes 245768 | tf_op jit(solution)/shard_map/ppermute | solution.py:552
  22.4 1.3 %collective-permute-start.6 = (f32[80,256]{1,0:T(8,128)S(1)}, f32[80,256]{1,0:T(8,128)S(1)}, u32[]{:S(2)}, u32[]{:S(2)}) collective-permute-start(f32[80,256]{1,0:T(8,128)S(1)} %collective-permute-done.4.refs_1_), channel_id=1, source_target_pairs={{0,8},{8,0},{16,24},{24,16},{1,9},{9,1},{17,25},{25,17},{2,10},{10... | collective-permute-start | bytes 245768 | tf_op jit(solution)/shard_map/ppermute | solution.py:552
  22.4 1.3 %copy-start.2 = (bf16[256,384]{1,0:T(8,128)(2,1)S(1)}, bf16[256,384]{1,0:T(8,128)(2,1)}, u32[]{:S(2)}) copy-start(bf16[256,384]{1,0:T(8,128)(2,1)} %constant.47.clone.corner_ref) | copy-start | bytes 589828

commit v5 on v4

--- a/solution.py
+++ b/solution.py
@@ -495,37 +495,39 @@
                 result.append(turned[0] + over[n * modes : (n + 1) * modes])
             return result
 
-        def carried(change, count):
-            left = dot(again_ref[: count * modes], stacked(change))
-            left = [left[i * modes : (i + 1) * modes] for i in range(count)]
-            if count == 1:
-                return [left[0] + unpairs(times_right(pairs(change), sideways_ref[0]))]
-            both = jnp.concatenate([pairs(change), pairs(left[0])], 0)
-            once = times_right(both, sideways_ref[0])
-            twice = times_right(pairs(change), sideways_ref[1])
-            rows = half * modes
-            return [left[0] + unpairs(once[:rows]), left[1] + unpairs(2.0 * once[rows:] + twice)]
-
         owns = [own_modes(slot) for slot in slots]
-        coeffs = None
-        for slot in range(root, -1, -1):
-            gain = slots[slot][low - 1 : low]
-            own = owns[slot]
-            new, changes, later = [], [], []
-            for w in range(windows):
+        gains = [slot[low - 1 : low] for slot in slots]
+        coeffs, changes, later = {}, {}, {}
+        for front in range(root + windows):
+            cells = [(root - front + w, w) for w in range(windows) if 0 <= root - front + w <= root]
+            inner, lefts, rights = {}, {}, {}
+            for slot, w in cells:
+                if slot < root:
+                    inner[slot, w] = times_right(pairs(coeffs[slot + 1, w]), col_ref[slot])
+                if w > 0:
+                    change = changes[slot, w - 1]
+                    count = windows - w
+                    left = dot(again_ref[: count * modes], stacked(change))
+                    lefts[slot] = left = [left[i * modes : (i + 1) * modes] for i in range(count)]
+                    rights[slot] = [unpairs(times_right(pairs(change), sideways_ref[i])) for i in range(count)]
+                    later[slot, w - 1, 1] = left[0] + rights[slot][0]
+            for slot, w in cells:
                 target = drive_ref[w]
                 if slot < root:
-                    inner = unpairs(times_right(pairs(coeffs[w]), col_ref[slot]))
-                    target = jnp.where(nest <= slot, target, dot(row_ref[slot], stacked(inner)))
-                before = own[w]
+                    found = dot(row_ref[slot], stacked(unpairs(inner[slot, w])))
+                    target = jnp.where(nest <= slot, target, found)
+                before = owns[slot][w]
                 for v in range(w):
-                    before = before + later[v][w - v - 1]
-                change = gain * (target - before)
-                if w < windows - 1:
-                    later.append(carried(change, windows - 1 - w))
-                changes.append(change)
-                new.append(before + change)
-            coeffs = new
+                    before = before + later[slot, v, w - v]
+                changes[slot, w] = gains[slot] * (target - before)
+                coeffs[slot, w] = before + changes[slot, w]
+            for slot, w in cells:
+                if w > 0 and windows - w > 1:
+                    left, right = lefts[slot], rights[slot]
+                    mixed = unpairs(times_right(pairs(left[0]), sideways_ref[0]))
+                    later[slot, w - 1, 2] = left[1] + (2.0 * mixed + right[1])
+        changes = [changes[0, w] for w in range(windows)]
+        coeffs = [coeffs[0, w] for w in range(windows)]
         for level in range(levels):
             modes_ref[0, level] = coeffs[-1][:, level * modes : (level + 1) * modes]
         spread = sum(dot(spread_x_ref[w], stacked(changes[w])) for w in range(windows))
@@ -582,10 +584,12 @@
     if crossed:
         core = swap(last, "nest", lambda i: i ^ 1)
         chip = swap(last, "nest", lambda i: i ^ 2)
+        stepped = step_patch(plan, initial_state, columns, halo, across)
+        chip, stepped = lax.optimization_barrier((chip, stepped))
         gathered = [last, chip, core, swap(chip, "nest", lambda i: i ^ 1)]
     else:
         gathered = [last] + [swap(last, "nest", lambda i, s=s: i + s) for s in range(1, plan.nest)]
-    stepped = step_patch(plan, initial_state, columns, halo, across)
+        stepped = step_patch(plan, initial_state, columns, halo, across)
     return nudge(plan, stepped, gathered, crossed, prepared)
 
 

time: 28.6 us -> 27.4 us (0.958)
  Pallas kernels: 9.24 us -> 8.02 us
    pallas_call x6, Pallas kernels: 9.24 us -> 8.02 us  [call(): pl.pallas_call(kernel, in_specs=specs, out_specs=jax.tree.map(lambda _: p...]
where the time goes in v5:
time: 27.4 us; the launch traced here: 27.3 us
  starting transfers between devices  9.58 us (35%)
  waiting for transfers between devices  8.88 us (32%)
  Pallas kernels  8.02 us (29%)
  between operations  0.73 us (3%)
    ppermute x7, starting transfers between devices, swap(): lax.ppermute(value, axis, [(i, partner(i)) for i in range(size) if 0 <= p...  9.58 us
    ppermute x7, waiting for transfers between devices, swap(): lax.ppermute(value, axis, [(i, partner(i)) for i in range(size) if 0 <= p...  8.88 us
    pallas_call x6, Pallas kernels, call(): pl.pallas_call(kernel, in_specs=specs, out_specs=jax.tree.map(lambda _: p...  8.02 us
  transfers between devices with their start and end apart: 7, of which 6 were waited for; matrix products, arithmetic and copies ran while one was open for 0% of the time, Pallas kernels for 10%

profile of v5, /device:TPU:0, one launch (start us, length us, event | category | flops | bytes accessed | tf_op | source)
XLA Modules:
  0.0 27.3 jit_solution(9875682656404714051)
XLA Ops:
  0.6 1.6 %shard_map.221 = (f32[88,256]{1,0:T(8,128)S(1)}, f32[88,256]{1,0:T(8,128)S(1)}) custom-call(f32[1,4,64,128]{3,2,1,0:T(8,128)} %state_ref.5, bf16[4,80,192]{2,1,0:T(8,128)(2,1)} %constant.36.clone.left_ref, bf16[2,256,256]{2,1,0:T(8,128)(2,1)} %constant.37.clone.right_ref, bf16[2,256,128]{2,1,0:T(8,128)(2,1)} %constant.38.clone.corner_ref, ...), custom_call_target="tpu_custom_call" | custom-call | tf_op jit(solution)/shard_map/pallas_call | solution.py:122
  2.2 4.0 %collective-permute-start.2 = (f32[88,256]{1,0:T(8,128)S(1)}, f32[88,256]{1,0:T(8,128)S(1)}, u32[]{:S(2)}, u32[]{:S(2)}) collective-permute-start(f32[88,256]{1,0:T(8,128)S(1)} %get-tuple-element.23.own_ref), channel_id=1, source_target_pairs={{0,5},{1,4},{2,7},{3,6},{4,1},{5,0},{6,3},{7,2},{8,13},{9,12},{10,... | collective-permute-start | bytes 270344 | tf_op jit(solution)/shard_map/ppermute | solution.py:554
  6.2 0.5 %collective-permute-start = (f32[88,256]{1,0:T(8,128)S(1)}, f32[88,256]{1,0:T(8,128)S(1)}, u32[]{:S(2)}, u32[]{:S(2)}) collective-permute-start(f32[88,256]{1,0:T(8,128)S(1)} %get-tuple-element.23.own_ref), channel_id=1, source_target_pairs={{0,4},{4,0},{1,5},{5,1},{2,6},{6,2},{3,7},{7,3},{8,12},{12,8},{9,1... | collective-permute-start | bytes 270344 | tf_op jit(solution)/shard_map/ppermute | solution.py:554
  6.7 0.1 collective-permute-start.1
  6.9 0.0 copy-start
  6.9 1.8 %shard_map.222 = (f32[3,64,256]{2,1,0:T(8,128)S(1)}, bf16[3,64,192]{2,1,0:T(8,128)(2,1)S(1)}, bf16[3,256,256]{2,1,0:T(8,128)(2,1)S(1)}, bf16[3,192,192]{2,1,0:T(8,128)(2,1)S(1)}, bf16[3,256,256]{2,1,0:T(8,128)(2,1)S(1)}) custom-call(f32[3,4,64,64]{3,2,1,0:T(8,128)} %drive_ref, f32[2,64,128]{2,1,0:T(8,128)} %constant.41.clone.maps_x_ref, ...), custom_call_target="tpu_custom_call" | custom-call | tf_op jit(solution)/shard_map/pallas_call | solution.py:122
  8.7 0.4 %collective-permute-done.2.both_ref = f32[88,256]{1,0:T(8,128)S(1)} collective-permute-done((f32[88,256]{1,0:T(8,128)S(1)}, f32[88,256]{1,0:T(8,128)S(1)}, u32[]{:S(2)}, u32[]{:S(2)}) %collective-permute-start.2) | collective-permute-done | bytes 90144 | tf_op jit(solution)/shard_map/ppermute | solution.py:554
  9.1 1.7 %collective-permute-done.y_ref.columns_ref = f32[88,256]{1,0:T(8,128)S(1)} collective-permute-done((f32[88,256]{1,0:T(8,128)S(1)}, f32[88,256]{1,0:T(8,128)S(1)}, u32[]{:S(2)}, u32[]{:S(2)}) %collective-permute-start) | collective-permute-done | bytes 90144 | tf_op jit(solution)/shard_map/ppermute | solution.py:554
  10.8 0.5 %collective-permute-done.1.x_ref = f32[88,256]{1,0:T(8,128)S(1)} collective-permute-done((f32[88,256]{1,0:T(8,128)S(1)}, f32[88,256]{1,0:T(8,128)S(1)}, u32[]{:S(2)}, u32[]{:S(2)}) %collective-permute-start.1) | collective-permute-done | bytes 90144 | tf_op jit(solution)/shard_map/ppermute | solution.py:554
  11.3 0.0 copy-done
  11.3 0.2 shard_map.223
  11.4 0.0 copy-start.8
  11.5 3.3 %collective-permute-start.3 = (f32[88,256]{1,0:T(8,128)S(1)}, f32[88,256]{1,0:T(8,128)S(1)}, u32[]{:S(2)}, u32[]{:S(2)}) collective-permute-start(f32[88,256]{1,0:T(8,128)S(1)} %get-tuple-element.33.own_ref), channel_id=1, source_target_pairs={{0,3},{1,2},{2,1},{3,0},{4,7},{5,6},{6,5},{7,4},{8,11},{9,10},{10,... | collective-permute-start | bytes 270344 | tf_op jit(solution)/shard_map/ppermute | solution.py:554
  14.8 3.1 %collective-permute-done.3.other_ref.second_ref = f32[88,256]{1,0:T(8,128)S(1)} collective-permute-done((f32[88,256]{1,0:T(8,128)S(1)}, f32[88,256]{1,0:T(8,128)S(1)}, u32[]{:S(2)}, u32[]{:S(2)}) %collective-permute-start.3) | collective-permute-done | bytes 90144 | tf_op jit(solution)/shard_map/ppermute | solution.py:554
  17.9 0.0 copy-start.3
  17.9 0.0 copy-start.4
  17.9 0.0 copy-start.5
  17.9 0.0 copy-start.6
  17.9 0.0 copy-start.7
  17.9 0.0 copy-start.1
  17.9 1.6 %collective-permute-start.4 = (f32[80,256]{1,0:T(8,128)S(1)}, f32[80,256]{1,0:T(8,128)S(1)}, u32[]{:S(2)}, u32[]{:S(2)}) collective-permute-start(f32[80,256]{1,0:T(8,128)S(1)} %shard_map.224.refs_0_), channel_id=1, source_target_pairs={{0,16},{8,24},{16,0},{24,8},{1,17},{9,25},{17,1},{25,9},{2,18},{10... | collective-permute-start | bytes 245768 | tf_op jit(solution)/shard_map/ppermute | solution.py:554
  19.5 0.0 collective-permute-start.5
  19.5 0.0 copy-done.8
  19.5 0.0 copy-start.2
  19.5 0.9 %shard_map.225.stepped_ref = f32[4,64,128]{2,1,0:T(8,128)S(1)} custom-call(f32[1,4,64,128]{3,2,1,0:T(8,128)S(1)} %copy-done, f32[88,256]{1,0:T(8,128)S(1)} %collective-permute-done.y_ref.columns_ref, f32[8,256]{1,0:T(8,128)S(1)} %get-tuple-element.34.first_ref, f32[88,256]{1,0:T(8,128)S(1)} %collective-permute-done.3.other_ref.second_ref, ...), custom_call_target="tpu_custom_call" | custom-call | tf_op jit(solution)/shard_map/pallas_call | solution.py:122
  20.4 2.0 %collective-permute-done.4.refs_1_ = f32[80,256]{1,0:T(8,128)S(1)} collective-permute-done((f32[80,256]{1,0:T(8,128)S(1)}, f32[80,256]{1,0:T(8,128)S(1)}, u32[]{:S(2)}, u32[]{:S(2)}) %collective-permute-start.4) | collective-permute-done | bytes 81952 | tf_op jit(solution)/shard_map/ppermute | solution.py:554
  22.4 0.0 collective-permute-start.6
  22.4 0.0 collective-permute-done.5.refs_2_
  22.4 1.3 %collective-permute-done.6.refs_3_ = f32[80,256]{1,0:T(8,128)S(1)} collective-permute-done((f32[80,256]{1,0:T(8,128)S(1)}, f32[80,256]{1,0:T(8,128)S(1)}, u32[]{:S(2)}, u32[]{:S(2)}) %collective-permute-start.6) | collective-permute-done | bytes 81952 | tf_op jit(solution)/shard_map/ppermute | solution.py:554
  23.7 0.0 copy-done.3
  23.7 0.0 copy-done.4
  23.7 0.0 copy-done.5
  23.7 0.0 copy-done.6
  23.7 0.0 copy-done.7
  23.7 0.0 copy-done.1
  23.7 0.0 copy-done.2
  23.7 3.5 %shard_map.226 = (f32[1,4,64,128]{3,2,1,0:T(8,128)}, f32[1,4,64,64]{3,2,1,0:T(8,128)}) custom-call(f32[4,64,128]{2,1,0:T(8,128)S(1)} %shard_map.225.stepped_ref, f32[3,64,256]{2,1,0:T(8,128)S(1)} %get-tuple-element.36.drive_ref, bf16[3,64,192]{2,1,0:T(8,128)(2,1)S(1)} %get-tuple-element.37.row_ref, bf16[3,256,256]{2,1,0:T(8,128)(2,1)S(1)} %get-tuple-element.38.col_ref, ...), custom_call_target="tpu_custom_call" | custom-call | tf_op jit(solution)/shard_map/pallas_call | solution.py:122
  (1 shorter events, 0.0 us)
Async XLA Ops:
  2.2 6.9 %collective-permute-start.2 = (f32[88,256]{1,0:T(8,128)S(1)}, f32[88,256]{1,0:T(8,128)S(1)}, u32[]{:S(2)}, u32[]{:S(2)}) collective-permute-start(f32[88,256]{1,0:T(8,128)S(1)} %get-tuple-element.23.own_ref), channel_id=1, source_target_pairs={{0,5},{1,4},{2,7},{3,6},{4,1},{5,0},{6,3},{7,2},{8,13},{9,12},{10,... | collective-permute-start | bytes 270344 | tf_op jit(solution)/shard_map/ppermute | solution.py:554
  6.2 4.5 %collective-permute-start = (f32[88,256]{1,0:T(8,128)S(1)}, f32[88,256]{1,0:T(8,128)S(1)}, u32[]{:S(2)}, u32[]{:S(2)}) collective-permute-start(f32[88,256]{1,0:T(8,128)S(1)} %get-tuple-element.23.own_ref), channel_id=1, source_target_pairs={{0,4},{4,0},{1,5},{5,1},{2,6},{6,2},{3,7},{7,3},{8,12},{12,8},{9,1... | collective-permute-start | bytes 270344 | tf_op jit(solution)/shard_map/ppermute | solution.py:554
  6.7 4.5 %collective-permute-start.1 = (f32[88,256]{1,0:T(8,128)S(1)}, f32[88,256]{1,0:T(8,128)S(1)}, u32[]{:S(2)}, u32[]{:S(2)}) collective-permute-start(f32[88,256]{1,0:T(8,128)S(1)} %get-tuple-element.24), channel_id=1, source_target_pairs={{0,1},{1,0},{2,3},{3,2},{4,5},{5,4},{6,7},{7,6},{8,9},{9,8},{10,11... | collective-permute-start | bytes 270344 | tf_op jit(solution)/shard_map/ppermute | solution.py:554
  6.9 4.4 %copy-start = (f32[1,4,64,128]{3,2,1,0:T(8,128)S(1)}, f32[1,4,64,128]{3,2,1,0:T(8,128)}, u32[]{:S(2)}) copy-start(f32[1,4,64,128]{3,2,1,0:T(8,128)} %state_ref.5) | copy-start | bytes 393220
  11.4 8.0 %copy-start.8 = (bf16[32,128]{1,0:T(8,128)(2,1)S(1)}, bf16[32,128]{1,0:T(8,128)(2,1)}, u32[]{:S(2)}) copy-start(bf16[32,128]{1,0:T(8,128)(2,1)} %constant.45.clone.place_ref) | copy-start | bytes 24580
  11.5 6.4 %collective-permute-start.3 = (f32[88,256]{1,0:T(8,128)S(1)}, f32[88,256]{1,0:T(8,128)S(1)}, u32[]{:S(2)}, u32[]{:S(2)}) collective-permute-start(f32[88,256]{1,0:T(8,128)S(1)} %get-tuple-element.33.own_ref), channel_id=1, source_target_pairs={{0,3},{1,2},{2,1},{3,0},{4,7},{5,6},{6,5},{7,4},{8,11},{9,10},{10,... | collective-permute-start | bytes 270344 | tf_op jit(solution)/shard_map/ppermute | solution.py:554
  17.9 5.8 %copy-start.3 = (bf16[128,192]{1,0:T(8,128)(2,1)S(1)}, bf16[128,192]{1,0:T(8,128)(2,1)}, u32[]{:S(2)}) copy-start(bf16[128,192]{1,0:T(8,128)(2,1)} %constant.51.clone.again_ref) | copy-start | bytes 147460
  17.9 5.8 %copy-start.4 = (f32[64,256]{1,0:T(8,128)S(1)}, f32[64,256]{1,0:T(8,128)}, u32[]{:S(2)}) copy-start(f32[64,256]{1,0:T(8,128)} %constant.49.clone.scale_x_ref) | copy-start | bytes 196612
  17.9 5.8 %copy-start.5 = (bf16[192,96]{1,0:T(8,128)(2,1)S(1)}, bf16[192,96]{1,0:T(8,128)(2,1)}, u32[]{:S(2)}) copy-start(bf16[192,96]{1,0:T(8,128)(2,1)} %constant.48.clone.across_ref) | copy-start | bytes 110596
  17.9 5.8 %copy-start.6 = (bf16[32,384]{1,0:T(8,128)(2,1)S(1)}, bf16[32,384]{1,0:T(8,128)(2,1)}, u32[]{:S(2)}) copy-start(bf16[32,384]{1,0:T(8,128)(2,1)} %constant.46.clone.inward_ref) | copy-start | bytes 73732
  17.9 5.9 %copy-start.7 = (f32[8,256]{1,0:T(8,128)S(1)}, f32[8,256]{1,0:T(8,128)}, u32[]{:S(2)}) copy-start(f32[8,256]{1,0:T(8,128)} %constant.50.clone.scale_y_ref) | copy-start | bytes 24580
  17.9 5.8 %copy-start.1 = (bf16[2,256,256]{2,1,0:T(8,128)(2,1)S(1)}, bf16[2,256,256]{2,1,0:T(8,128)(2,1)}, u32[]{:S(2)}) copy-start(bf16[2,256,256]{2,1,0:T(8,128)(2,1)} %constant.58.sideways_ref) | copy-start | bytes 786436
  17.9 4.5 %collective-permute-start.4 = (f32[80,256]{1,0:T(8,128)S(1)}, f32[80,256]{1,0:T(8,128)S(1)}, u32[]{:S(2)}, u32[]{:S(2)}) collective-permute-start(f32[80,256]{1,0:T(8,128)S(1)} %shard_map.224.refs_0_), channel_id=1, source_target_pairs={{0,16},{8,24},{16,0},{24,8},{1,17},{9,25},{17,1},{25,9},{2,18},{10... | collective-permute-start | bytes 245768 | tf_op jit(solution)/shard_map/ppermute | solution.py:554
  19.5 3.0 %collective-permute-start.5 = (f32[80,256]{1,0:T(8,128)S(1)}, f32[80,256]{1,0:T(8,128)S(1)}, u32[]{:S(2)}, u32[]{:S(2)}) collective-permute-start(f32[80,256]{1,0:T(8,128)S(1)} %shard_map.224.refs_0_), channel_id=1, source_target_pairs={{0,8},{8,0},{16,24},{24,16},{1,9},{9,1},{17,25},{25,17},{2,10},{10... | collective-permute-start | bytes 245768 | tf_op jit(solution)/shard_map/ppermute | solution.py:554
  19.5 4.3 %copy-start.2 = (bf16[256,384]{1,0:T(8,128)(2,1)S(1)}, bf16[256,384]{1,0:T(8,128)(2,1)}, u32[]{:S(2)}) copy-start(bf16[256,384]{1,0:T(8,128)(2,1)} %constant.47.clone.corner_ref) | copy-start | bytes 589828
  22.4 1.3 %collective-permute-start.6 = (f32[80,256]{1,0:T(8,128)S(1)}, f32[80,256]{1,0:T(8,128)S(1)}, u32[]{:S(2)}, u32[]{:S(2)}) collective-permute-start(f32[80,256]{1,0:T(8,128)S(1)} %collective-permute-done.4.refs_1_), channel_id=1, source_target_pairs={{0,8},{8,0},{16,24},{24,16},{1,9},{9,1},{17,25},{25,17},{2,10},{10... | collective-permute-start | bytes 245768 | tf_op jit(solution)/shard_map/ppermute | solution.py:554

commit v6 on v5

--- a/solution.py
+++ b/solution.py
@@ -72,10 +72,7 @@
 
 
 def right_table(value):
-    high, low = parts_of(value)
-    upper = np.concatenate([high, low], -1)
-    lower = np.concatenate([high, np.zeros_like(low)], -1)
-    return jnp.asarray(np.concatenate([upper, lower], -2))
+    return jnp.asarray(np.concatenate(parts_of(value), -1))
 
 
 def halves(value):
@@ -99,8 +96,9 @@
 
 
 def times_right(value, table):
-    out = dot(jnp.concatenate(halves(value), 1), table)
-    width = out.shape[1] // 2
+    width = table.shape[1] // 2
+    lower = jnp.concatenate([table[:, :width], jnp.zeros_like(table[:, width:])], 1)
+    out = dot(jnp.concatenate(halves(value), 1), jnp.concatenate([table, lower], 0))
     return out[:, :width] + out[:, width:]
 
 
@@ -390,17 +388,13 @@
             row_out[slot] = as_left(maps_x_ref[0] * cos_x[at] - maps_x_ref[1] * sin_x[at])
             col_map = maps_y_ref[0] * cos_y[:, at] - maps_y_ref[1] * sin_y[:, at]
             high, small = halves(col_map)
-            upper = jnp.concatenate([high, small], 1)
-            lower = jnp.concatenate([high, jnp.zeros_like(high)], 1)
-            col_out[slot] = jnp.concatenate([upper, lower], 0)
+            col_out[slot] = jnp.concatenate([high, small], 1)
         for w in range(windows):
             p = windows - 1 - w
-            for j in range(windows):
-                if j <= p:
-                    combined = sum(multinomial(p, i, j) * rows_x_ref[px, i] for i in range(p - j + 1))
-                    spread_x_out[w, j * nx : (j + 1) * nx] = as_left(combined)
-                else:
-                    spread_x_out[w, j * nx : (j + 1) * nx] = jnp.zeros((nx, 3 * modes), jnp.bfloat16)
+            for j in range(p + 1):
+                combined = sum(multinomial(p, i, j) * rows_x_ref[px, i] for i in range(p - j + 1))
+                at = (sum(range(p + 1)) + j) * nx
+                spread_x_out[at : at + nx] = as_left(combined)
         for j in range(windows):
             table = rows_y_ref[py, j]
             blank = jnp.zeros_like(table)
@@ -413,19 +407,15 @@
     shapes = (
         shape_of(windows, modes, lanes),
         shape_of(steps, modes, 3 * modes, kind=jnp.bfloat16),
-        shape_of(steps, 4 * modes, 4 * modes, kind=jnp.bfloat16),
-        shape_of(windows, windows * nx, 3 * modes, kind=jnp.bfloat16),
+        shape_of(steps, 2 * modes, 4 * modes, kind=jnp.bfloat16),
+        shape_of(sum(range(windows + 1)) * nx, 3 * modes, kind=jnp.bfloat16),
         shape_of(windows, 4 * modes, 2 * ny, kind=jnp.bfloat16),
     )
     return call(kernel, shapes, drive, maps_x, maps_y, f32(rows_x), f32(rows_y), nest_offsets.T, first=True)
 
 
-def nudge(plan, stepped, gathered, crossed, prepared):
-    modes, low, lanes, levels = plan.modes, plan.low, plan.lanes, plan.levels
-    windows, half, nx, ny = plan.windows, plan.half, plan.nx, plan.ny
-    x, y, sums = plan.x, plan.y, plan.sums
-    pairs, unpairs = plan.pairs, plan.unpairs
-
+def own_tables(plan):
+    x, y, modes, windows = plan.x, plan.y, plan.modes, plan.windows
     inward = np.concatenate([np.tile(y["spill"][j].T, (1, 2)) for j in range(1, windows + 1)], 1)
     high, small = parts_of(inward)
     inward = jnp.asarray(np.concatenate([high, small, high, np.zeros_like(high)], 0))
@@ -442,8 +432,67 @@
             )
     high, small = parts_of(across)
     across = jnp.asarray(np.pad(np.concatenate([high, small, high], 1), ((0, 0), (0, 3 * EDGE))))
-    scale_x = f32(np.broadcast_to(1.0 + x["factor"][:, None], (modes, lanes)))
-    scale_y = f32(np.broadcast_to(np.tile(y["factor"], levels), (EDGE, lanes)))
+    scale_x = f32(np.broadcast_to(1.0 + x["factor"][:, None], (modes, plan.lanes)))
+    scale_y = f32(np.broadcast_to(np.tile(y["factor"], plan.levels), (EDGE, plan.lanes)))
+    return inward, corner, across, scale_x, scale_y
+
+
+def own_modes_of(plan, inward_ref, corner_ref, across_ref, scale_x_ref, scale_y_ref):
+    modes, low, lanes, sums = plan.modes, plan.low, plan.lanes, plan.sums
+    windows, half, ny = plan.windows, plan.half, plan.ny
+    scale_x, scale_y = scale_x_ref[...], scale_y_ref[:1]
+    row = lax.broadcasted_iota(jnp.int32, (EDGE, lanes), 0)
+    lane = lax.broadcasted_iota(jnp.int32, (EDGE, lanes), 1)
+    mine = lane % EDGE == row
+    left_lane = lax.broadcasted_iota(jnp.int32, (modes, ny), 1) < modes
+
+    def own_modes(message):
+        rows, ends = message[:modes], message[modes:low]
+        sides = dot(short_stacked(message[low:sums], 4 * EDGE), inward_ref[...], ((0,), (0,)))
+        cells = jnp.where(mine, jnp.broadcast_to(ends[EDGE - 2 : EDGE - 1], (EDGE, lanes)), 0.0)
+        cells = jnp.concatenate([cells[:, i * ny : (i + 1) * ny] for i in range(half)], 0)
+        cells = by_parts(cells, corner_ref[:ny], corner_ref[ny:])
+        turned, ends = [rows], [ends]
+        for j in range(windows):
+            at = slice(j * ny, (j + 1) * ny)
+            side = [
+                jnp.where(
+                    left_lane,
+                    sides[2 * i * modes : (2 * i + 1) * modes, at],
+                    sides[(2 * i + 1) * modes : (2 * i + 2) * modes, at],
+                )
+                for i in range(half)
+            ]
+            cell = [cells[i * EDGE : (i + 1) * EDGE, at] for i in range(half)]
+            power = scale_y if j == 0 else power * scale_y
+            turned.append(rows * power + jnp.concatenate(side, 1))
+            ends.append(ends[0] * power + jnp.concatenate(cell, 1))
+        over = dot(across_ref[...], short_stacked(jnp.concatenate(ends[:windows], 0), 12 * EDGE))
+        result = []
+        for n in range(windows):
+            turned = [a * scale_x + b for a, b in zip(turned[:-1], turned[1:])]
+            result.append(turned[0] + over[n * modes : (n + 1) * modes])
+        return result
+
+    return own_modes
+
+
+def own_early(plan, tables, messages):
+    def kernel(*refs):
+        count = len(messages)
+        own_modes = own_modes_of(plan, *refs[count : count + len(tables)])
+        for i in range(count):
+            for w, value in enumerate(own_modes(refs[i][...])):
+                refs[count + len(tables)][i, w] = value
+
+    return call(kernel, shape_of(len(messages), plan.windows, plan.modes, plan.lanes), *messages, *tables)
+
+
+def nudge(plan, stepped, gathered, early, tables, crossed, prepared):
+    modes, low, lanes, levels = plan.modes, plan.low, plan.lanes, plan.levels
+    windows, half, nx, ny = plan.windows, plan.half, plan.nx, plan.ny
+    x, y = plan.x, plan.y
+    pairs, unpairs = plan.pairs, plan.unpairs
     again = []
     for p in range(1, windows):
         again.append(sum(multinomial(p, i, 0) * x["within"][i] for i in range(p + 1)))
@@ -452,51 +501,21 @@
     drive, row_maps, col_maps, spread_x, spread_y = prepared
 
     def kernel(
-        stepped_ref, drive_ref, row_ref, col_ref, spread_x_ref, spread_y_ref, inward_ref, corner_ref,
-        across_ref, scale_x_ref, scale_y_ref, again_ref, sideways_ref, *refs,
+        stepped_ref, drive_ref, row_ref, col_ref, spread_x_ref, spread_y_ref, again_ref, sideways_ref,
+        early_ref, *refs,
     ):
         refs, (state_ref, modes_ref) = refs[:-2], refs[-2:]
         root = plan.nest - 1
         nest = lax.axis_index("nest")
-        slots = [ref[...] for ref in refs]
+        refs, table_refs = refs[: plan.nest], refs[plan.nest :]
+        gains = [ref[low - 1 : low] for ref in refs]
+        owns = [[early_ref[i, w] for w in range(windows)] for i in range(root)]
+        owns.append(own_modes_of(plan, *table_refs)(refs[root][...]))
         if crossed:
-            slots = [slots[0], jnp.where(nest % 2 == 1, slots[2], slots[3]), slots[1], slots[3]]
-        scale_x, scale_y = scale_x_ref[...], scale_y_ref[:1]
-        row = lax.broadcasted_iota(jnp.int32, (EDGE, lanes), 0)
-        lane = lax.broadcasted_iota(jnp.int32, (EDGE, lanes), 1)
-        mine = lane % EDGE == row
-        left_lane = lax.broadcasted_iota(jnp.int32, (modes, ny), 1) < modes
-
-        def own_modes(message):
-            rows, ends = message[:modes], message[modes:low]
-            sides = dot(short_stacked(message[low:sums], 4 * EDGE), inward_ref[...], ((0,), (0,)))
-            cells = jnp.where(mine, jnp.broadcast_to(ends[EDGE - 2 : EDGE - 1], (EDGE, lanes)), 0.0)
-            cells = jnp.concatenate([cells[:, i * ny : (i + 1) * ny] for i in range(half)], 0)
-            cells = by_parts(cells, corner_ref[:ny], corner_ref[ny:])
-            turned, ends = [rows], [ends]
-            for j in range(windows):
-                at = slice(j * ny, (j + 1) * ny)
-                side = [
-                    jnp.where(
-                        left_lane,
-                        sides[2 * i * modes : (2 * i + 1) * modes, at],
-                        sides[(2 * i + 1) * modes : (2 * i + 2) * modes, at],
-                    )
-                    for i in range(half)
-                ]
-                cell = [cells[i * EDGE : (i + 1) * EDGE, at] for i in range(half)]
-                power = scale_y if j == 0 else power * scale_y
-                turned.append(rows * power + jnp.concatenate(side, 1))
-                ends.append(ends[0] * power + jnp.concatenate(cell, 1))
-            over = dot(across_ref[...], short_stacked(jnp.concatenate(ends[:windows], 0), 12 * EDGE))
-            result = []
-            for n in range(windows):
-                turned = [a * scale_x + b for a, b in zip(turned[:-1], turned[1:])]
-                result.append(turned[0] + over[n * modes : (n + 1) * modes])
-            return result
-
-        owns = [own_modes(slot) for slot in slots]
-        gains = [slot[low - 1 : low] for slot in slots]
+            odd = nest % 2 == 1
+            gains = [gains[0], jnp.where(odd, gains[2], gains[3]), gains[1], gains[3]]
+            mixed = [jnp.where(odd, a, b) for a, b in zip(owns[2], owns[3])]
+            owns = [owns[0], mixed, owns[1], owns[3]]
         coeffs, changes, later = {}, {}, {}
         for front in range(root + windows):
             cells = [(root - front + w, w) for w in range(windows) if 0 <= root - front + w <= root]
@@ -530,11 +549,17 @@
         coeffs = [coeffs[0, w] for w in range(windows)]
         for level in range(levels):
             modes_ref[0, level] = coeffs[-1][:, level * modes : (level + 1) * modes]
-        spread = sum(dot(spread_x_ref[w], stacked(changes[w])) for w in range(windows))
+        spread = [0.0] * windows
+        for w in range(windows):
+            p = windows - 1 - w
+            at = sum(range(p + 1)) * nx
+            found = dot(spread_x_ref[at : at + (p + 1) * nx], stacked(changes[w]))
+            for j in range(p + 1):
+                spread[j] = spread[j] + found[j * nx : (j + 1) * nx]
         field = 0.0
         for j in range(windows):
             table = spread_y_ref[j]
-            part = by_parts(pairs(spread[j * nx : (j + 1) * nx]), table[: 2 * modes], table[2 * modes :])
+            part = by_parts(pairs(spread[j]), table[: 2 * modes], table[2 * modes :])
             field = field + part
         for level in range(levels):
             at_row, at = level // 2 * nx, level % 2 * ny
@@ -543,8 +568,7 @@
     return call(
         kernel,
         (shape_of(1, levels, nx, ny), shape_of(1, levels, modes, modes)),
-        stepped, drive, row_maps, col_maps, spread_x, spread_y, inward, corner, across, scale_x, scale_y,
-        again, sideways, *gathered,
+        stepped, drive, row_maps, col_maps, spread_x, spread_y, again, sideways, early, *gathered, *tables,
         final=True,
     )
 
@@ -590,7 +614,9 @@
     else:
         gathered = [last] + [swap(last, "nest", lambda i, s=s: i + s) for s in range(1, plan.nest)]
         stepped = step_patch(plan, initial_state, columns, halo, across)
-    return nudge(plan, stepped, gathered, crossed, prepared)
+    tables = own_tables(plan)
+    early = own_early(plan, tables, gathered[:-1])
+    return nudge(plan, stepped, gathered, early, tables, crossed, prepared)
 
 
 def solution(mesh):

time: 27.4 us -> 27 us (0.985)
  waiting for transfers between devices: 8.88 us -> 7.45 us
  local copies, waits for them, and re-layouts: 0.04 us -> 0.72 us
  Pallas kernels: 8.02 us -> 8.35 us
    ppermute x7, waiting for transfers between devices: 8.88 us -> 7.45 us  [swap(): lax.ppermute(value, axis, [(i, partner(i)) for i in range(size) if 0 <= p...]
    unnamed x18 -> x22, local copies, waits for them, and re-layouts: 0.04 us -> 0.72 us
    pallas_call x6 -> x7, Pallas kernels: 8.02 us -> 8.35 us  [call(): pl.pallas_call(kernel, in_specs=specs, out_specs=jax.tree.map(lambda _: p...]
  transfers between devices with their start and end apart: 7 -> 7, of which waited for: 6 -> 5; matrix products, arithmetic and copies ran while one was open for 0% -> 0% of each run, Pallas kernels for 10% -> 13%
where the time goes in v6:
time: 27 us; the launch traced here: 26.9 us
  starting transfers between devices  9.58 us (35%)
  Pallas kernels  8.35 us (31%)
  waiting for transfers between devices  7.45 us (28%)
  between operations  0.78 us (3%)
  local copies, waits for them, and re-layouts  0.72 us (3%)
    ppermute x7, starting transfers between devices, swap(): lax.ppermute(value, axis, [(i, partner(i)) for i in range(size) if 0 <= p...  9.58 us
    pallas_call x7, Pallas kernels, call(): pl.pallas_call(kernel, in_specs=specs, out_specs=jax.tree.map(lambda _: p...  8.35 us
    ppermute x7, waiting for transfers between devices, swap(): lax.ppermute(value, axis, [(i, partner(i)) for i in range(size) if 0 <= p...  7.45 us
    unnamed x22, local copies, waits for them, and re-layouts  0.72 us
  transfers between devices with their start and end apart: 7, of which 5 were waited for; matrix products, arithmetic and copies ran while one was open for 0% of the time, Pallas kernels for 13%

profile of v6, /device:TPU:0, one launch (start us, length us, event | category | flops | bytes accessed | tf_op | source)
XLA Modules:
  0.0 26.9 jit_solution(3090958824844506534)
XLA Ops:
  0.6 1.6 %shard_map.221 = (f32[88,256]{1,0:T(8,128)S(1)}, f32[88,256]{1,0:T(8,128)S(1)}) custom-call(f32[1,4,64,128]{3,2,1,0:T(8,128)} %state_ref.5, bf16[4,80,192]{2,1,0:T(8,128)(2,1)} %constant.36.clone.left_ref, bf16[2,256,256]{2,1,0:T(8,128)(2,1)} %constant.37.clone.right_ref, bf16[2,256,128]{2,1,0:T(8,128)(2,1)} %constant.38.clone.corner_ref, ...), custom_call_target="tpu_custom_call" | custom-call | tf_op jit(solution)/shard_map/pallas_call | solution.py:120
  2.2 4.0 %collective-permute-start.2 = (f32[88,256]{1,0:T(8,128)S(1)}, f32[88,256]{1,0:T(8,128)S(1)}, u32[]{:S(2)}, u32[]{:S(2)}) collective-permute-start(f32[88,256]{1,0:T(8,128)S(1)} %get-tuple-element.23.own_ref), channel_id=1, source_target_pairs={{0,5},{1,4},{2,7},{3,6},{4,1},{5,0},{6,3},{7,2},{8,13},{9,12},{10,... | collective-permute-start | bytes 270344 | tf_op jit(solution)/shard_map/ppermute | solution.py:578
  6.2 0.5 %collective-permute-start = (f32[88,256]{1,0:T(8,128)S(1)}, f32[88,256]{1,0:T(8,128)S(1)}, u32[]{:S(2)}, u32[]{:S(2)}) collective-permute-start(f32[88,256]{1,0:T(8,128)S(1)} %get-tuple-element.23.own_ref), channel_id=1, source_target_pairs={{0,4},{4,0},{1,5},{5,1},{2,6},{6,2},{3,7},{7,3},{8,12},{12,8},{9,1... | collective-permute-start | bytes 270344 | tf_op jit(solution)/shard_map/ppermute | solution.py:578
  6.7 0.1 collective-permute-start.1
  6.9 0.0 copy-start
  6.9 1.8 %shard_map.222 = (f32[3,64,256]{2,1,0:T(8,128)S(1)}, bf16[3,64,192]{2,1,0:T(8,128)(2,1)S(1)}, bf16[3,128,256]{2,1,0:T(8,128)(2,1)S(1)}, bf16[384,192]{1,0:T(8,128)(2,1)S(1)}, bf16[3,256,256]{2,1,0:T(8,128)(2,1)S(1)}) custom-call(f32[3,4,64,64]{3,2,1,0:T(8,128)} %drive_ref, f32[2,64,128]{2,1,0:T(8,128)} %constant.41.clone.maps_x_ref, ...), custom_call_target="tpu_custom_call" | custom-call | tf_op jit(solution)/shard_map/pallas_call | solution.py:120
  8.7 0.0 copy-start.3
  8.7 0.7 %copy-done.3 = bf16[3,128,256]{2,1,0:T(8,128)(2,1)} copy-done((bf16[3,128,256]{2,1,0:T(8,128)(2,1)}, bf16[3,128,256]{2,1,0:T(8,128)(2,1)S(1)}, u32[]{:S(2)}) %copy-start.3) | copy-done | bytes 196632
  9.4 0.0 collective-permute-done.2.both_ref
  9.4 1.4 %collective-permute-done.y_ref.columns_ref = f32[88,256]{1,0:T(8,128)S(1)} collective-permute-done((f32[88,256]{1,0:T(8,128)S(1)}, f32[88,256]{1,0:T(8,128)S(1)}, u32[]{:S(2)}, u32[]{:S(2)}) %collective-permute-start) | collective-permute-done | bytes 90144 | tf_op jit(solution)/shard_map/ppermute | solution.py:578
  10.8 0.5 %collective-permute-done.1.x_ref = f32[88,256]{1,0:T(8,128)S(1)} collective-permute-done((f32[88,256]{1,0:T(8,128)S(1)}, f32[88,256]{1,0:T(8,128)S(1)}, u32[]{:S(2)}, u32[]{:S(2)}) %collective-permute-start.1) | collective-permute-done | bytes 90144 | tf_op jit(solution)/shard_map/ppermute | solution.py:578
  11.3 0.0 copy-done
  11.3 0.2 shard_map.223
  11.4 0.0 copy-start.10
  11.5 3.3 %collective-permute-start.3 = (f32[88,256]{1,0:T(8,128)S(1)}, f32[88,256]{1,0:T(8,128)S(1)}, u32[]{:S(2)}, u32[]{:S(2)}) collective-permute-start(f32[88,256]{1,0:T(8,128)S(1)} %get-tuple-element.33.own_ref), channel_id=1, source_target_pairs={{0,3},{1,2},{2,1},{3,0},{4,7},{5,6},{6,5},{7,4},{8,11},{9,10},{10,... | collective-permute-start | bytes 270344 | tf_op jit(solution)/shard_map/ppermute | solution.py:578
  14.8 3.1 %collective-permute-done.3.other_ref.second_ref = f32[88,256]{1,0:T(8,128)S(1)} collective-permute-done((f32[88,256]{1,0:T(8,128)S(1)}, f32[88,256]{1,0:T(8,128)S(1)}, u32[]{:S(2)}, u32[]{:S(2)}) %collective-permute-start.3) | collective-permute-done | bytes 90144 | tf_op jit(solution)/shard_map/ppermute | solution.py:578
  17.9 1.6 %collective-permute-start.4 = (f32[80,256]{1,0:T(8,128)S(1)}, f32[80,256]{1,0:T(8,128)S(1)}, u32[]{:S(2)}, u32[]{:S(2)}) collective-permute-start(f32[80,256]{1,0:T(8,128)S(1)} %shard_map.224.refs_0_), channel_id=1, source_target_pairs={{0,16},{8,24},{16,0},{24,8},{1,17},{9,25},{17,1},{25,9},{2,18},{10... | collective-permute-start | bytes 245768 | tf_op jit(solution)/shard_map/ppermute | solution.py:578
  19.4 0.0 collective-permute-start.5
  19.4 0.0 copy-done.10
  19.4 0.0 copy-start.1
  19.4 0.0 copy-start.2
  19.4 0.0 copy-start.5
  19.5 0.0 copy-start.7
  19.5 0.0 copy-start.9
  19.5 0.9 %shard_map.225.stepped_ref = f32[4,64,128]{2,1,0:T(8,128)S(1)} custom-call(f32[1,4,64,128]{3,2,1,0:T(8,128)S(1)} %copy-done, f32[88,256]{1,0:T(8,128)S(1)} %collective-permute-done.y_ref.columns_ref, f32[8,256]{1,0:T(8,128)S(1)} %get-tuple-element.34.first_ref, f32[88,256]{1,0:T(8,128)S(1)} %collective-permute-done.3.other_ref.second_ref, ...), custom_call_target="tpu_custom_call" | custom-call | tf_op jit(solution)/shard_map/pallas_call | solution.py:120
  20.4 0.0 copy-start.4
  20.4 0.0 copy-start.6
  20.4 0.0 copy-start.8
  20.5 1.9 %collective-permute-done.4.refs_1_ = f32[80,256]{1,0:T(8,128)S(1)} collective-permute-done((f32[80,256]{1,0:T(8,128)S(1)}, f32[80,256]{1,0:T(8,128)S(1)}, u32[]{:S(2)}, u32[]{:S(2)}) %collective-permute-start.4) | collective-permute-done | bytes 81952 | tf_op jit(solution)/shard_map/ppermute | solution.py:578
  22.4 0.0 collective-permute-start.6
  22.4 0.0 collective-permute-done.5.refs_2_
  22.4 0.0 copy-done.1
  22.4 0.0 copy-done.2
  22.4 0.0 copy-done.5
  22.4 0.0 copy-done.7
  22.4 0.0 copy-done.9
  22.4 0.6 %shard_map.226.early_ref = f32[3,3,64,256]{3,2,1,0:T(8,128)S(1)} custom-call(f32[80,256]{1,0:T(8,128)S(1)} %shard_map.224.refs_0_, f32[80,256]{1,0:T(8,128)S(1)} %collective-permute-done.4.refs_1_, f32[80,256]{1,0:T(8,128)S(1)} %collective-permute-done.5.refs_2_, bf16[32,384]{1,0:T(8,128)(2,1)S(1)} %copy-done.7, bf16[256,384]{1,0:T(8,128)(2,1)S(1)} %copy-done.1, ...), custom_call_target="tpu_custom_call" | custom-call | tf_op jit(solution)/shard_map/pallas_call | solution.py:120
  23.1 0.6 %collective-permute-done.6.refs_3_ = f32[80,256]{1,0:T(8,128)S(1)} collective-permute-done((f32[80,256]{1,0:T(8,128)S(1)}, f32[80,256]{1,0:T(8,128)S(1)}, u32[]{:S(2)}, u32[]{:S(2)}) %collective-permute-start.6) | collective-permute-done | bytes 81952 | tf_op jit(solution)/shard_map/ppermute | solution.py:578
  23.7 0.0 copy-done.4
  23.7 0.0 copy-done.6
  23.7 0.0 copy-done.8
  23.7 3.2 %shard_map.227 = (f32[1,4,64,128]{3,2,1,0:T(8,128)}, f32[1,4,64,64]{3,2,1,0:T(8,128)}) custom-call(f32[4,64,128]{2,1,0:T(8,128)S(1)} %shard_map.225.stepped_ref, f32[3,64,256]{2,1,0:T(8,128)S(1)} %get-tuple-element.36.drive_ref, bf16[3,64,192]{2,1,0:T(8,128)(2,1)S(1)} %get-tuple-element.37.row_ref, bf16[3,128,256]{2,1,0:T(8,128)(2,1)S(1)} %copy-done.4, ...), custom_call_target="tpu_custom_call" | custom-call | tf_op jit(solution)/shard_map/pallas_call | solution.py:120
  (1 shorter events, 0.0 us)
Async XLA Ops:
  2.2 7.2 %collective-permute-start.2 = (f32[88,256]{1,0:T(8,128)S(1)}, f32[88,256]{1,0:T(8,128)S(1)}, u32[]{:S(2)}, u32[]{:S(2)}) collective-permute-start(f32[88,256]{1,0:T(8,128)S(1)} %get-tuple-element.23.own_ref), channel_id=1, source_target_pairs={{0,5},{1,4},{2,7},{3,6},{4,1},{5,0},{6,3},{7,2},{8,13},{9,12},{10,... | collective-permute-start | bytes 270344 | tf_op jit(solution)/shard_map/ppermute | solution.py:578
  6.2 4.5 %collective-permute-start = (f32[88,256]{1,0:T(8,128)S(1)}, f32[88,256]{1,0:T(8,128)S(1)}, u32[]{:S(2)}, u32[]{:S(2)}) collective-permute-start(f32[88,256]{1,0:T(8,128)S(1)} %get-tuple-element.23.own_ref), channel_id=1, source_target_pairs={{0,4},{4,0},{1,5},{5,1},{2,6},{6,2},{3,7},{7,3},{8,12},{12,8},{9,1... | collective-permute-start | bytes 270344 | tf_op jit(solution)/shard_map/ppermute | solution.py:578
  6.7 4.5 %collective-permute-start.1 = (f32[88,256]{1,0:T(8,128)S(1)}, f32[88,256]{1,0:T(8,128)S(1)}, u32[]{:S(2)}, u32[]{:S(2)}) collective-permute-start(f32[88,256]{1,0:T(8,128)S(1)} %get-tuple-element.24), channel_id=1, source_target_pairs={{0,1},{1,0},{2,3},{3,2},{4,5},{5,4},{6,7},{7,6},{8,9},{9,8},{10,11... | collective-permute-start | bytes 270344 | tf_op jit(solution)/shard_map/ppermute | solution.py:578
  6.9 4.4 %copy-start = (f32[1,4,64,128]{3,2,1,0:T(8,128)S(1)}, f32[1,4,64,128]{3,2,1,0:T(8,128)}, u32[]{:S(2)}) copy-start(f32[1,4,64,128]{3,2,1,0:T(8,128)} %state_ref.5) | copy-start | bytes 393220
  8.7 0.7 %copy-start.3 = (bf16[3,128,256]{2,1,0:T(8,128)(2,1)}, bf16[3,128,256]{2,1,0:T(8,128)(2,1)S(1)}, u32[]{:S(2)}) copy-start(bf16[3,128,256]{2,1,0:T(8,128)(2,1)S(1)} %get-tuple-element.38.col_ref) | copy-start | bytes 589828
  11.4 8.0 %copy-start.10 = (bf16[32,128]{1,0:T(8,128)(2,1)S(1)}, bf16[32,128]{1,0:T(8,128)(2,1)}, u32[]{:S(2)}) copy-start(bf16[32,128]{1,0:T(8,128)(2,1)} %constant.45.clone.place_ref) | copy-start | bytes 24580
  11.5 6.4 %collective-permute-start.3 = (f32[88,256]{1,0:T(8,128)S(1)}, f32[88,256]{1,0:T(8,128)S(1)}, u32[]{:S(2)}, u32[]{:S(2)}) collective-permute-start(f32[88,256]{1,0:T(8,128)S(1)} %get-tuple-element.33.own_ref), channel_id=1, source_target_pairs={{0,3},{1,2},{2,1},{3,0},{4,7},{5,6},{6,5},{7,4},{8,11},{9,10},{10,... | collective-permute-start | bytes 270344 | tf_op jit(solution)/shard_map/ppermute | solution.py:578
  17.9 4.5 %collective-permute-start.4 = (f32[80,256]{1,0:T(8,128)S(1)}, f32[80,256]{1,0:T(8,128)S(1)}, u32[]{:S(2)}, u32[]{:S(2)}) collective-permute-start(f32[80,256]{1,0:T(8,128)S(1)} %shard_map.224.refs_0_), channel_id=1, source_target_pairs={{0,16},{8,24},{16,0},{24,8},{1,17},{9,25},{17,1},{25,9},{2,18},{10... | collective-permute-start | bytes 245768 | tf_op jit(solution)/shard_map/ppermute | solution.py:578
  19.4 3.0 %collective-permute-start.5 = (f32[80,256]{1,0:T(8,128)S(1)}, f32[80,256]{1,0:T(8,128)S(1)}, u32[]{:S(2)}, u32[]{:S(2)}) collective-permute-start(f32[80,256]{1,0:T(8,128)S(1)} %shard_map.224.refs_0_), channel_id=1, source_target_pairs={{0,8},{8,0},{16,24},{24,16},{1,9},{9,1},{17,25},{25,17},{2,10},{10... | collective-permute-start | bytes 245768 | tf_op jit(solution)/shard_map/ppermute | solution.py:578
  19.4 3.0 %copy-start.1 = (bf16[256,384]{1,0:T(8,128)(2,1)S(1)}, bf16[256,384]{1,0:T(8,128)(2,1)}, u32[]{:S(2)}) copy-start(bf16[256,384]{1,0:T(8,128)(2,1)} %constant.47.clone.refs_4_.refs_5_) | copy-start | bytes 589828
  19.4 3.0 %copy-start.2 = (f32[64,256]{1,0:T(8,128)S(1)}, f32[64,256]{1,0:T(8,128)}, u32[]{:S(2)}) copy-start(f32[64,256]{1,0:T(8,128)} %constant.49.clone.refs_6_.refs_7_) | copy-start | bytes 196612
  19.4 3.0 %copy-start.5 = (bf16[192,96]{1,0:T(8,128)(2,1)S(1)}, bf16[192,96]{1,0:T(8,128)(2,1)}, u32[]{:S(2)}) copy-start(bf16[192,96]{1,0:T(8,128)(2,1)} %constant.48.clone.refs_5_.refs_6_) | copy-start | bytes 110596
  19.5 3.0 %copy-start.7 = (bf16[32,384]{1,0:T(8,128)(2,1)S(1)}, bf16[32,384]{1,0:T(8,128)(2,1)}, u32[]{:S(2)}) copy-start(bf16[32,384]{1,0:T(8,128)(2,1)} %constant.46.clone.refs_3_.refs_4_) | copy-start | bytes 73732
  19.5 3.0 %copy-start.9 = (f32[8,256]{1,0:T(8,128)S(1)}, f32[8,256]{1,0:T(8,128)}, u32[]{:S(2)}) copy-start(f32[8,256]{1,0:T(8,128)} %constant.50.clone.refs_7_.refs_8_) | copy-start | bytes 24580
  20.4 3.2 %copy-start.4 = (bf16[3,128,256]{2,1,0:T(8,128)(2,1)S(1)}, bf16[3,128,256]{2,1,0:T(8,128)(2,1)}, u32[]{:S(2)}) copy-start(bf16[3,128,256]{2,1,0:T(8,128)(2,1)} %copy-done.3) | copy-start | bytes 589828
  20.4 3.2 %copy-start.6 = (bf16[2,128,256]{2,1,0:T(8,128)(2,1)S(1)}, bf16[2,128,256]{2,1,0:T(8,128)(2,1)}, u32[]{:S(2)}) copy-start(bf16[2,128,256]{2,1,0:T(8,128)(2,1)} %constant.58.sideways_ref) | copy-start | bytes 393220
  20.4 3.2 %copy-start.8 = (bf16[128,192]{1,0:T(8,128)(2,1)S(1)}, bf16[128,192]{1,0:T(8,128)(2,1)}, u32[]{:S(2)}) copy-start(bf16[128,192]{1,0:T(8,128)(2,1)} %constant.51.clone.again_ref) | copy-start | bytes 147460
  22.4 1.3 %collective-permute-start.6 = (f32[80,256]{1,0:T(8,128)S(1)}, f32[80,256]{1,0:T(8,128)S(1)}, u32[]{:S(2)}, u32[]{:S(2)}) collective-permute-start(f32[80,256]{1,0:T(8,128)S(1)} %collective-permute-done.4.refs_1_), channel_id=1, source_target_pairs={{0,8},{8,0},{16,24},{24,16},{1,9},{9,1},{17,25},{25,17},{2,10},{10... | collective-permute-start | bytes 245768 | tf_op jit(solution)/shard_map/ppermute | solution.py:578

commit v7 on v6

--- a/solution.py
+++ b/solution.py
@@ -140,8 +140,7 @@
         self.lanes = self.levels * self.modes
         self.half = self.levels // 2
         self.low = self.modes + EDGE
-        self.sums = self.low + EDGE
-        self.rows = self.sums + EDGE
+        self.rows = self.low + EDGE
         self.x = tables(self.nx * self.px, self.modes, self.windows)
         self.y = tables(self.ny * self.py, self.modes, self.windows)
         assert self.levels % 4 == 0 and self.modes * 2 == self.ny and self.nx == self.modes
@@ -156,7 +155,7 @@
         return jnp.concatenate([value[i * rows : (i + 1) * rows] for i in range(self.half)], 1)
 
 
-def project(plan, state, rates):
+def project(plan, state, rates, halved):
     low, half, lanes, levels = plan.low, plan.half, plan.lanes, plan.levels
     modes, nx, ny, windows = plan.modes, plan.nx, plan.ny, plan.windows
     bases = np.concatenate([plan.x["base"], plan.x["edges"], np.zeros((nx * plan.px, EDGE))], 1)
@@ -193,25 +192,32 @@
         row = lax.broadcasted_iota(jnp.int32, (EDGE, lanes), 0)
         lane = lax.broadcasted_iota(jnp.int32, (EDGE, lanes), 1)
         cells = jnp.sum(jnp.where(lane % EDGE == row, cells, 0.0), 0, keepdims=True)
-        gain = jnp.zeros((EDGE, lanes), jnp.float32)
+        lane = lane[:1]
+        gain = jnp.zeros((1, lanes), jnp.float32)
         for i in range(levels):
             gain = jnp.where(lane // modes == i, rates_ref[0, i], gain)
-        gain = jnp.where((px == 0) & (py == 0), gain, 0.0)
-        ends = jnp.where(row == EDGE - 1, gain, jnp.where(row == EDGE - 2, cells, ends))
-        out_ref[modes:low] = ends
+        gain = jnp.where((px == 0) & (py == 0) & (lane % modes >= 2 * windows * EDGE), gain, 0.0)
         upright = jnp.concatenate([rows[:modes, i * ny : (i + 1) * ny] for i in range(levels)], 0)
         upright = jnp.concatenate(halves(upright), 1)
-        out_ref[low : plan.sums] = dot(edge_ref[py], upright, ((1,), (1,)))[:EDGE]
+        sides = dot(edge_ref[py], upright, ((1,), (1,)))[: 2 * windows]
         patch = jnp.concatenate([state_ref[0, level] for level in range(levels)], 0)
         patch = jnp.concatenate(halves(patch), 1)
-        out_ref[plan.sums :] = dot(pick_ref[...], patch, ((1,), (1,)))[:EDGE]
-        along_ref[: plan.sums] = out_ref[: plan.sums]
-        lines = facing_rows(plan, state_ref, px % 2 == 0)
-        along_ref[plan.sums :] = jnp.concatenate([lines, jnp.zeros((2, lanes), jnp.float32)], 0)
+        columns = dot(pick_ref[...], patch, ((1,), (1,)))[:EDGE]
+        if halved:
+            ends = jnp.where(px < plan.px // 2, ends[:windows], ends[windows : 2 * windows])
+            out_ref[modes:low] = jnp.concatenate([sides, cells + gain, ends[:1]], 0)
+            out_ref[low:] = jnp.concatenate([ends[1:], columns[: 2 * windows]], 0)
+            along_ref[:low] = out_ref[:low]
+            along_ref[low:] = jnp.concatenate([ends[1:], facing_rows(plan, state_ref, px % 2 == 0)], 0)
+        else:
+            blank = jnp.zeros((2, lanes), jnp.float32)
+            out_ref[modes:low] = jnp.concatenate([sides, cells + gain, blank[:1]], 0)
+            out_ref[low:] = jnp.concatenate([ends[: 2 * windows], blank], 0)
+            along_ref[...] = columns
 
     return call(
         kernel,
-        (shape_of(plan.rows, lanes), shape_of(plan.rows, lanes)),
+        (shape_of(plan.rows, lanes), shape_of(plan.rows if halved else EDGE, lanes)),
         state, left, jnp.asarray(np.stack(right)), jnp.asarray(np.stack(corner)), jnp.asarray(np.stack(edge)),
         jnp.asarray(bf16(pick)), rates,
         first=True,
@@ -229,51 +235,74 @@
 
 
 def facing_corners(plan, columns, bottom):
-    lane = lax.broadcasted_iota(jnp.int32, (EDGE, plan.lanes), 1)
+    lane = lax.broadcasted_iota(jnp.int32, columns.shape, 1)
     moved = pltpu.roll(columns, plan.lanes - (plan.nx - plan.windows), 1)
     near = jnp.where(lane % plan.nx < plan.windows, jnp.where(bottom, moved, columns), 0.0)
-    packed = near[:1]
+    first = columns.shape[0] - 2 * plan.windows
+    packed = near[first : first + 1]
     for i in range(1, 2 * plan.windows):
-        packed = packed + pltpu.roll(near, EDGE * i, 1)[i : i + 1]
-    return jnp.concatenate([packed, jnp.zeros((1, plan.lanes), jnp.float32)], 0)
+        packed = packed + pltpu.roll(near, EDGE * i, 1)[first + i : first + i + 1]
+    return packed
 
 
 def join_first(plan, own, from_y, from_x, from_both, state):
-    sums, windows = plan.sums, plan.windows
+    low, modes, windows, lanes = plan.low, plan.modes, plan.windows, plan.lanes
 
     def kernel(own_ref, y_ref, x_ref, both_ref, state_ref, out_ref, halo_ref):
-        odd = lax.axis_index("px") % 2 == 1
-        out_ref[:sums] = (own_ref[:sums] + y_ref[:sums]) + (x_ref[:sums] + both_ref[:sums])
-        corners = facing_corners(plan, y_ref[sums:], odd)
-        out_ref[sums:] = jnp.concatenate([facing_rows(plan, state_ref, odd), corners], 0)
-        corners = facing_corners(plan, both_ref[sums:], odd)
-        halo_ref[...] = jnp.concatenate([x_ref[sums : sums + 2 * windows], corners], 0)
-
-    shapes = shape_of(plan.rows, plan.lanes), shape_of(EDGE, plan.lanes)
+        px = lax.axis_index("px")
+        odd, lower = px % 2 == 1, px < plan.px // 2
+        out_ref[:modes] = (own_ref[:modes] + y_ref[:modes]) + (x_ref[:modes] + both_ref[:modes])
+        middle = (own_ref[modes:low] + y_ref[modes:low]) + (x_ref[modes:low] + both_ref[modes:low])
+        corners = facing_corners(plan, y_ref[low:], odd)
+        corners = jnp.where(lower, pltpu.roll(corners, windows, 1), corners)
+        row = lax.broadcasted_iota(jnp.int32, (EDGE, lanes), 0)
+        out_ref[modes:low] = middle + jnp.where(row == 2 * windows, corners, 0.0)
+        ends = (own_ref[low:] + y_ref[low:]) + (x_ref[low:] + both_ref[low:])
+        out_ref[low:] = jnp.concatenate([ends[: windows - 1], facing_rows(plan, state_ref, odd)], 0)
+        corners = facing_corners(plan, both_ref[low:], odd)
+        lines = x_ref[low:][windows - 1 :]
+        halo_ref[...] = jnp.concatenate([lines, corners, jnp.zeros((1, lanes), jnp.float32)], 0)
+
+    shapes = shape_of(plan.rows, lanes), shape_of(EDGE, lanes)
     return call(kernel, shapes, own, from_y, from_x, from_both, state)
 
 
 def both_facing(plan, state, columns):
     def kernel(state_ref, columns_ref, top_ref, bottom_ref):
-        columns = columns_ref[plan.sums :]
+        columns = columns_ref[...]
+        columns = jnp.concatenate([jnp.zeros((2, plan.lanes), jnp.float32), columns[: 2 * plan.windows]], 0)
         for ref, bottom in ((top_ref, False), (bottom_ref, True)):
             rows = [facing_rows(plan, state_ref, bottom), facing_corners(plan, columns, bottom)]
-            ref[...] = jnp.concatenate(rows, 0)
+            ref[...] = jnp.concatenate(rows + [jnp.zeros((1, plan.lanes), jnp.float32)], 0)
 
     return call(kernel, (shape_of(EDGE, plan.lanes),) * 2, state, columns)
 
 
 def join_last(plan, own, other):
-    sums = plan.sums
+    low, modes, windows, lanes = plan.low, plan.modes, plan.windows, plan.lanes
 
     def kernel(own_ref, other_ref, out_ref):
-        out_ref[...] = own_ref[:sums] + other_ref[:sums]
-
-    return call(kernel, shape_of(sums, plan.lanes), own, other)
+        lower = lax.axis_index("px") < plan.px // 2
+        out_ref[:modes] = own_ref[:modes] + other_ref[:modes]
+        row = lax.broadcasted_iota(jnp.int32, (EDGE, lanes), 0)
+        lane = lax.broadcasted_iota(jnp.int32, (EDGE, lanes), 1)
+        one, two = own_ref[modes:low], other_ref[modes:low]
+        early, late = jnp.where(lower, one, two), jnp.where(lower, two, one)
+        kept = (row < 2 * windows) | (lane % modes >= 2 * windows * EDGE)
+        middle = jnp.where(kept | (lane % EDGE < windows), early, 0.0)
+        middle = middle + jnp.where(kept | (lane % EDGE >= windows), late, 0.0)
+        out_ref[modes:low] = jnp.where(row <= 2 * windows, middle, 0.0)
+        ends = []
+        for block, rest in ((early, jnp.where(lower, own_ref[low:], other_ref[low:])),
+                            (late, jnp.where(lower, other_ref[low:], own_ref[low:]))):
+            ends += [block[EDGE - 1 :], rest[: windows - 1]]
+        out_ref[low:] = jnp.concatenate(ends + [jnp.zeros((EDGE - 2 * windows, lanes), jnp.float32)], 0)
+
+    return call(kernel, shape_of(plan.rows, lanes), own, other)
 
 
 def step_patch(plan, state, columns, first, second):
-    nx, ny, windows, sums, levels = plan.nx, plan.ny, plan.windows, plan.sums, plan.levels
+    nx, ny, windows, low, levels = plan.nx, plan.ny, plan.windows, plan.low, plan.levels
     place = np.zeros((4 * EDGE, ny))
     for i in range(windows):
         for part in range(3):
@@ -309,9 +338,14 @@
             ]
 
         even = px % 2 == 0
-        one, two = first_ref[...], second_ref[second_ref.shape[0] - EDGE :]
+        one, two, columns = first_ref[...], second_ref[-EDGE:], columns_ref[-EDGE:]
+        if second_ref.shape[0] > EDGE:
+            mixed = second_ref[low - 2 : low - 1]
+            mixed = jnp.where(px < plan.px // 2, mixed, pltpu.roll(mixed, plan.lanes - windows, 1))
+            two = jnp.concatenate([two[windows - 1 :], mixed, mixed], 0)
+            columns = jnp.concatenate([columns[windows - 1 :], columns[: windows - 1]], 0)
         above, below = jnp.where(even, two, one), jnp.where(even, one, two)
-        beside = spread(columns_ref[sums:])
+        beside = spread(columns)
         beside_above, beside_below = corners(above), corners(below)
         blank = jnp.zeros((EDGE - windows, lanes), jnp.float32)
         for level in range(levels):
@@ -438,7 +472,7 @@
 
 
 def own_modes_of(plan, inward_ref, corner_ref, across_ref, scale_x_ref, scale_y_ref):
-    modes, low, lanes, sums = plan.modes, plan.low, plan.lanes, plan.sums
+    modes, low, lanes = plan.modes, plan.low, plan.lanes
     windows, half, ny = plan.windows, plan.half, plan.ny
     scale_x, scale_y = scale_x_ref[...], scale_y_ref[:1]
     row = lax.broadcasted_iota(jnp.int32, (EDGE, lanes), 0)
@@ -447,9 +481,9 @@
     left_lane = lax.broadcasted_iota(jnp.int32, (modes, ny), 1) < modes
 
     def own_modes(message):
-        rows, ends = message[:modes], message[modes:low]
-        sides = dot(short_stacked(message[low:sums], 4 * EDGE), inward_ref[...], ((0,), (0,)))
-        cells = jnp.where(mine, jnp.broadcast_to(ends[EDGE - 2 : EDGE - 1], (EDGE, lanes)), 0.0)
+        rows, middle, ends = message[:modes], message[modes:low], message[low:]
+        sides = dot(short_stacked(middle, 4 * EDGE), inward_ref[...], ((0,), (0,)))
+        cells = jnp.where(mine, jnp.broadcast_to(middle[EDGE - 2 : EDGE - 1], (EDGE, lanes)), 0.0)
         cells = jnp.concatenate([cells[:, i * ny : (i + 1) * ny] for i in range(half)], 0)
         cells = by_parts(cells, corner_ref[:ny], corner_ref[ny:])
         turned, ends = [rows], [ends]
@@ -508,7 +542,12 @@
         root = plan.nest - 1
         nest = lax.axis_index("nest")
         refs, table_refs = refs[: plan.nest], refs[plan.nest :]
-        gains = [ref[low - 1 : low] for ref in refs]
+        lane = lax.broadcasted_iota(jnp.int32, (1, lanes), 1)
+        gains = []
+        for ref in refs:
+            gain = jnp.where(lane % modes >= modes - 2 * EDGE, ref[low - 2 : low - 1], 0.0)
+            gain = gain + pltpu.roll(gain, lanes - 2 * EDGE, 1)
+            gains.append(gain + pltpu.roll(gain, lanes - 4 * EDGE, 1))
         owns = [[early_ref[i, w] for w in range(windows)] for i in range(root)]
         owns.append(own_modes_of(plan, *table_refs)(refs[root][...]))
         if crossed:
@@ -580,8 +619,9 @@
 
 def body(initial_state, drive_modes, relax_rates, nest_offsets):
     plan = Plan(initial_state, drive_modes)
-    share, along = project(plan, initial_state, relax_rates)
-    if plan.py == 2 and plan.px == 4:
+    halved = plan.py == 2 and plan.px == 4
+    share, along = project(plan, initial_state, relax_rates, halved)
+    if halved:
         share, drive_modes, nest_offsets = lax.optimization_barrier((share, drive_modes, nest_offsets))
         from_y = swap(share, "py", lambda i: i ^ 1)
         from_x = swap(along, "px", lambda i: i ^ 1)
@@ -593,16 +633,16 @@
         across = swap(total, "px", lambda i: i ^ 3)
         last = join_last(plan, total, across)
     else:
-        from_right = jnp.arange(plan.rows)[:, None] < plan.sums + plan.windows
-        right = swap(share, "py", lambda i: i - 1)
-        left = swap(share, "py", lambda i: i + 1)
+        from_right = jnp.arange(EDGE)[:, None] < plan.windows
+        right = swap(along, "py", lambda i: i - 1)
+        left = swap(along, "py", lambda i: i + 1)
         columns = jnp.where(from_right, right, left)
         top, bottom = both_facing(plan, initial_state, columns)
         above = swap(bottom, "px", lambda i: i + 1)
         below = swap(top, "px", lambda i: i - 1)
         even = lax.axis_index("px") % 2 == 0
         halo, across = jnp.where(even, below, above), jnp.where(even, above, below)
-        last = lax.psum(share[: plan.sums], ("py", "px"))
+        last = lax.psum(share, ("py", "px"))
         prepared = prepare(plan, drive_modes, nest_offsets)
     crossed = plan.nest == 4
     if crossed:

time: 27 us -> 26.9 us (level)
  starting transfers between devices: 9.58 us -> 9.28 us
    ppermute x7, starting transfers between devices: 9.58 us -> 9.28 us  [swap(): lax.ppermute(value, axis, [(i, partner(i)) for i in range(size) if 0 <= p...]
where the time goes in v7:
time: 26.9 us; the launch traced here: 26.7 us
  starting transfers between devices  9.28 us (34%)
  Pallas kernels  8.44 us (31%)
  waiting for transfers between devices  7.52 us (28%)
  between operations  0.76 us (3%)
  local copies, waits for them, and re-layouts  0.71 us (3%)
    ppermute x7, starting transfers between devices, swap(): lax.ppermute(value, axis, [(i, partner(i)) for i in range(size) if 0 <= p...  9.28 us
    pallas_call x7, Pallas kernels, call(): pl.pallas_call(kernel, in_specs=specs, out_specs=jax.tree.map(lambda _: p...  8.44 us
    ppermute x7, waiting for transfers between devices, swap(): lax.ppermute(value, axis, [(i, partner(i)) for i in range(size) if 0 <= p...  7.52 us
    unnamed x22, local copies, waits for them, and re-layouts  0.71 us
  transfers between devices with their start and end apart: 7, of which 5 were waited for; matrix products, arithmetic and copies ran while one was open for 0% of the time, Pallas kernels for 13%

profile of v7, /device:TPU:0, one launch (start us, length us, event | category | flops | bytes accessed | tf_op | source)
XLA Modules:
  0.0 26.7 jit_solution(6673294177491088344)
XLA Ops:
  0.6 1.6 %shard_map.221 = (f32[80,256]{1,0:T(8,128)S(1)}, f32[80,256]{1,0:T(8,128)S(1)}) custom-call(f32[1,4,64,128]{3,2,1,0:T(8,128)} %state_ref.5, bf16[4,80,192]{2,1,0:T(8,128)(2,1)} %constant.36.clone.left_ref, bf16[2,256,256]{2,1,0:T(8,128)(2,1)} %constant.37.clone.right_ref, bf16[2,256,128]{2,1,0:T(8,128)(2,1)} %constant.38.clone.corner_ref, ...), custom_call_target="tpu_custom_call" | custom-call | tf_op jit(solution)/shard_map/pallas_call | solution.py:120
  2.2 4.0 %collective-permute-start.2 = (f32[80,256]{1,0:T(8,128)S(1)}, f32[80,256]{1,0:T(8,128)S(1)}, u32[]{:S(2)}, u32[]{:S(2)}) collective-permute-start(f32[80,256]{1,0:T(8,128)S(1)} %get-tuple-element.23.own_ref), channel_id=1, source_target_pairs={{0,5},{1,4},{2,7},{3,6},{4,1},{5,0},{6,3},{7,2},{8,13},{9,12},{10,... | collective-permute-start | bytes 245768 | tf_op jit(solution)/shard_map/ppermute | solution.py:617
  6.2 0.5 %collective-permute-start = (f32[80,256]{1,0:T(8,128)S(1)}, f32[80,256]{1,0:T(8,128)S(1)}, u32[]{:S(2)}, u32[]{:S(2)}) collective-permute-start(f32[80,256]{1,0:T(8,128)S(1)} %get-tuple-element.23.own_ref), channel_id=1, source_target_pairs={{0,4},{4,0},{1,5},{5,1},{2,6},{6,2},{3,7},{7,3},{8,12},{12,8},{9,1... | collective-permute-start | bytes 245768 | tf_op jit(solution)/shard_map/ppermute | solution.py:617
  6.7 0.1 collective-permute-start.1
  6.9 0.0 copy-start
  6.9 1.8 %shard_map.222 = (f32[3,64,256]{2,1,0:T(8,128)S(1)}, bf16[3,64,192]{2,1,0:T(8,128)(2,1)S(1)}, bf16[3,128,256]{2,1,0:T(8,128)(2,1)S(1)}, bf16[384,192]{1,0:T(8,128)(2,1)S(1)}, bf16[3,256,256]{2,1,0:T(8,128)(2,1)S(1)}) custom-call(f32[3,4,64,64]{3,2,1,0:T(8,128)} %drive_ref, f32[2,64,128]{2,1,0:T(8,128)} %constant.41.clone.maps_x_ref, ...), custom_call_target="tpu_custom_call" | custom-call | tf_op jit(solution)/shard_map/pallas_call | solution.py:120
  8.7 0.0 copy-start.3
  8.7 0.7 %copy-done.3 = bf16[3,128,256]{2,1,0:T(8,128)(2,1)} copy-done((bf16[3,128,256]{2,1,0:T(8,128)(2,1)}, bf16[3,128,256]{2,1,0:T(8,128)(2,1)S(1)}, u32[]{:S(2)}) %copy-start.3) | copy-done | bytes 196632
  9.4 0.0 collective-permute-done.2.both_ref
  9.4 1.3 %collective-permute-done.y_ref.columns_ref = f32[80,256]{1,0:T(8,128)S(1)} collective-permute-done((f32[80,256]{1,0:T(8,128)S(1)}, f32[80,256]{1,0:T(8,128)S(1)}, u32[]{:S(2)}, u32[]{:S(2)}) %collective-permute-start) | collective-permute-done | bytes 81952 | tf_op jit(solution)/shard_map/ppermute | solution.py:617
  10.7 0.5 %collective-permute-done.1.x_ref = f32[80,256]{1,0:T(8,128)S(1)} collective-permute-done((f32[80,256]{1,0:T(8,128)S(1)}, f32[80,256]{1,0:T(8,128)S(1)}, u32[]{:S(2)}, u32[]{:S(2)}) %collective-permute-start.1) | collective-permute-done | bytes 81952 | tf_op jit(solution)/shard_map/ppermute | solution.py:617
  11.2 0.0 copy-done
  11.2 0.2 shard_map.223
  11.4 0.0 copy-start.10
  11.4 3.0 %collective-permute-start.3 = (f32[80,256]{1,0:T(8,128)S(1)}, f32[80,256]{1,0:T(8,128)S(1)}, u32[]{:S(2)}, u32[]{:S(2)}) collective-permute-start(f32[80,256]{1,0:T(8,128)S(1)} %get-tuple-element.33.own_ref), channel_id=1, source_target_pairs={{0,3},{1,2},{2,1},{3,0},{4,7},{5,6},{6,5},{7,4},{8,11},{9,10},{10,... | collective-permute-start | bytes 245768 | tf_op jit(solution)/shard_map/ppermute | solution.py:617
  14.5 3.2 %collective-permute-done.3.other_ref.second_ref = f32[80,256]{1,0:T(8,128)S(1)} collective-permute-done((f32[80,256]{1,0:T(8,128)S(1)}, f32[80,256]{1,0:T(8,128)S(1)}, u32[]{:S(2)}, u32[]{:S(2)}) %collective-permute-start.3) | collective-permute-done | bytes 81952 | tf_op jit(solution)/shard_map/ppermute | solution.py:617
  17.7 1.6 %collective-permute-start.4 = (f32[80,256]{1,0:T(8,128)S(1)}, f32[80,256]{1,0:T(8,128)S(1)}, u32[]{:S(2)}, u32[]{:S(2)}) collective-permute-start(f32[80,256]{1,0:T(8,128)S(1)} %shard_map.224.refs_0_), channel_id=1, source_target_pairs={{0,16},{8,24},{16,0},{24,8},{1,17},{9,25},{17,1},{25,9},{2,18},{10... | collective-permute-start | bytes 245768 | tf_op jit(solution)/shard_map/ppermute | solution.py:617
  19.3 0.0 collective-permute-start.5
  19.3 0.0 copy-done.10
  19.3 0.0 copy-start.1
  19.3 0.0 copy-start.2
  19.3 0.0 copy-start.5
  19.3 0.0 copy-start.7
  19.3 0.0 copy-start.9
  19.3 1.0 %shard_map.225.stepped_ref = f32[4,64,128]{2,1,0:T(8,128)S(1)} custom-call(f32[1,4,64,128]{3,2,1,0:T(8,128)S(1)} %copy-done, f32[80,256]{1,0:T(8,128)S(1)} %collective-permute-done.y_ref.columns_ref, f32[8,256]{1,0:T(8,128)S(1)} %get-tuple-element.34.first_ref, f32[80,256]{1,0:T(8,128)S(1)} %collective-permute-done.3.other_ref.second_ref, ...), custom_call_target="tpu_custom_call" | custom-call | tf_op jit(solution)/shard_map/pallas_call | solution.py:120
  20.3 0.0 copy-start.4
  20.3 0.0 copy-start.6
  20.3 0.0 copy-start.8
  20.3 1.9 %collective-permute-done.4.refs_1_ = f32[80,256]{1,0:T(8,128)S(1)} collective-permute-done((f32[80,256]{1,0:T(8,128)S(1)}, f32[80,256]{1,0:T(8,128)S(1)}, u32[]{:S(2)}, u32[]{:S(2)}) %collective-permute-start.4) | collective-permute-done | bytes 81952 | tf_op jit(solution)/shard_map/ppermute | solution.py:617
  22.2 0.0 collective-permute-start.6
  22.2 0.0 collective-permute-done.5.refs_2_
  22.2 0.0 copy-done.1
  22.2 0.0 copy-done.2
  22.2 0.0 copy-done.5
  22.2 0.0 copy-done.7
  22.2 0.0 copy-done.9
  22.3 0.6 %shard_map.226.early_ref = f32[3,3,64,256]{3,2,1,0:T(8,128)S(1)} custom-call(f32[80,256]{1,0:T(8,128)S(1)} %shard_map.224.refs_0_, f32[80,256]{1,0:T(8,128)S(1)} %collective-permute-done.4.refs_1_, f32[80,256]{1,0:T(8,128)S(1)} %collective-permute-done.5.refs_2_, bf16[32,384]{1,0:T(8,128)(2,1)S(1)} %copy-done.7, bf16[256,384]{1,0:T(8,128)(2,1)S(1)} %copy-done.1, ...), custom_call_target="tpu_custom_call" | custom-call | tf_op jit(solution)/shard_map/pallas_call | solution.py:120
  22.9 0.6 %collective-permute-done.6.refs_3_ = f32[80,256]{1,0:T(8,128)S(1)} collective-permute-done((f32[80,256]{1,0:T(8,128)S(1)}, f32[80,256]{1,0:T(8,128)S(1)}, u32[]{:S(2)}, u32[]{:S(2)}) %collective-permute-start.6) | collective-permute-done | bytes 81952 | tf_op jit(solution)/shard_map/ppermute | solution.py:617
  23.5 0.0 copy-done.4
  23.5 0.0 copy-done.6
  23.5 0.0 copy-done.8
  23.5 3.2 %shard_map.227 = (f32[1,4,64,128]{3,2,1,0:T(8,128)}, f32[1,4,64,64]{3,2,1,0:T(8,128)}) custom-call(f32[4,64,128]{2,1,0:T(8,128)S(1)} %shard_map.225.stepped_ref, f32[3,64,256]{2,1,0:T(8,128)S(1)} %get-tuple-element.36.drive_ref, bf16[3,64,192]{2,1,0:T(8,128)(2,1)S(1)} %get-tuple-element.37.row_ref, bf16[3,128,256]{2,1,0:T(8,128)(2,1)S(1)} %copy-done.4, ...), custom_call_target="tpu_custom_call" | custom-call | tf_op jit(solution)/shard_map/pallas_call | solution.py:120
  (1 shorter events, 0.0 us)
Async XLA Ops:
  2.2 7.2 %collective-permute-start.2 = (f32[80,256]{1,0:T(8,128)S(1)}, f32[80,256]{1,0:T(8,128)S(1)}, u32[]{:S(2)}, u32[]{:S(2)}) collective-permute-start(f32[80,256]{1,0:T(8,128)S(1)} %get-tuple-element.23.own_ref), channel_id=1, source_target_pairs={{0,5},{1,4},{2,7},{3,6},{4,1},{5,0},{6,3},{7,2},{8,13},{9,12},{10,... | collective-permute-start | bytes 245768 | tf_op jit(solution)/shard_map/ppermute | solution.py:617
  6.2 4.4 %collective-permute-start = (f32[80,256]{1,0:T(8,128)S(1)}, f32[80,256]{1,0:T(8,128)S(1)}, u32[]{:S(2)}, u32[]{:S(2)}) collective-permute-start(f32[80,256]{1,0:T(8,128)S(1)} %get-tuple-element.23.own_ref), channel_id=1, source_target_pairs={{0,4},{4,0},{1,5},{5,1},{2,6},{6,2},{3,7},{7,3},{8,12},{12,8},{9,1... | collective-permute-start | bytes 245768 | tf_op jit(solution)/shard_map/ppermute | solution.py:617
  6.7 4.4 %collective-permute-start.1 = (f32[80,256]{1,0:T(8,128)S(1)}, f32[80,256]{1,0:T(8,128)S(1)}, u32[]{:S(2)}, u32[]{:S(2)}) collective-permute-start(f32[80,256]{1,0:T(8,128)S(1)} %get-tuple-element.24), channel_id=1, source_target_pairs={{0,1},{1,0},{2,3},{3,2},{4,5},{5,4},{6,7},{7,6},{8,9},{9,8},{10,11... | collective-permute-start | bytes 245768 | tf_op jit(solution)/shard_map/ppermute | solution.py:617
  6.9 4.3 %copy-start = (f32[1,4,64,128]{3,2,1,0:T(8,128)S(1)}, f32[1,4,64,128]{3,2,1,0:T(8,128)}, u32[]{:S(2)}) copy-start(f32[1,4,64,128]{3,2,1,0:T(8,128)} %state_ref.5) | copy-start | bytes 393220
  8.7 0.7 %copy-start.3 = (bf16[3,128,256]{2,1,0:T(8,128)(2,1)}, bf16[3,128,256]{2,1,0:T(8,128)(2,1)S(1)}, u32[]{:S(2)}) copy-start(bf16[3,128,256]{2,1,0:T(8,128)(2,1)S(1)} %get-tuple-element.38.col_ref) | copy-start | bytes 589828
  11.4 7.8 %copy-start.10 = (bf16[32,128]{1,0:T(8,128)(2,1)S(1)}, bf16[32,128]{1,0:T(8,128)(2,1)}, u32[]{:S(2)}) copy-start(bf16[32,128]{1,0:T(8,128)(2,1)} %constant.45.clone.place_ref) | copy-start | bytes 24580
  11.4 6.3 %collective-permute-start.3 = (f32[80,256]{1,0:T(8,128)S(1)}, f32[80,256]{1,0:T(8,128)S(1)}, u32[]{:S(2)}, u32[]{:S(2)}) collective-permute-start(f32[80,256]{1,0:T(8,128)S(1)} %get-tuple-element.33.own_ref), channel_id=1, source_target_pairs={{0,3},{1,2},{2,1},{3,0},{4,7},{5,6},{6,5},{7,4},{8,11},{9,10},{10,... | collective-permute-start | bytes 245768 | tf_op jit(solution)/shard_map/ppermute | solution.py:617
  17.7 4.5 %collective-permute-start.4 = (f32[80,256]{1,0:T(8,128)S(1)}, f32[80,256]{1,0:T(8,128)S(1)}, u32[]{:S(2)}, u32[]{:S(2)}) collective-permute-start(f32[80,256]{1,0:T(8,128)S(1)} %shard_map.224.refs_0_), channel_id=1, source_target_pairs={{0,16},{8,24},{16,0},{24,8},{1,17},{9,25},{17,1},{25,9},{2,18},{10... | collective-permute-start | bytes 245768 | tf_op jit(solution)/shard_map/ppermute | solution.py:617
  19.3 3.0 %collective-permute-start.5 = (f32[80,256]{1,0:T(8,128)S(1)}, f32[80,256]{1,0:T(8,128)S(1)}, u32[]{:S(2)}, u32[]{:S(2)}) collective-permute-start(f32[80,256]{1,0:T(8,128)S(1)} %shard_map.224.refs_0_), channel_id=1, source_target_pairs={{0,8},{8,0},{16,24},{24,16},{1,9},{9,1},{17,25},{25,17},{2,10},{10... | collective-permute-start | bytes 245768 | tf_op jit(solution)/shard_map/ppermute | solution.py:617
  19.3 3.0 %copy-start.1 = (bf16[256,384]{1,0:T(8,128)(2,1)S(1)}, bf16[256,384]{1,0:T(8,128)(2,1)}, u32[]{:S(2)}) copy-start(bf16[256,384]{1,0:T(8,128)(2,1)} %constant.47.clone.refs_4_.refs_5_) | copy-start | bytes 589828
  19.3 3.0 %copy-start.2 = (f32[64,256]{1,0:T(8,128)S(1)}, f32[64,256]{1,0:T(8,128)}, u32[]{:S(2)}) copy-start(f32[64,256]{1,0:T(8,128)} %constant.49.clone.refs_6_.refs_7_) | copy-start | bytes 196612
  19.3 3.0 %copy-start.5 = (bf16[192,96]{1,0:T(8,128)(2,1)S(1)}, bf16[192,96]{1,0:T(8,128)(2,1)}, u32[]{:S(2)}) copy-start(bf16[192,96]{1,0:T(8,128)(2,1)} %constant.48.clone.refs_5_.refs_6_) | copy-start | bytes 110596
  19.3 3.0 %copy-start.7 = (bf16[32,384]{1,0:T(8,128)(2,1)S(1)}, bf16[32,384]{1,0:T(8,128)(2,1)}, u32[]{:S(2)}) copy-start(bf16[32,384]{1,0:T(8,128)(2,1)} %constant.46.clone.refs_3_.refs_4_) | copy-start | bytes 73732
  19.3 3.0 %copy-start.9 = (f32[8,256]{1,0:T(8,128)S(1)}, f32[8,256]{1,0:T(8,128)}, u32[]{:S(2)}) copy-start(f32[8,256]{1,0:T(8,128)} %constant.50.clone.refs_7_.refs_8_) | copy-start | bytes 24580
  20.3 3.2 %copy-start.4 = (bf16[3,128,256]{2,1,0:T(8,128)(2,1)S(1)}, bf16[3,128,256]{2,1,0:T(8,128)(2,1)}, u32[]{:S(2)}) copy-start(bf16[3,128,256]{2,1,0:T(8,128)(2,1)} %copy-done.3) | copy-start | bytes 589828
  20.3 3.2 %copy-start.6 = (bf16[2,128,256]{2,1,0:T(8,128)(2,1)S(1)}, bf16[2,128,256]{2,1,0:T(8,128)(2,1)}, u32[]{:S(2)}) copy-start(bf16[2,128,256]{2,1,0:T(8,128)(2,1)} %constant.58.sideways_ref) | copy-start | bytes 393220
  20.3 3.2 %copy-start.8 = (bf16[128,192]{1,0:T(8,128)(2,1)S(1)}, bf16[128,192]{1,0:T(8,128)(2,1)}, u32[]{:S(2)}) copy-start(bf16[128,192]{1,0:T(8,128)(2,1)} %constant.51.clone.again_ref) | copy-start | bytes 147460
  22.2 1.3 %collective-permute-start.6 = (f32[80,256]{1,0:T(8,128)S(1)}, f32[80,256]{1,0:T(8,128)S(1)}, u32[]{:S(2)}, u32[]{:S(2)}) collective-permute-start(f32[80,256]{1,0:T(8,128)S(1)} %collective-permute-done.4.refs_1_), channel_id=1, source_target_pairs={{0,8},{8,0},{16,24},{24,16},{1,9},{9,1},{17,25},{25,17},{2,10},{10... | collective-permute-start | bytes 245768 | tf_op jit(solution)/shard_map/ppermute | solution.py:617

commit v8 on v7

--- a/solution.py
+++ b/solution.py
@@ -159,36 +159,40 @@
     low, half, lanes, levels = plan.low, plan.half, plan.lanes, plan.levels
     modes, nx, ny, windows = plan.modes, plan.nx, plan.ny, plan.windows
     bases = np.concatenate([plan.x["base"], plan.x["edges"], np.zeros((nx * plan.px, EDGE))], 1)
-    left = left_table(bases.T.reshape(low + EDGE, plan.px, nx).transpose(1, 0, 2))
+    left = right_table(bases.T.reshape(low + EDGE, plan.px, nx).transpose(1, 0, 2))
     base_y = plan.y["base"].reshape(plan.py, ny, modes)
     edge_y = plan.y["edges"].reshape(plan.py, ny, EDGE)
-    right, corner, edge = [], [], []
+    right, edge = [], []
     for at in range(plan.py):
-        high, small = parts_of(kron(2, base_y[at]))
-        right.append(np.concatenate([high, small], 1))
-        corner.append(bf16(kron(2, np.repeat(edge_y[at], EDGE, 1))))
+        high, small = parts_of(base_y[at])
+        corner = bf16(np.repeat(edge_y[at], EDGE, 1))
+        right.append(np.concatenate([high, small, corner, np.zeros_like(corner)], 1))
         edge.append(bf16(np.pad(np.tile(edge_y[at].T, (1, 2)), ((0, EDGE), (0, 0)))))
     pick = np.zeros((2 * EDGE, 2 * ny))
     for i in range(windows):
         pick[i, [i, ny + i]] = 1
         pick[windows + i, [ny - windows + i, 2 * ny - windows + i]] = 1
 
-    def kernel(state_ref, left_ref, right_ref, corner_ref, edge_ref, pick_ref, rates_ref, out_ref, along_ref):
+    def kernel(state_ref, left_ref, right_ref, edge_ref, pick_ref, rates_ref, out_ref, along_ref):
         px, py = lax.axis_index("px"), lax.axis_index("py")
         field = jnp.concatenate([state_ref[0, level] for level in range(levels)], 1)
-        rows = dot(left_ref[px], stacked(field))
-        width = 2 * ny
-        both = jnp.concatenate([rows[:low, i * width : (i + 1) * width] for i in range(half)], 0)
-        high, small = halves(both)
+        high, small = halves(field)
+        table = left_ref[px]
+        rows = dot(table, jnp.concatenate([high, high], 0)) + dot(table[:, :nx], small)
+        found = jnp.concatenate([rows[:low, i * ny : (i + 1) * ny] for i in range(levels)], 0)
+        high, small = halves(found)
         table = right_ref[py]
-        found = dot(high, table)
-        found = found[:, :ny] + found[:, ny:] + dot(small, table[:, :ny])
-        out_ref[:modes] = jnp.concatenate([found[i * low : i * low + modes] for i in range(half)], 1)
-        ends = jnp.concatenate([found[i * low + modes : (i + 1) * low] for i in range(half)], 1)
-        cells = jnp.concatenate([rows[modes:low, i * width : (i + 1) * width] for i in range(half)], 0)
-        cells = dot(jnp.concatenate(halves(cells), 0), corner_ref[py])
-        cells = cells[: half * EDGE] + cells[half * EDGE :]
-        cells = jnp.concatenate([cells[i * EDGE : (i + 1) * EDGE] for i in range(half)], 1)
+        found = dot(high, table) + dot(small, table)
+        both = found[:, :ny] + pltpu.roll(found[:, :ny], modes, 1)
+        left_lane = lax.broadcasted_iota(jnp.int32, (low, ny), 1) < modes
+        both = [both[i * low : (i + 1) * low] for i in range(levels)]
+        both = [jnp.where(left_lane, both[2 * i], both[2 * i + 1]) for i in range(half)]
+        both = jnp.concatenate(both, 1)
+        out_ref[:modes] = both[:modes]
+        ends = both[modes:]
+        cells = [found[i * low + modes : (i + 1) * low, ny:] for i in range(levels)]
+        cells = [cells[2 * i] + pltpu.roll(cells[2 * i + 1], modes, 1) for i in range(half)]
+        cells = jnp.concatenate(cells, 1)
         row = lax.broadcasted_iota(jnp.int32, (EDGE, lanes), 0)
         lane = lax.broadcasted_iota(jnp.int32, (EDGE, lanes), 1)
         cells = jnp.sum(jnp.where(lane % EDGE == row, cells, 0.0), 0, keepdims=True)
@@ -218,7 +222,7 @@
     return call(
         kernel,
         (shape_of(plan.rows, lanes), shape_of(plan.rows if halved else EDGE, lanes)),
-        state, left, jnp.asarray(np.stack(right)), jnp.asarray(np.stack(corner)), jnp.asarray(np.stack(edge)),
+        state, left, jnp.asarray(np.stack(right)), jnp.asarray(np.stack(edge)),
         jnp.asarray(bf16(pick)), rates,
         first=True,
     )
@@ -622,15 +626,16 @@
     halved = plan.py == 2 and plan.px == 4
     share, along = project(plan, initial_state, relax_rates, halved)
     if halved:
-        share, drive_modes, nest_offsets = lax.optimization_barrier((share, drive_modes, nest_offsets))
+        share = lax.optimization_barrier(share)
         from_y = swap(share, "py", lambda i: i ^ 1)
         from_x = swap(along, "px", lambda i: i ^ 1)
         from_both = swap(share, ("py", "px"), lambda i: i ^ (plan.px + 1))
-        prepared = prepare(plan, drive_modes, nest_offsets)
-        from_both, prepared = lax.optimization_barrier((from_both, prepared))
         total, halo = join_first(plan, share, from_y, from_x, from_both, initial_state)
         columns = from_y
+        total, drive_modes, nest_offsets = lax.optimization_barrier((total, drive_modes, nest_offsets))
         across = swap(total, "px", lambda i: i ^ 3)
+        prepared = prepare(plan, drive_modes, nest_offsets)
+        across, prepared = lax.optimization_barrier((across, prepared))
         last = join_last(plan, total, across)
     else:
         from_right = jnp.arange(EDGE)[:, None] < plan.windows

time: 26.9 us -> 26.9 us (level)
  transfers between devices with their start and end apart: 7 -> 7, of which waited for: 5 -> 6; matrix products, arithmetic and copies ran while one was open for 0% -> 0% of each run, Pallas kernels for 13% -> 13%
where the time goes in v8:
time: 26.9 us; the launch traced here: 26.7 us
  starting transfers between devices  9.31 us (35%)
  Pallas kernels  8.39 us (31%)
  waiting for transfers between devices  7.55 us (28%)
  between operations  0.78 us (3%)
  local copies, waits for them, and re-layouts  0.71 us (3%)
    ppermute x7, starting transfers between devices, swap(): lax.ppermute(value, axis, [(i, partner(i)) for i in range(size) if 0 <= p...  9.31 us
    pallas_call x7, Pallas kernels, call(): pl.pallas_call(kernel, in_specs=specs, out_specs=jax.tree.map(lambda _: p...  8.39 us
    ppermute x7, waiting for transfers between devices, swap(): lax.ppermute(value, axis, [(i, partner(i)) for i in range(size) if 0 <= p...  7.55 us
    unnamed x22, local copies, waits for them, and re-layouts  0.71 us
  transfers between devices with their start and end apart: 7, of which 6 were waited for; matrix products, arithmetic and copies ran while one was open for 0% of the time, Pallas kernels for 13%

profile of v8, /device:TPU:0, one launch (start us, length us, event | category | flops | bytes accessed | tf_op | source)
XLA Modules:
  0.0 26.7 jit_solution(8964919313842575097)
XLA Ops:
  0.6 0.0 copy-start
  0.6 1.6 %shard_map.212 = (f32[80,256]{1,0:T(8,128)S(1)}, f32[80,256]{1,0:T(8,128)S(1)}) custom-call(f32[1,4,64,128]{3,2,1,0:T(8,128)} %state_ref.5, bf16[4,80,128]{2,1,0:T(8,128)(2,1)} %constant.34.clone.left_ref, bf16[2,128,256]{2,1,0:T(8,128)(2,1)} %constant.35.clone.right_ref, bf16[2,16,256]{2,1,0:T(8,128)(2,1)} %constant.36.clone.edge_ref, ...), custom_call_target="tpu_custom_call" | custom-call | tf_op jit(solution)/shard_map/pallas_call | solution.py:120
  2.2 4.1 %collective-permute-start.2 = (f32[80,256]{1,0:T(8,128)S(1)}, f32[80,256]{1,0:T(8,128)S(1)}, u32[]{:S(2)}, u32[]{:S(2)}) collective-permute-start(f32[80,256]{1,0:T(8,128)S(1)} %get-tuple-element.22.own_ref), channel_id=1, source_target_pairs={{0,5},{1,4},{2,7},{3,6},{4,1},{5,0},{6,3},{7,2},{8,13},{9,12},{10,... | collective-permute-start | bytes 245768 | tf_op jit(solution)/shard_map/ppermute | solution.py:621
  6.3 0.5 %collective-permute-start = (f32[80,256]{1,0:T(8,128)S(1)}, f32[80,256]{1,0:T(8,128)S(1)}, u32[]{:S(2)}, u32[]{:S(2)}) collective-permute-start(f32[80,256]{1,0:T(8,128)S(1)} %get-tuple-element.22.own_ref), channel_id=1, source_target_pairs={{0,4},{4,0},{1,5},{5,1},{2,6},{6,2},{3,7},{7,3},{8,12},{12,8},{9,1... | collective-permute-start | bytes 245768 | tf_op jit(solution)/shard_map/ppermute | solution.py:621
  6.8 0.1 collective-permute-start.1
  6.9 1.9 %collective-permute-done.2.both_ref = f32[80,256]{1,0:T(8,128)S(1)} collective-permute-done((f32[80,256]{1,0:T(8,128)S(1)}, f32[80,256]{1,0:T(8,128)S(1)}, u32[]{:S(2)}, u32[]{:S(2)}) %collective-permute-start.2) | collective-permute-done | bytes 81952 | tf_op jit(solution)/shard_map/ppermute | solution.py:621
  8.9 1.9 %collective-permute-done.y_ref.columns_ref = f32[80,256]{1,0:T(8,128)S(1)} collective-permute-done((f32[80,256]{1,0:T(8,128)S(1)}, f32[80,256]{1,0:T(8,128)S(1)}, u32[]{:S(2)}, u32[]{:S(2)}) %collective-permute-start) | collective-permute-done | bytes 81952 | tf_op jit(solution)/shard_map/ppermute | solution.py:621
  10.7 0.5 %collective-permute-done.1.x_ref = f32[80,256]{1,0:T(8,128)S(1)} collective-permute-done((f32[80,256]{1,0:T(8,128)S(1)}, f32[80,256]{1,0:T(8,128)S(1)}, u32[]{:S(2)}, u32[]{:S(2)}) %collective-permute-start.1) | collective-permute-done | bytes 81952 | tf_op jit(solution)/shard_map/ppermute | solution.py:621
  11.2 0.0 copy-done
  11.2 0.2 shard_map.213
  11.5 3.0 %collective-permute-start.3 = (f32[80,256]{1,0:T(8,128)S(1)}, f32[80,256]{1,0:T(8,128)S(1)}, u32[]{:S(2)}, u32[]{:S(2)}) collective-permute-start(f32[80,256]{1,0:T(8,128)S(1)} %get-tuple-element.25.own_ref), channel_id=1, source_target_pairs={{0,3},{1,2},{2,1},{3,0},{4,7},{5,6},{6,5},{7,4},{8,11},{9,10},{10,... | collective-permute-start | bytes 245768 | tf_op jit(solution)/shard_map/ppermute | solution.py:621
  14.5 1.8 %shard_map.214 = (f32[3,64,256]{2,1,0:T(8,128)S(1)}, bf16[3,64,192]{2,1,0:T(8,128)(2,1)S(1)}, bf16[3,128,256]{2,1,0:T(8,128)(2,1)S(1)}, bf16[384,192]{1,0:T(8,128)(2,1)S(1)}, bf16[3,256,256]{2,1,0:T(8,128)(2,1)S(1)}) custom-call(f32[3,4,64,64]{3,2,1,0:T(8,128)} %drive_ref, f32[2,64,128]{2,1,0:T(8,128)} %constant.38.clone.maps_x_ref, ...), custom_call_target="tpu_custom_call" | custom-call | tf_op jit(solution)/shard_map/pallas_call | solution.py:120
  16.3 0.0 copy-start.3
  16.3 0.7 %copy-done.3 = bf16[3,128,256]{2,1,0:T(8,128)(2,1)} copy-done((bf16[3,128,256]{2,1,0:T(8,128)(2,1)}, bf16[3,128,256]{2,1,0:T(8,128)(2,1)S(1)}, u32[]{:S(2)}) %copy-start.3) | copy-done | bytes 196632
  16.9 0.8 %collective-permute-done.3.other_ref.second_ref = f32[80,256]{1,0:T(8,128)S(1)} collective-permute-done((f32[80,256]{1,0:T(8,128)S(1)}, f32[80,256]{1,0:T(8,128)S(1)}, u32[]{:S(2)}, u32[]{:S(2)}) %collective-permute-start.3) | collective-permute-done | bytes 81952 | tf_op jit(solution)/shard_map/ppermute | solution.py:621
  17.7 0.0 copy-start.10
  17.7 1.6 %collective-permute-start.4 = (f32[80,256]{1,0:T(8,128)S(1)}, f32[80,256]{1,0:T(8,128)S(1)}, u32[]{:S(2)}, u32[]{:S(2)}) collective-permute-start(f32[80,256]{1,0:T(8,128)S(1)} %shard_map.215.refs_0_), channel_id=1, source_target_pairs={{0,16},{8,24},{16,0},{24,8},{1,17},{9,25},{17,1},{25,9},{2,18},{10... | collective-permute-start | bytes 245768 | tf_op jit(solution)/shard_map/ppermute | solution.py:621
  19.3 0.0 collective-permute-start.5
  19.3 0.0 copy-done.10
  19.3 0.0 copy-start.1
  19.3 0.0 copy-start.2
  19.3 0.0 copy-start.5
  19.3 0.0 copy-start.7
  19.3 0.0 copy-start.9
  19.3 1.0 %shard_map.216.stepped_ref = f32[4,64,128]{2,1,0:T(8,128)S(1)} custom-call(f32[1,4,64,128]{3,2,1,0:T(8,128)S(1)} %copy-done, f32[80,256]{1,0:T(8,128)S(1)} %collective-permute-done.y_ref.columns_ref, f32[8,256]{1,0:T(8,128)S(1)} %get-tuple-element.34.first_ref, f32[80,256]{1,0:T(8,128)S(1)} %collective-permute-done.3.other_ref.second_ref, ...), custom_call_target="tpu_custom_call" | custom-call | tf_op jit(solution)/shard_map/pallas_call | solution.py:120
  20.3 0.0 copy-start.4
  20.3 0.0 copy-start.6
  20.3 0.0 copy-start.8
  20.3 1.9 %collective-permute-done.4.refs_1_ = f32[80,256]{1,0:T(8,128)S(1)} collective-permute-done((f32[80,256]{1,0:T(8,128)S(1)}, f32[80,256]{1,0:T(8,128)S(1)}, u32[]{:S(2)}, u32[]{:S(2)}) %collective-permute-start.4) | collective-permute-done | bytes 81952 | tf_op jit(solution)/shard_map/ppermute | solution.py:621
  22.2 0.0 collective-permute-start.6
  22.2 0.0 collective-permute-done.5.refs_2_
  22.2 0.0 copy-done.1
  22.3 0.0 copy-done.2
  22.3 0.0 copy-done.5
  22.3 0.0 copy-done.7
  22.3 0.0 copy-done.9
  22.3 0.6 %shard_map.217.early_ref = f32[3,3,64,256]{3,2,1,0:T(8,128)S(1)} custom-call(f32[80,256]{1,0:T(8,128)S(1)} %shard_map.215.refs_0_, f32[80,256]{1,0:T(8,128)S(1)} %collective-permute-done.4.refs_1_, f32[80,256]{1,0:T(8,128)S(1)} %collective-permute-done.5.refs_2_, bf16[32,384]{1,0:T(8,128)(2,1)S(1)} %copy-done.7, bf16[256,384]{1,0:T(8,128)(2,1)S(1)} %copy-done.1, ...), custom_call_target="tpu_custom_call" | custom-call | tf_op jit(solution)/shard_map/pallas_call | solution.py:120
  22.9 0.6 %collective-permute-done.6.refs_3_ = f32[80,256]{1,0:T(8,128)S(1)} collective-permute-done((f32[80,256]{1,0:T(8,128)S(1)}, f32[80,256]{1,0:T(8,128)S(1)}, u32[]{:S(2)}, u32[]{:S(2)}) %collective-permute-start.6) | collective-permute-done | bytes 81952 | tf_op jit(solution)/shard_map/ppermute | solution.py:621
  23.5 0.0 copy-done.4
  23.5 0.0 copy-done.6
  23.5 0.0 copy-done.8
  23.5 3.2 %shard_map.218 = (f32[1,4,64,128]{3,2,1,0:T(8,128)}, f32[1,4,64,64]{3,2,1,0:T(8,128)}) custom-call(f32[4,64,128]{2,1,0:T(8,128)S(1)} %shard_map.216.stepped_ref, f32[3,64,256]{2,1,0:T(8,128)S(1)} %get-tuple-element.36.drive_ref, bf16[3,64,192]{2,1,0:T(8,128)(2,1)S(1)} %get-tuple-element.37.row_ref, bf16[3,128,256]{2,1,0:T(8,128)(2,1)S(1)} %copy-done.4, ...), custom_call_target="tpu_custom_call" | custom-call | tf_op jit(solution)/shard_map/pallas_call | solution.py:120
  (1 shorter events, 0.0 us)
Async XLA Ops:
  0.6 10.6 %copy-start = (f32[1,4,64,128]{3,2,1,0:T(8,128)S(1)}, f32[1,4,64,128]{3,2,1,0:T(8,128)}, u32[]{:S(2)}) copy-start(f32[1,4,64,128]{3,2,1,0:T(8,128)} %state_ref.5) | copy-start | bytes 393220
  2.2 6.7 %collective-permute-start.2 = (f32[80,256]{1,0:T(8,128)S(1)}, f32[80,256]{1,0:T(8,128)S(1)}, u32[]{:S(2)}, u32[]{:S(2)}) collective-permute-start(f32[80,256]{1,0:T(8,128)S(1)} %get-tuple-element.22.own_ref), channel_id=1, source_target_pairs={{0,5},{1,4},{2,7},{3,6},{4,1},{5,0},{6,3},{7,2},{8,13},{9,12},{10,... | collective-permute-start | bytes 245768 | tf_op jit(solution)/shard_map/ppermute | solution.py:621
  6.3 4.4 %collective-permute-start = (f32[80,256]{1,0:T(8,128)S(1)}, f32[80,256]{1,0:T(8,128)S(1)}, u32[]{:S(2)}, u32[]{:S(2)}) collective-permute-start(f32[80,256]{1,0:T(8,128)S(1)} %get-tuple-element.22.own_ref), channel_id=1, source_target_pairs={{0,4},{4,0},{1,5},{5,1},{2,6},{6,2},{3,7},{7,3},{8,12},{12,8},{9,1... | collective-permute-start | bytes 245768 | tf_op jit(solution)/shard_map/ppermute | solution.py:621
  6.8 4.4 %collective-permute-start.1 = (f32[80,256]{1,0:T(8,128)S(1)}, f32[80,256]{1,0:T(8,128)S(1)}, u32[]{:S(2)}, u32[]{:S(2)}) collective-permute-start(f32[80,256]{1,0:T(8,128)S(1)} %get-tuple-element.23), channel_id=1, source_target_pairs={{0,1},{1,0},{2,3},{3,2},{4,5},{5,4},{6,7},{7,6},{8,9},{9,8},{10,11... | collective-permute-start | bytes 245768 | tf_op jit(solution)/shard_map/ppermute | solution.py:621
  11.5 6.3 %collective-permute-start.3 = (f32[80,256]{1,0:T(8,128)S(1)}, f32[80,256]{1,0:T(8,128)S(1)}, u32[]{:S(2)}, u32[]{:S(2)}) collective-permute-start(f32[80,256]{1,0:T(8,128)S(1)} %get-tuple-element.25.own_ref), channel_id=1, source_target_pairs={{0,3},{1,2},{2,1},{3,0},{4,7},{5,6},{6,5},{7,4},{8,11},{9,10},{10,... | collective-permute-start | bytes 245768 | tf_op jit(solution)/shard_map/ppermute | solution.py:621
  16.3 0.7 %copy-start.3 = (bf16[3,128,256]{2,1,0:T(8,128)(2,1)}, bf16[3,128,256]{2,1,0:T(8,128)(2,1)S(1)}, u32[]{:S(2)}) copy-start(bf16[3,128,256]{2,1,0:T(8,128)(2,1)S(1)} %get-tuple-element.38.col_ref) | copy-start | bytes 589828
  17.7 1.6 %copy-start.10 = (bf16[32,128]{1,0:T(8,128)(2,1)S(1)}, bf16[32,128]{1,0:T(8,128)(2,1)}, u32[]{:S(2)}) copy-start(bf16[32,128]{1,0:T(8,128)(2,1)} %constant.42.clone.place_ref) | copy-start | bytes 24580
  17.7 4.5 %collective-permute-start.4 = (f32[80,256]{1,0:T(8,128)S(1)}, f32[80,256]{1,0:T(8,128)S(1)}, u32[]{:S(2)}, u32[]{:S(2)}) collective-permute-start(f32[80,256]{1,0:T(8,128)S(1)} %shard_map.215.refs_0_), channel_id=1, source_target_pairs={{0,16},{8,24},{16,0},{24,8},{1,17},{9,25},{17,1},{25,9},{2,18},{10... | collective-permute-start | bytes 245768 | tf_op jit(solution)/shard_map/ppermute | solution.py:621
  19.3 3.0 %collective-permute-start.5 = (f32[80,256]{1,0:T(8,128)S(1)}, f32[80,256]{1,0:T(8,128)S(1)}, u32[]{:S(2)}, u32[]{:S(2)}) collective-permute-start(f32[80,256]{1,0:T(8,128)S(1)} %shard_map.215.refs_0_), channel_id=1, source_target_pairs={{0,8},{8,0},{16,24},{24,16},{1,9},{9,1},{17,25},{25,17},{2,10},{10... | collective-permute-start | bytes 245768 | tf_op jit(solution)/shard_map/ppermute | solution.py:621
  19.3 3.0 %copy-start.1 = (bf16[256,384]{1,0:T(8,128)(2,1)S(1)}, bf16[256,384]{1,0:T(8,128)(2,1)}, u32[]{:S(2)}) copy-start(bf16[256,384]{1,0:T(8,128)(2,1)} %constant.44.clone.refs_4_.refs_5_) | copy-start | bytes 589828
  19.3 3.0 %copy-start.2 = (f32[64,256]{1,0:T(8,128)S(1)}, f32[64,256]{1,0:T(8,128)}, u32[]{:S(2)}) copy-start(f32[64,256]{1,0:T(8,128)} %constant.46.clone.refs_6_.refs_7_) | copy-start | bytes 196612
  19.3 3.0 %copy-start.5 = (bf16[192,96]{1,0:T(8,128)(2,1)S(1)}, bf16[192,96]{1,0:T(8,128)(2,1)}, u32[]{:S(2)}) copy-start(bf16[192,96]{1,0:T(8,128)(2,1)} %constant.45.clone.refs_5_.refs_6_) | copy-start | bytes 110596
  19.3 3.0 %copy-start.7 = (bf16[32,384]{1,0:T(8,128)(2,1)S(1)}, bf16[32,384]{1,0:T(8,128)(2,1)}, u32[]{:S(2)}) copy-start(bf16[32,384]{1,0:T(8,128)(2,1)} %constant.43.clone.refs_3_.refs_4_) | copy-start | bytes 73732
  19.3 3.0 %copy-start.9 = (f32[8,256]{1,0:T(8,128)S(1)}, f32[8,256]{1,0:T(8,128)}, u32[]{:S(2)}) copy-start(f32[8,256]{1,0:T(8,128)} %constant.47.clone.refs_7_.refs_8_) | copy-start | bytes 24580
  20.3 3.2 %copy-start.4 = (bf16[3,128,256]{2,1,0:T(8,128)(2,1)S(1)}, bf16[3,128,256]{2,1,0:T(8,128)(2,1)}, u32[]{:S(2)}) copy-start(bf16[3,128,256]{2,1,0:T(8,128)(2,1)} %copy-done.3) | copy-start | bytes 589828
  20.3 3.2 %copy-start.6 = (bf16[2,128,256]{2,1,0:T(8,128)(2,1)S(1)}, bf16[2,128,256]{2,1,0:T(8,128)(2,1)}, u32[]{:S(2)}) copy-start(bf16[2,128,256]{2,1,0:T(8,128)(2,1)} %constant.55.sideways_ref) | copy-start | bytes 393220
  20.3 3.2 %copy-start.8 = (bf16[128,192]{1,0:T(8,128)(2,1)S(1)}, bf16[128,192]{1,0:T(8,128)(2,1)}, u32[]{:S(2)}) copy-start(bf16[128,192]{1,0:T(8,128)(2,1)} %constant.48.clone.again_ref) | copy-start | bytes 147460
  22.2 1.3 %collective-permute-start.6 = (f32[80,256]{1,0:T(8,128)S(1)}, f32[80,256]{1,0:T(8,128)S(1)}, u32[]{:S(2)}, u32[]{:S(2)}) collective-permute-start(f32[80,256]{1,0:T(8,128)S(1)} %collective-permute-done.4.refs_1_), channel_id=1, source_target_pairs={{0,8},{8,0},{16,24},{24,16},{1,9},{9,1},{17,25},{25,17},{2,10},{10... | collective-permute-start | bytes 245768 | tf_op jit(solution)/shard_map/ppermute | solution.py:621

commit v9 on v8

--- a/solution.py
+++ b/solution.py
@@ -434,20 +434,14 @@
                 at = (sum(range(p + 1)) + j) * nx
                 spread_x_out[at : at + nx] = as_left(combined)
         for j in range(windows):
-            table = rows_y_ref[py, j]
-            blank = jnp.zeros_like(table)
-            table = jnp.concatenate(
-                [jnp.concatenate([table, blank], 1), jnp.concatenate([blank, table], 1)], 0
-            )
-            high, small = halves(table)
-            spread_y_out[j] = jnp.concatenate([high, small], 0)
+            spread_y_out[j] = jnp.concatenate(halves(rows_y_ref[py, j]), 0)
 
     shapes = (
         shape_of(windows, modes, lanes),
         shape_of(steps, modes, 3 * modes, kind=jnp.bfloat16),
         shape_of(steps, 2 * modes, 4 * modes, kind=jnp.bfloat16),
         shape_of(sum(range(windows + 1)) * nx, 3 * modes, kind=jnp.bfloat16),
-        shape_of(windows, 4 * modes, 2 * ny, kind=jnp.bfloat16),
+        shape_of(windows, 2 * modes, ny, kind=jnp.bfloat16),
     )
     return call(kernel, shapes, drive, maps_x, maps_y, f32(rows_x), f32(rows_y), nest_offsets.T, first=True)
 
@@ -601,8 +595,12 @@
                 spread[j] = spread[j] + found[j * nx : (j + 1) * nx]
         field = 0.0
         for j in range(windows):
-            table = spread_y_ref[j]
-            part = by_parts(pairs(spread[j]), table[: 2 * modes], table[2 * modes :])
+            table, blank = spread_y_ref[j], jnp.zeros((modes, ny), jnp.bfloat16)
+            both = [
+                jnp.concatenate([jnp.concatenate([t, blank], 1), jnp.concatenate([blank, t], 1)], 0)
+                for t in (table[:modes], table[modes:])
+            ]
+            part = by_parts(pairs(spread[j]), *both)
             field = field + part
         for level in range(levels):
             at_row, at = level // 2 * nx, level % 2 * ny
@@ -626,16 +624,15 @@
     halved = plan.py == 2 and plan.px == 4
     share, along = project(plan, initial_state, relax_rates, halved)
     if halved:
-        share = lax.optimization_barrier(share)
+        share, drive_modes, nest_offsets = lax.optimization_barrier((share, drive_modes, nest_offsets))
         from_y = swap(share, "py", lambda i: i ^ 1)
         from_x = swap(along, "px", lambda i: i ^ 1)
         from_both = swap(share, ("py", "px"), lambda i: i ^ (plan.px + 1))
+        prepared = prepare(plan, drive_modes, nest_offsets)
+        from_both, prepared = lax.optimization_barrier((from_both, prepared))
         total, halo = join_first(plan, share, from_y, from_x, from_both, initial_state)
         columns = from_y
-        total, drive_modes, nest_offsets = lax.optimization_barrier((total, drive_modes, nest_offsets))
         across = swap(total, "px", lambda i: i ^ 3)
-        prepared = prepare(plan, drive_modes, nest_offsets)
-        across, prepared = lax.optimization_barrier((across, prepared))
         last = join_last(plan, total, across)
     else:
         from_right = jnp.arange(EDGE)[:, None] < plan.windows
@@ -655,7 +652,7 @@
         chip = swap(last, "nest", lambda i: i ^ 2)
         stepped = step_patch(plan, initial_state, columns, halo, across)
         chip, stepped = lax.optimization_barrier((chip, stepped))
-        gathered = [last, chip, core, swap(chip, "nest", lambda i: i ^ 1)]
+        gathered = [last, chip, core, swap(last, "nest", lambda i: i ^ 3)]
     else:
         gathered = [last] + [swap(last, "nest", lambda i, s=s: i + s) for s in range(1, plan.nest)]
         stepped = step_patch(plan, initial_state, columns, halo, across)

time: 26.9 us -> 26.7 us (level)
  local copies, waits for them, and re-layouts: 0.71 us -> 0.05 us
  starting transfers between devices: 9.31 us -> 9.96 us
    unnamed x22 -> x18, local copies, waits for them, and re-layouts: 0.71 us -> 0.05 us
    ppermute x7, starting transfers between devices: 9.31 us -> 9.96 us  [swap(): lax.ppermute(value, axis, [(i, partner(i)) for i in range(size) if 0 <= p...]
where the time goes in v9:
time: 26.7 us; the launch traced here: 26.5 us
  starting transfers between devices  9.96 us (37%)
  Pallas kernels  8.37 us (31%)
  waiting for transfers between devices  7.41 us (28%)
  between operations  0.73 us (3%)
    ppermute x7, starting transfers between devices, swap(): lax.ppermute(value, axis, [(i, partner(i)) for i in range(size) if 0 <= p...  9.96 us
    pallas_call x7, Pallas kernels, call(): pl.pallas_call(kernel, in_specs=specs, out_specs=jax.tree.map(lambda _: p...  8.37 us
    ppermute x7, waiting for transfers between devices, swap(): lax.ppermute(value, axis, [(i, partner(i)) for i in range(size) if 0 <= p...  7.41 us
  transfers between devices with their start and end apart: 7, of which 6 were waited for; matrix products, arithmetic and copies ran while one was open for 0% of the time, Pallas kernels for 13%

profile of v9, /device:TPU:0, one launch (start us, length us, event | category | flops | bytes accessed | tf_op | source)
XLA Modules:
  0.0 26.5 jit_solution(12543407310101546107)
XLA Ops:
  0.6 1.5 %shard_map.212 = (f32[80,256]{1,0:T(8,128)S(1)}, f32[80,256]{1,0:T(8,128)S(1)}) custom-call(f32[1,4,64,128]{3,2,1,0:T(8,128)} %state_ref.5, bf16[4,80,128]{2,1,0:T(8,128)(2,1)} %constant.34.clone.left_ref, bf16[2,128,256]{2,1,0:T(8,128)(2,1)} %constant.35.clone.right_ref, bf16[2,16,256]{2,1,0:T(8,128)(2,1)} %constant.36.clone.edge_ref, ...), custom_call_target="tpu_custom_call" | custom-call | tf_op jit(solution)/shard_map/pallas_call | solution.py:120
  2.2 4.1 %collective-permute-start.2 = (f32[80,256]{1,0:T(8,128)S(1)}, f32[80,256]{1,0:T(8,128)S(1)}, u32[]{:S(2)}, u32[]{:S(2)}) collective-permute-start(f32[80,256]{1,0:T(8,128)S(1)} %get-tuple-element.23.own_ref), channel_id=1, source_target_pairs={{0,5},{1,4},{2,7},{3,6},{4,1},{5,0},{6,3},{7,2},{8,13},{9,12},{10,... | collective-permute-start | bytes 245768 | tf_op jit(solution)/shard_map/ppermute | solution.py:619
  6.2 0.5 %collective-permute-start = (f32[80,256]{1,0:T(8,128)S(1)}, f32[80,256]{1,0:T(8,128)S(1)}, u32[]{:S(2)}, u32[]{:S(2)}) collective-permute-start(f32[80,256]{1,0:T(8,128)S(1)} %get-tuple-element.23.own_ref), channel_id=1, source_target_pairs={{0,4},{4,0},{1,5},{5,1},{2,6},{6,2},{3,7},{7,3},{8,12},{12,8},{9,1... | collective-permute-start | bytes 245768 | tf_op jit(solution)/shard_map/ppermute | solution.py:619
  6.7 0.1 collective-permute-start.1
  6.9 0.0 copy-start
  6.9 1.8 %shard_map.213 = (f32[3,64,256]{2,1,0:T(8,128)S(1)}, bf16[3,64,192]{2,1,0:T(8,128)(2,1)S(1)}, bf16[3,128,256]{2,1,0:T(8,128)(2,1)S(1)}, bf16[384,192]{1,0:T(8,128)(2,1)S(1)}, bf16[3,128,128]{2,1,0:T(8,128)(2,1)S(1)}) custom-call(f32[3,4,64,64]{3,2,1,0:T(8,128)} %drive_ref, f32[2,64,128]{2,1,0:T(8,128)} %constant.38.clone.maps_x_ref, ...), custom_call_target="tpu_custom_call" | custom-call | tf_op jit(solution)/shard_map/pallas_call | solution.py:120
  8.7 0.1 collective-permute-done.2.both_ref
  8.8 1.9 %collective-permute-done.y_ref.columns_ref = f32[80,256]{1,0:T(8,128)S(1)} collective-permute-done((f32[80,256]{1,0:T(8,128)S(1)}, f32[80,256]{1,0:T(8,128)S(1)}, u32[]{:S(2)}, u32[]{:S(2)}) %collective-permute-start) | collective-permute-done | bytes 81952 | tf_op jit(solution)/shard_map/ppermute | solution.py:619
  10.7 0.5 %collective-permute-done.1.x_ref = f32[80,256]{1,0:T(8,128)S(1)} collective-permute-done((f32[80,256]{1,0:T(8,128)S(1)}, f32[80,256]{1,0:T(8,128)S(1)}, u32[]{:S(2)}, u32[]{:S(2)}) %collective-permute-start.1) | collective-permute-done | bytes 81952 | tf_op jit(solution)/shard_map/ppermute | solution.py:619
  11.2 0.0 copy-done
  11.2 0.2 shard_map.214
  11.4 0.0 copy-start.8
  11.4 3.0 %collective-permute-start.3 = (f32[80,256]{1,0:T(8,128)S(1)}, f32[80,256]{1,0:T(8,128)S(1)}, u32[]{:S(2)}, u32[]{:S(2)}) collective-permute-start(f32[80,256]{1,0:T(8,128)S(1)} %get-tuple-element.33.own_ref), channel_id=1, source_target_pairs={{0,3},{1,2},{2,1},{3,0},{4,7},{5,6},{6,5},{7,4},{8,11},{9,10},{10,... | collective-permute-start | bytes 245768 | tf_op jit(solution)/shard_map/ppermute | solution.py:619
  14.5 3.2 %collective-permute-done.3.other_ref.second_ref = f32[80,256]{1,0:T(8,128)S(1)} collective-permute-done((f32[80,256]{1,0:T(8,128)S(1)}, f32[80,256]{1,0:T(8,128)S(1)}, u32[]{:S(2)}, u32[]{:S(2)}) %collective-permute-start.3) | collective-permute-done | bytes 81952 | tf_op jit(solution)/shard_map/ppermute | solution.py:619
  17.7 1.6 %collective-permute-start.4 = (f32[80,256]{1,0:T(8,128)S(1)}, f32[80,256]{1,0:T(8,128)S(1)}, u32[]{:S(2)}, u32[]{:S(2)}) collective-permute-start(f32[80,256]{1,0:T(8,128)S(1)} %shard_map.215.refs_0_), channel_id=1, source_target_pairs={{0,16},{8,24},{16,0},{24,8},{1,17},{9,25},{17,1},{25,9},{2,18},{10... | collective-permute-start | bytes 245768 | tf_op jit(solution)/shard_map/ppermute | solution.py:619
  19.3 0.0 collective-permute-start.5
  19.3 0.6 %collective-permute-start.6 = (f32[80,256]{1,0:T(8,128)S(1)}, f32[80,256]{1,0:T(8,128)S(1)}, u32[]{:S(2)}, u32[]{:S(2)}) collective-permute-start(f32[80,256]{1,0:T(8,128)S(1)} %shard_map.215.refs_0_), channel_id=1, source_target_pairs={{0,24},{8,16},{16,8},{24,0},{1,25},{9,17},{17,9},{25,1},{2,26},{10... | collective-permute-start | bytes 245768 | tf_op jit(solution)/shard_map/ppermute | solution.py:619
  19.9 0.0 copy-done.8
  19.9 0.0 copy-start.1
  19.9 0.0 copy-start.2
  19.9 0.0 copy-start.3
  19.9 0.0 copy-start.5
  19.9 0.0 copy-start.7
  19.9 1.0 %shard_map.216.stepped_ref = f32[4,64,128]{2,1,0:T(8,128)S(1)} custom-call(f32[1,4,64,128]{3,2,1,0:T(8,128)S(1)} %copy-done, f32[80,256]{1,0:T(8,128)S(1)} %collective-permute-done.y_ref.columns_ref, f32[8,256]{1,0:T(8,128)S(1)} %get-tuple-element.34.first_ref, f32[80,256]{1,0:T(8,128)S(1)} %collective-permute-done.3.other_ref.second_ref, ...), custom_call_target="tpu_custom_call" | custom-call | tf_op jit(solution)/shard_map/pallas_call | solution.py:120
  20.9 0.0 copy-start.4
  20.9 0.0 copy-start.6
  20.9 1.3 %collective-permute-done.4.refs_1_ = f32[80,256]{1,0:T(8,128)S(1)} collective-permute-done((f32[80,256]{1,0:T(8,128)S(1)}, f32[80,256]{1,0:T(8,128)S(1)}, u32[]{:S(2)}, u32[]{:S(2)}) %collective-permute-start.4) | collective-permute-done | bytes 81952 | tf_op jit(solution)/shard_map/ppermute | solution.py:619
  22.2 0.0 collective-permute-done.5.refs_2_
  22.2 0.0 copy-done.1
  22.2 0.0 copy-done.2
  22.2 0.0 copy-done.3
  22.2 0.0 copy-done.5
  22.2 0.0 copy-done.7
  22.2 0.6 %shard_map.217.early_ref = f32[3,3,64,256]{3,2,1,0:T(8,128)S(1)} custom-call(f32[80,256]{1,0:T(8,128)S(1)} %shard_map.215.refs_0_, f32[80,256]{1,0:T(8,128)S(1)} %collective-permute-done.4.refs_1_, f32[80,256]{1,0:T(8,128)S(1)} %collective-permute-done.5.refs_2_, bf16[32,384]{1,0:T(8,128)(2,1)S(1)} %copy-done.5, bf16[256,384]{1,0:T(8,128)(2,1)S(1)} %copy-done.1, ...), custom_call_target="tpu_custom_call" | custom-call | tf_op jit(solution)/shard_map/pallas_call | solution.py:120
  22.9 0.4 %collective-permute-done.6.refs_3_ = f32[80,256]{1,0:T(8,128)S(1)} collective-permute-done((f32[80,256]{1,0:T(8,128)S(1)}, f32[80,256]{1,0:T(8,128)S(1)}, u32[]{:S(2)}, u32[]{:S(2)}) %collective-permute-start.6) | collective-permute-done | bytes 81952 | tf_op jit(solution)/shard_map/ppermute | solution.py:619
  23.3 0.0 copy-done.4
  23.3 0.0 copy-done.6
  23.3 3.2 %shard_map.218 = (f32[1,4,64,128]{3,2,1,0:T(8,128)}, f32[1,4,64,64]{3,2,1,0:T(8,128)}) custom-call(f32[4,64,128]{2,1,0:T(8,128)S(1)} %shard_map.216.stepped_ref, f32[3,64,256]{2,1,0:T(8,128)S(1)} %get-tuple-element.36.drive_ref, bf16[3,64,192]{2,1,0:T(8,128)(2,1)S(1)} %get-tuple-element.37.row_ref, bf16[3,128,256]{2,1,0:T(8,128)(2,1)S(1)} %get-tuple-element.38.col_ref, ...), custom_call_target="tpu_custom_call" | custom-call | tf_op jit(solution)/shard_map/pallas_call | solution.py:120
  (1 shorter events, 0.0 us)
Async XLA Ops:
  2.2 6.7 %collective-permute-start.2 = (f32[80,256]{1,0:T(8,128)S(1)}, f32[80,256]{1,0:T(8,128)S(1)}, u32[]{:S(2)}, u32[]{:S(2)}) collective-permute-start(f32[80,256]{1,0:T(8,128)S(1)} %get-tuple-element.23.own_ref), channel_id=1, source_target_pairs={{0,5},{1,4},{2,7},{3,6},{4,1},{5,0},{6,3},{7,2},{8,13},{9,12},{10,... | collective-permute-start | bytes 245768 | tf_op jit(solution)/shard_map/ppermute | solution.py:619
  6.2 4.4 %collective-permute-start = (f32[80,256]{1,0:T(8,128)S(1)}, f32[80,256]{1,0:T(8,128)S(1)}, u32[]{:S(2)}, u32[]{:S(2)}) collective-permute-start(f32[80,256]{1,0:T(8,128)S(1)} %get-tuple-element.23.own_ref), channel_id=1, source_target_pairs={{0,4},{4,0},{1,5},{5,1},{2,6},{6,2},{3,7},{7,3},{8,12},{12,8},{9,1... | collective-permute-start | bytes 245768 | tf_op jit(solution)/shard_map/ppermute | solution.py:619
  6.7 4.4 %collective-permute-start.1 = (f32[80,256]{1,0:T(8,128)S(1)}, f32[80,256]{1,0:T(8,128)S(1)}, u32[]{:S(2)}, u32[]{:S(2)}) collective-permute-start(f32[80,256]{1,0:T(8,128)S(1)} %get-tuple-element.24), channel_id=1, source_target_pairs={{0,1},{1,0},{2,3},{3,2},{4,5},{5,4},{6,7},{7,6},{8,9},{9,8},{10,11... | collective-permute-start | bytes 245768 | tf_op jit(solution)/shard_map/ppermute | solution.py:619
  6.9 4.3 %copy-start = (f32[1,4,64,128]{3,2,1,0:T(8,128)S(1)}, f32[1,4,64,128]{3,2,1,0:T(8,128)}, u32[]{:S(2)}) copy-start(f32[1,4,64,128]{3,2,1,0:T(8,128)} %state_ref.5) | copy-start | bytes 393220
  11.4 8.5 %copy-start.8 = (bf16[32,128]{1,0:T(8,128)(2,1)S(1)}, bf16[32,128]{1,0:T(8,128)(2,1)}, u32[]{:S(2)}) copy-start(bf16[32,128]{1,0:T(8,128)(2,1)} %constant.42.clone.place_ref) | copy-start | bytes 24580
  11.4 6.3 %collective-permute-start.3 = (f32[80,256]{1,0:T(8,128)S(1)}, f32[80,256]{1,0:T(8,128)S(1)}, u32[]{:S(2)}, u32[]{:S(2)}) collective-permute-start(f32[80,256]{1,0:T(8,128)S(1)} %get-tuple-element.33.own_ref), channel_id=1, source_target_pairs={{0,3},{1,2},{2,1},{3,0},{4,7},{5,6},{6,5},{7,4},{8,11},{9,10},{10,... | collective-permute-start | bytes 245768 | tf_op jit(solution)/shard_map/ppermute | solution.py:619
  17.7 4.5 %collective-permute-start.4 = (f32[80,256]{1,0:T(8,128)S(1)}, f32[80,256]{1,0:T(8,128)S(1)}, u32[]{:S(2)}, u32[]{:S(2)}) collective-permute-start(f32[80,256]{1,0:T(8,128)S(1)} %shard_map.215.refs_0_), channel_id=1, source_target_pairs={{0,16},{8,24},{16,0},{24,8},{1,17},{9,25},{17,1},{25,9},{2,18},{10... | collective-permute-start | bytes 245768 | tf_op jit(solution)/shard_map/ppermute | solution.py:619
  19.3 3.0 %collective-permute-start.5 = (f32[80,256]{1,0:T(8,128)S(1)}, f32[80,256]{1,0:T(8,128)S(1)}, u32[]{:S(2)}, u32[]{:S(2)}) collective-permute-start(f32[80,256]{1,0:T(8,128)S(1)} %shard_map.215.refs_0_), channel_id=1, source_target_pairs={{0,8},{8,0},{16,24},{24,16},{1,9},{9,1},{17,25},{25,17},{2,10},{10... | collective-permute-start | bytes 245768 | tf_op jit(solution)/shard_map/ppermute | solution.py:619
  19.3 4.1 %collective-permute-start.6 = (f32[80,256]{1,0:T(8,128)S(1)}, f32[80,256]{1,0:T(8,128)S(1)}, u32[]{:S(2)}, u32[]{:S(2)}) collective-permute-start(f32[80,256]{1,0:T(8,128)S(1)} %shard_map.215.refs_0_), channel_id=1, source_target_pairs={{0,24},{8,16},{16,8},{24,0},{1,25},{9,17},{17,9},{25,1},{2,26},{10... | collective-permute-start | bytes 245768 | tf_op jit(solution)/shard_map/ppermute | solution.py:619
  19.9 2.3 %copy-start.1 = (bf16[256,384]{1,0:T(8,128)(2,1)S(1)}, bf16[256,384]{1,0:T(8,128)(2,1)}, u32[]{:S(2)}) copy-start(bf16[256,384]{1,0:T(8,128)(2,1)} %constant.44.clone.refs_4_.refs_5_) | copy-start | bytes 589828
  19.9 2.3 %copy-start.2 = (f32[64,256]{1,0:T(8,128)S(1)}, f32[64,256]{1,0:T(8,128)}, u32[]{:S(2)}) copy-start(f32[64,256]{1,0:T(8,128)} %constant.46.clone.refs_6_.refs_7_) | copy-start | bytes 196612
  19.9 2.3 %copy-start.3 = (bf16[192,96]{1,0:T(8,128)(2,1)S(1)}, bf16[192,96]{1,0:T(8,128)(2,1)}, u32[]{:S(2)}) copy-start(bf16[192,96]{1,0:T(8,128)(2,1)} %constant.45.clone.refs_5_.refs_6_) | copy-start | bytes 110596
  19.9 2.3 %copy-start.5 = (bf16[32,384]{1,0:T(8,128)(2,1)S(1)}, bf16[32,384]{1,0:T(8,128)(2,1)}, u32[]{:S(2)}) copy-start(bf16[32,384]{1,0:T(8,128)(2,1)} %constant.43.clone.refs_3_.refs_4_) | copy-start | bytes 73732
  19.9 2.3 %copy-start.7 = (f32[8,256]{1,0:T(8,128)S(1)}, f32[8,256]{1,0:T(8,128)}, u32[]{:S(2)}) copy-start(f32[8,256]{1,0:T(8,128)} %constant.47.clone.refs_7_.refs_8_) | copy-start | bytes 24580
  20.9 2.4 %copy-start.4 = (bf16[2,128,256]{2,1,0:T(8,128)(2,1)S(1)}, bf16[2,128,256]{2,1,0:T(8,128)(2,1)}, u32[]{:S(2)}) copy-start(bf16[2,128,256]{2,1,0:T(8,128)(2,1)} %constant.55.sideways_ref) | copy-start | bytes 393220
  20.9 2.4 %copy-start.6 = (bf16[128,192]{1,0:T(8,128)(2,1)S(1)}, bf16[128,192]{1,0:T(8,128)(2,1)}, u32[]{:S(2)}) copy-start(bf16[128,192]{1,0:T(8,128)(2,1)} %constant.48.clone.again_ref) | copy-start | bytes 147460

commit v10 on v9

--- a/solution.py
+++ b/solution.py
@@ -624,15 +624,16 @@
     halved = plan.py == 2 and plan.px == 4
     share, along = project(plan, initial_state, relax_rates, halved)
     if halved:
-        share, drive_modes, nest_offsets = lax.optimization_barrier((share, drive_modes, nest_offsets))
+        share = lax.optimization_barrier(share)
         from_y = swap(share, "py", lambda i: i ^ 1)
         from_x = swap(along, "px", lambda i: i ^ 1)
         from_both = swap(share, ("py", "px"), lambda i: i ^ (plan.px + 1))
-        prepared = prepare(plan, drive_modes, nest_offsets)
-        from_both, prepared = lax.optimization_barrier((from_both, prepared))
         total, halo = join_first(plan, share, from_y, from_x, from_both, initial_state)
         columns = from_y
+        total, drive_modes, nest_offsets = lax.optimization_barrier((total, drive_modes, nest_offsets))
         across = swap(total, "px", lambda i: i ^ 3)
+        prepared = prepare(plan, drive_modes, nest_offsets)
+        across, prepared = lax.optimization_barrier((across, prepared))
         last = join_last(plan, total, across)
     else:
         from_right = jnp.arange(EDGE)[:, None] < plan.windows

time: 26.7 us -> 26.7 us (level)
  no operation moved by 1% of the time
where the time goes in v10:
time: 26.7 us; the launch traced here: 26.6 us
  starting transfers between devices  9.95 us (37%)
  Pallas kernels  8.36 us (31%)
  waiting for transfers between devices  7.45 us (28%)
  between operations  0.74 us (3%)
    ppermute x7, starting transfers between devices, swap(): lax.ppermute(value, axis, [(i, partner(i)) for i in range(size) if 0 <= p...  9.95 us
    pallas_call x7, Pallas kernels, call(): pl.pallas_call(kernel, in_specs=specs, out_specs=jax.tree.map(lambda _: p...  8.36 us
    ppermute x7, waiting for transfers between devices, swap(): lax.ppermute(value, axis, [(i, partner(i)) for i in range(size) if 0 <= p...  7.45 us
  transfers between devices with their start and end apart: 7, of which 6 were waited for; matrix products, arithmetic and copies ran while one was open for 0% of the time, Pallas kernels for 13%

profile of v10, /device:TPU:0, one launch (start us, length us, event | category | flops | bytes accessed | tf_op | source)
XLA Modules:
  0.0 26.6 jit_solution(2279278962241238692)
XLA Ops:
  0.6 0.0 copy-start
  0.6 1.6 %shard_map.212 = (f32[80,256]{1,0:T(8,128)S(1)}, f32[80,256]{1,0:T(8,128)S(1)}) custom-call(f32[1,4,64,128]{3,2,1,0:T(8,128)} %state_ref.5, bf16[4,80,128]{2,1,0:T(8,128)(2,1)} %constant.34.clone.left_ref, bf16[2,128,256]{2,1,0:T(8,128)(2,1)} %constant.35.clone.right_ref, bf16[2,16,256]{2,1,0:T(8,128)(2,1)} %constant.36.clone.edge_ref, ...), custom_call_target="tpu_custom_call" | custom-call | tf_op jit(solution)/shard_map/pallas_call | solution.py:120
  2.2 4.1 %collective-permute-start.2 = (f32[80,256]{1,0:T(8,128)S(1)}, f32[80,256]{1,0:T(8,128)S(1)}, u32[]{:S(2)}, u32[]{:S(2)}) collective-permute-start(f32[80,256]{1,0:T(8,128)S(1)} %get-tuple-element.22.own_ref), channel_id=1, source_target_pairs={{0,5},{1,4},{2,7},{3,6},{4,1},{5,0},{6,3},{7,2},{8,13},{9,12},{10,... | collective-permute-start | bytes 245768 | tf_op jit(solution)/shard_map/ppermute | solution.py:619
  6.3 0.5 %collective-permute-start = (f32[80,256]{1,0:T(8,128)S(1)}, f32[80,256]{1,0:T(8,128)S(1)}, u32[]{:S(2)}, u32[]{:S(2)}) collective-permute-start(f32[80,256]{1,0:T(8,128)S(1)} %get-tuple-element.22.own_ref), channel_id=1, source_target_pairs={{0,4},{4,0},{1,5},{5,1},{2,6},{6,2},{3,7},{7,3},{8,12},{12,8},{9,1... | collective-permute-start | bytes 245768 | tf_op jit(solution)/shard_map/ppermute | solution.py:619
  6.8 0.1 collective-permute-start.1
  6.9 1.9 %collective-permute-done.2.both_ref = f32[80,256]{1,0:T(8,128)S(1)} collective-permute-done((f32[80,256]{1,0:T(8,128)S(1)}, f32[80,256]{1,0:T(8,128)S(1)}, u32[]{:S(2)}, u32[]{:S(2)}) %collective-permute-start.2) | collective-permute-done | bytes 81952 | tf_op jit(solution)/shard_map/ppermute | solution.py:619
  8.9 1.9 %collective-permute-done.y_ref.columns_ref = f32[80,256]{1,0:T(8,128)S(1)} collective-permute-done((f32[80,256]{1,0:T(8,128)S(1)}, f32[80,256]{1,0:T(8,128)S(1)}, u32[]{:S(2)}, u32[]{:S(2)}) %collective-permute-start) | collective-permute-done | bytes 81952 | tf_op jit(solution)/shard_map/ppermute | solution.py:619
  10.7 0.5 %collective-permute-done.1.x_ref = f32[80,256]{1,0:T(8,128)S(1)} collective-permute-done((f32[80,256]{1,0:T(8,128)S(1)}, f32[80,256]{1,0:T(8,128)S(1)}, u32[]{:S(2)}, u32[]{:S(2)}) %collective-permute-start.1) | collective-permute-done | bytes 81952 | tf_op jit(solution)/shard_map/ppermute | solution.py:619
  11.2 0.0 copy-done
  11.2 0.2 shard_map.213
  11.5 3.0 %collective-permute-start.3 = (f32[80,256]{1,0:T(8,128)S(1)}, f32[80,256]{1,0:T(8,128)S(1)}, u32[]{:S(2)}, u32[]{:S(2)}) collective-permute-start(f32[80,256]{1,0:T(8,128)S(1)} %get-tuple-element.25.own_ref), channel_id=1, source_target_pairs={{0,3},{1,2},{2,1},{3,0},{4,7},{5,6},{6,5},{7,4},{8,11},{9,10},{10,... | collective-permute-start | bytes 245768 | tf_op jit(solution)/shard_map/ppermute | solution.py:619
  14.5 1.8 %shard_map.214 = (f32[3,64,256]{2,1,0:T(8,128)S(1)}, bf16[3,64,192]{2,1,0:T(8,128)(2,1)S(1)}, bf16[3,128,256]{2,1,0:T(8,128)(2,1)S(1)}, bf16[384,192]{1,0:T(8,128)(2,1)S(1)}, bf16[3,128,128]{2,1,0:T(8,128)(2,1)S(1)}) custom-call(f32[3,4,64,64]{3,2,1,0:T(8,128)} %drive_ref, f32[2,64,128]{2,1,0:T(8,128)} %constant.38.clone.maps_x_ref, ...), custom_call_target="tpu_custom_call" | custom-call | tf_op jit(solution)/shard_map/pallas_call | solution.py:120
  16.3 1.4 %collective-permute-done.3.other_ref.second_ref = f32[80,256]{1,0:T(8,128)S(1)} collective-permute-done((f32[80,256]{1,0:T(8,128)S(1)}, f32[80,256]{1,0:T(8,128)S(1)}, u32[]{:S(2)}, u32[]{:S(2)}) %collective-permute-start.3) | collective-permute-done | bytes 81952 | tf_op jit(solution)/shard_map/ppermute | solution.py:619
  17.7 0.0 copy-start.8
  17.7 1.6 %collective-permute-start.4 = (f32[80,256]{1,0:T(8,128)S(1)}, f32[80,256]{1,0:T(8,128)S(1)}, u32[]{:S(2)}, u32[]{:S(2)}) collective-permute-start(f32[80,256]{1,0:T(8,128)S(1)} %shard_map.215.refs_0_), channel_id=1, source_target_pairs={{0,16},{8,24},{16,0},{24,8},{1,17},{9,25},{17,1},{25,9},{2,18},{10... | collective-permute-start | bytes 245768 | tf_op jit(solution)/shard_map/ppermute | solution.py:619
  19.3 0.0 collective-permute-start.5
  19.3 0.6 %collective-permute-start.6 = (f32[80,256]{1,0:T(8,128)S(1)}, f32[80,256]{1,0:T(8,128)S(1)}, u32[]{:S(2)}, u32[]{:S(2)}) collective-permute-start(f32[80,256]{1,0:T(8,128)S(1)} %shard_map.215.refs_0_), channel_id=1, source_target_pairs={{0,24},{8,16},{16,8},{24,0},{1,25},{9,17},{17,9},{25,1},{2,26},{10... | collective-permute-start | bytes 245768 | tf_op jit(solution)/shard_map/ppermute | solution.py:619
  19.9 0.0 copy-done.8
  19.9 0.0 copy-start.1
  19.9 0.0 copy-start.2
  19.9 0.0 copy-start.3
  20.0 0.0 copy-start.5
  20.0 0.0 copy-start.7
  20.0 1.0 %shard_map.216.stepped_ref = f32[4,64,128]{2,1,0:T(8,128)S(1)} custom-call(f32[1,4,64,128]{3,2,1,0:T(8,128)S(1)} %copy-done, f32[80,256]{1,0:T(8,128)S(1)} %collective-permute-done.y_ref.columns_ref, f32[8,256]{1,0:T(8,128)S(1)} %get-tuple-element.34.first_ref, f32[80,256]{1,0:T(8,128)S(1)} %collective-permute-done.3.other_ref.second_ref, ...), custom_call_target="tpu_custom_call" | custom-call | tf_op jit(solution)/shard_map/pallas_call | solution.py:120
  20.9 0.0 copy-start.4
  21.0 0.0 copy-start.6
  21.0 1.3 %collective-permute-done.4.refs_1_ = f32[80,256]{1,0:T(8,128)S(1)} collective-permute-done((f32[80,256]{1,0:T(8,128)S(1)}, f32[80,256]{1,0:T(8,128)S(1)}, u32[]{:S(2)}, u32[]{:S(2)}) %collective-permute-start.4) | collective-permute-done | bytes 81952 | tf_op jit(solution)/shard_map/ppermute | solution.py:619
  22.2 0.0 collective-permute-done.5.refs_2_
  22.2 0.0 copy-done.1
  22.2 0.0 copy-done.2
  22.2 0.0 copy-done.3
  22.3 0.0 copy-done.5
  22.3 0.0 copy-done.7
  22.3 0.6 %shard_map.217.early_ref = f32[3,3,64,256]{3,2,1,0:T(8,128)S(1)} custom-call(f32[80,256]{1,0:T(8,128)S(1)} %shard_map.215.refs_0_, f32[80,256]{1,0:T(8,128)S(1)} %collective-permute-done.4.refs_1_, f32[80,256]{1,0:T(8,128)S(1)} %collective-permute-done.5.refs_2_, bf16[32,384]{1,0:T(8,128)(2,1)S(1)} %copy-done.5, bf16[256,384]{1,0:T(8,128)(2,1)S(1)} %copy-done.1, ...), custom_call_target="tpu_custom_call" | custom-call | tf_op jit(solution)/shard_map/pallas_call | solution.py:120
  22.9 0.4 %collective-permute-done.6.refs_3_ = f32[80,256]{1,0:T(8,128)S(1)} collective-permute-done((f32[80,256]{1,0:T(8,128)S(1)}, f32[80,256]{1,0:T(8,128)S(1)}, u32[]{:S(2)}, u32[]{:S(2)}) %collective-permute-start.6) | collective-permute-done | bytes 81952 | tf_op jit(solution)/shard_map/ppermute | solution.py:619
  23.3 0.0 copy-done.4
  23.3 0.0 copy-done.6
  23.4 3.2 %shard_map.218 = (f32[1,4,64,128]{3,2,1,0:T(8,128)}, f32[1,4,64,64]{3,2,1,0:T(8,128)}) custom-call(f32[4,64,128]{2,1,0:T(8,128)S(1)} %shard_map.216.stepped_ref, f32[3,64,256]{2,1,0:T(8,128)S(1)} %get-tuple-element.36.drive_ref, bf16[3,64,192]{2,1,0:T(8,128)(2,1)S(1)} %get-tuple-element.37.row_ref, bf16[3,128,256]{2,1,0:T(8,128)(2,1)S(1)} %get-tuple-element.38.col_ref, ...), custom_call_target="tpu_custom_call" | custom-call | tf_op jit(solution)/shard_map/pallas_call | solution.py:120
  (1 shorter events, 0.0 us)
Async XLA Ops:
  0.6 10.6 %copy-start = (f32[1,4,64,128]{3,2,1,0:T(8,128)S(1)}, f32[1,4,64,128]{3,2,1,0:T(8,128)}, u32[]{:S(2)}) copy-start(f32[1,4,64,128]{3,2,1,0:T(8,128)} %state_ref.5) | copy-start | bytes 393220
  2.2 6.7 %collective-permute-start.2 = (f32[80,256]{1,0:T(8,128)S(1)}, f32[80,256]{1,0:T(8,128)S(1)}, u32[]{:S(2)}, u32[]{:S(2)}) collective-permute-start(f32[80,256]{1,0:T(8,128)S(1)} %get-tuple-element.22.own_ref), channel_id=1, source_target_pairs={{0,5},{1,4},{2,7},{3,6},{4,1},{5,0},{6,3},{7,2},{8,13},{9,12},{10,... | collective-permute-start | bytes 245768 | tf_op jit(solution)/shard_map/ppermute | solution.py:619
  6.3 4.4 %collective-permute-start = (f32[80,256]{1,0:T(8,128)S(1)}, f32[80,256]{1,0:T(8,128)S(1)}, u32[]{:S(2)}, u32[]{:S(2)}) collective-permute-start(f32[80,256]{1,0:T(8,128)S(1)} %get-tuple-element.22.own_ref), channel_id=1, source_target_pairs={{0,4},{4,0},{1,5},{5,1},{2,6},{6,2},{3,7},{7,3},{8,12},{12,8},{9,1... | collective-permute-start | bytes 245768 | tf_op jit(solution)/shard_map/ppermute | solution.py:619
  6.8 4.4 %collective-permute-start.1 = (f32[80,256]{1,0:T(8,128)S(1)}, f32[80,256]{1,0:T(8,128)S(1)}, u32[]{:S(2)}, u32[]{:S(2)}) collective-permute-start(f32[80,256]{1,0:T(8,128)S(1)} %get-tuple-element.23), channel_id=1, source_target_pairs={{0,1},{1,0},{2,3},{3,2},{4,5},{5,4},{6,7},{7,6},{8,9},{9,8},{10,11... | collective-permute-start | bytes 245768 | tf_op jit(solution)/shard_map/ppermute | solution.py:619
  11.5 6.3 %collective-permute-start.3 = (f32[80,256]{1,0:T(8,128)S(1)}, f32[80,256]{1,0:T(8,128)S(1)}, u32[]{:S(2)}, u32[]{:S(2)}) collective-permute-start(f32[80,256]{1,0:T(8,128)S(1)} %get-tuple-element.25.own_ref), channel_id=1, source_target_pairs={{0,3},{1,2},{2,1},{3,0},{4,7},{5,6},{6,5},{7,4},{8,11},{9,10},{10,... | collective-permute-start | bytes 245768 | tf_op jit(solution)/shard_map/ppermute | solution.py:619
  17.7 2.2 %copy-start.8 = (bf16[32,128]{1,0:T(8,128)(2,1)S(1)}, bf16[32,128]{1,0:T(8,128)(2,1)}, u32[]{:S(2)}) copy-start(bf16[32,128]{1,0:T(8,128)(2,1)} %constant.42.clone.place_ref) | copy-start | bytes 24580
  17.7 4.5 %collective-permute-start.4 = (f32[80,256]{1,0:T(8,128)S(1)}, f32[80,256]{1,0:T(8,128)S(1)}, u32[]{:S(2)}, u32[]{:S(2)}) collective-permute-start(f32[80,256]{1,0:T(8,128)S(1)} %shard_map.215.refs_0_), channel_id=1, source_target_pairs={{0,16},{8,24},{16,0},{24,8},{1,17},{9,25},{17,1},{25,9},{2,18},{10... | collective-permute-start | bytes 245768 | tf_op jit(solution)/shard_map/ppermute | solution.py:619
  19.3 3.0 %collective-permute-start.5 = (f32[80,256]{1,0:T(8,128)S(1)}, f32[80,256]{1,0:T(8,128)S(1)}, u32[]{:S(2)}, u32[]{:S(2)}) collective-permute-start(f32[80,256]{1,0:T(8,128)S(1)} %shard_map.215.refs_0_), channel_id=1, source_target_pairs={{0,8},{8,0},{16,24},{24,16},{1,9},{9,1},{17,25},{25,17},{2,10},{10... | collective-permute-start | bytes 245768 | tf_op jit(solution)/shard_map/ppermute | solution.py:619
  19.3 4.1 %collective-permute-start.6 = (f32[80,256]{1,0:T(8,128)S(1)}, f32[80,256]{1,0:T(8,128)S(1)}, u32[]{:S(2)}, u32[]{:S(2)}) collective-permute-start(f32[80,256]{1,0:T(8,128)S(1)} %shard_map.215.refs_0_), channel_id=1, source_target_pairs={{0,24},{8,16},{16,8},{24,0},{1,25},{9,17},{17,9},{25,1},{2,26},{10... | collective-permute-start | bytes 245768 | tf_op jit(solution)/shard_map/ppermute | solution.py:619
  19.9 2.3 %copy-start.1 = (bf16[256,384]{1,0:T(8,128)(2,1)S(1)}, bf16[256,384]{1,0:T(8,128)(2,1)}, u32[]{:S(2)}) copy-start(bf16[256,384]{1,0:T(8,128)(2,1)} %constant.44.clone.refs_4_.refs_5_) | copy-start | bytes 589828
  19.9 2.3 %copy-start.2 = (f32[64,256]{1,0:T(8,128)S(1)}, f32[64,256]{1,0:T(8,128)}, u32[]{:S(2)}) copy-start(f32[64,256]{1,0:T(8,128)} %constant.46.clone.refs_6_.refs_7_) | copy-start | bytes 196612
  19.9 2.3 %copy-start.3 = (bf16[192,96]{1,0:T(8,128)(2,1)S(1)}, bf16[192,96]{1,0:T(8,128)(2,1)}, u32[]{:S(2)}) copy-start(bf16[192,96]{1,0:T(8,128)(2,1)} %constant.45.clone.refs_5_.refs_6_) | copy-start | bytes 110596
  20.0 2.3 %copy-start.5 = (bf16[32,384]{1,0:T(8,128)(2,1)S(1)}, bf16[32,384]{1,0:T(8,128)(2,1)}, u32[]{:S(2)}) copy-start(bf16[32,384]{1,0:T(8,128)(2,1)} %constant.43.clone.refs_3_.refs_4_) | copy-start | bytes 73732
  20.0 2.3 %copy-start.7 = (f32[8,256]{1,0:T(8,128)S(1)}, f32[8,256]{1,0:T(8,128)}, u32[]{:S(2)}) copy-start(f32[8,256]{1,0:T(8,128)} %constant.47.clone.refs_7_.refs_8_) | copy-start | bytes 24580
  20.9 2.4 %copy-start.4 = (bf16[2,128,256]{2,1,0:T(8,128)(2,1)S(1)}, bf16[2,128,256]{2,1,0:T(8,128)(2,1)}, u32[]{:S(2)}) copy-start(bf16[2,128,256]{2,1,0:T(8,128)(2,1)} %constant.55.sideways_ref) | copy-start | bytes 393220
  21.0 2.4 %copy-start.6 = (bf16[128,192]{1,0:T(8,128)(2,1)S(1)}, bf16[128,192]{1,0:T(8,128)(2,1)}, u32[]{:S(2)}) copy-start(bf16[128,192]{1,0:T(8,128)(2,1)} %constant.48.clone.again_ref) | copy-start | bytes 147460

commit v11 on v8

--- a/solution.py
+++ b/solution.py
@@ -112,13 +112,17 @@
     return value if INTERPRET else pltpu.with_memory_space_constraint(value, pltpu.VMEM)
 
 
-def call(kernel, shapes, *args, first=False, final=False):
+def call(kernel, shapes, *args, first=False, final=False, split=0):
     scalars = [a.ndim == 2 and a.size <= 16 for a in args]
     specs = [pl.BlockSpec(memory_space=pltpu.SMEM if s else pltpu.VMEM) for s in scalars]
+    for i in range(split):
+        block = (1, 1) + args[i].shape[2:]
+        specs[i] = pl.BlockSpec(block, lambda _, i=i: (0, i, 0, 0), memory_space=pltpu.VMEM)
     if not final and not INTERPRET:
         shapes = jax.tree.map(lambda s: pltpu.VMEM(s.shape, s.dtype), shapes)
     return pl.pallas_call(
         kernel,
+        grid=(1,) if split else (),
         in_specs=specs,
         out_specs=jax.tree.map(lambda _: pl.BlockSpec(memory_space=pltpu.VMEM), shapes),
         out_shape=shapes,
@@ -153,6 +157,14 @@
     def unpairs(self, value):
         rows = value.shape[0] // self.half
         return jnp.concatenate([value[i * rows : (i + 1) * rows] for i in range(self.half)], 1)
+
+
+class Levels:
+    def __init__(self, refs):
+        self.refs = refs
+
+    def __getitem__(self, at):
+        return self.refs[at[1]][0, 0]
 
 
 def project(plan, state, rates, halved):
@@ -173,7 +185,9 @@
         pick[i, [i, ny + i]] = 1
         pick[windows + i, [ny - windows + i, 2 * ny - windows + i]] = 1
 
-    def kernel(state_ref, left_ref, right_ref, edge_ref, pick_ref, rates_ref, out_ref, along_ref):
+    def kernel(*refs):
+        state_ref = Levels(refs[:levels])
+        left_ref, right_ref, edge_ref, pick_ref, rates_ref, out_ref, along_ref = refs[levels:]
         px, py = lax.axis_index("px"), lax.axis_index("py")
         field = jnp.concatenate([state_ref[0, level] for level in range(levels)], 1)
         high, small = halves(field)
@@ -222,9 +236,10 @@
     return call(
         kernel,
         (shape_of(plan.rows, lanes), shape_of(plan.rows if halved else EDGE, lanes)),
-        state, left, jnp.asarray(np.stack(right)), jnp.asarray(np.stack(edge)),
+        *[state] * levels, left, jnp.asarray(np.stack(right)), jnp.asarray(np.stack(edge)),
         jnp.asarray(bf16(pick)), rates,
         first=True,
+        split=levels,
     )
 
 

time: 26.9 us -> 26.9 us (level)
  no operation moved by 1% of the time
where the time goes in v11:
time: 26.9 us; the launch traced here: 26.7 us
  starting transfers between devices  9.31 us (35%)
  Pallas kernels  8.4 us (31%)
  waiting for transfers between devices  7.55 us (28%)
  between operations  0.78 us (3%)
  local copies, waits for them, and re-layouts  0.71 us (3%)
    ppermute x7, starting transfers between devices, swap(): lax.ppermute(value, axis, [(i, partner(i)) for i in range(size) if 0 <= p...  9.31 us
    pallas_call x7, Pallas kernels, call(): pl.pallas_call(kernel, grid=(1,) if split else (), in_specs=specs, out_sp...  8.4 us
    ppermute x7, waiting for transfers between devices, swap(): lax.ppermute(value, axis, [(i, partner(i)) for i in range(size) if 0 <= p...  7.55 us
    unnamed x22, local copies, waits for them, and re-layouts  0.71 us
  transfers between devices with their start and end apart: 7, of which 6 were waited for; matrix products, arithmetic and copies ran while one was open for 0% of the time, Pallas kernels for 13%

profile of v11, /device:TPU:0, one launch (start us, length us, event | category | flops | bytes accessed | tf_op | source)
XLA Modules:
  0.0 26.7 jit_solution(11339941979685204303)
XLA Ops:
  0.6 0.0 copy-start
  0.6 1.6 %shard_map.212 = (f32[80,256]{1,0:T(8,128)S(1)}, f32[80,256]{1,0:T(8,128)S(1)}) custom-call(f32[1,4,64,128]{3,2,1,0:T(8,128)} %state_ref.3, f32[1,4,64,128]{3,2,1,0:T(8,128)} %state_ref.3, f32[1,4,64,128]{3,2,1,0:T(8,128)} %state_ref.3, f32[1,4,64,128]{3,2,1,0:T(8,128)} %state_ref.3, bf16[4,80,128]{2,1,0:T(8,128)(2,1)} %constant.34.clone.refs_4_, ...), custom_call_target="tpu_custom_call" | custom-call | tf_op jit(solution)/shard_map/pallas_call | solution.py:123
  2.2 4.1 %collective-permute-start.2 = (f32[80,256]{1,0:T(8,128)S(1)}, f32[80,256]{1,0:T(8,128)S(1)}, u32[]{:S(2)}, u32[]{:S(2)}) collective-permute-start(f32[80,256]{1,0:T(8,128)S(1)} %get-tuple-element.22.own_ref), channel_id=1, source_target_pairs={{0,5},{1,4},{2,7},{3,6},{4,1},{5,0},{6,3},{7,2},{8,13},{9,12},{10,... | collective-permute-start | bytes 245768 | tf_op jit(solution)/shard_map/ppermute | solution.py:636
  6.3 0.5 %collective-permute-start = (f32[80,256]{1,0:T(8,128)S(1)}, f32[80,256]{1,0:T(8,128)S(1)}, u32[]{:S(2)}, u32[]{:S(2)}) collective-permute-start(f32[80,256]{1,0:T(8,128)S(1)} %get-tuple-element.22.own_ref), channel_id=1, source_target_pairs={{0,4},{4,0},{1,5},{5,1},{2,6},{6,2},{3,7},{7,3},{8,12},{12,8},{9,1... | collective-permute-start | bytes 245768 | tf_op jit(solution)/shard_map/ppermute | solution.py:636
  6.8 0.1 collective-permute-start.1
  6.9 1.9 %collective-permute-done.2.both_ref = f32[80,256]{1,0:T(8,128)S(1)} collective-permute-done((f32[80,256]{1,0:T(8,128)S(1)}, f32[80,256]{1,0:T(8,128)S(1)}, u32[]{:S(2)}, u32[]{:S(2)}) %collective-permute-start.2) | collective-permute-done | bytes 81952 | tf_op jit(solution)/shard_map/ppermute | solution.py:636
  8.9 1.9 %collective-permute-done.y_ref.columns_ref = f32[80,256]{1,0:T(8,128)S(1)} collective-permute-done((f32[80,256]{1,0:T(8,128)S(1)}, f32[80,256]{1,0:T(8,128)S(1)}, u32[]{:S(2)}, u32[]{:S(2)}) %collective-permute-start) | collective-permute-done | bytes 81952 | tf_op jit(solution)/shard_map/ppermute | solution.py:636
  10.7 0.5 %collective-permute-done.1.x_ref = f32[80,256]{1,0:T(8,128)S(1)} collective-permute-done((f32[80,256]{1,0:T(8,128)S(1)}, f32[80,256]{1,0:T(8,128)S(1)}, u32[]{:S(2)}, u32[]{:S(2)}) %collective-permute-start.1) | collective-permute-done | bytes 81952 | tf_op jit(solution)/shard_map/ppermute | solution.py:636
  11.2 0.0 copy-done
  11.2 0.2 shard_map.213
  11.5 3.0 %collective-permute-start.3 = (f32[80,256]{1,0:T(8,128)S(1)}, f32[80,256]{1,0:T(8,128)S(1)}, u32[]{:S(2)}, u32[]{:S(2)}) collective-permute-start(f32[80,256]{1,0:T(8,128)S(1)} %get-tuple-element.25.own_ref), channel_id=1, source_target_pairs={{0,3},{1,2},{2,1},{3,0},{4,7},{5,6},{6,5},{7,4},{8,11},{9,10},{10,... | collective-permute-start | bytes 245768 | tf_op jit(solution)/shard_map/ppermute | solution.py:636
  14.5 1.8 %shard_map.214 = (f32[3,64,256]{2,1,0:T(8,128)S(1)}, bf16[3,64,192]{2,1,0:T(8,128)(2,1)S(1)}, bf16[3,128,256]{2,1,0:T(8,128)(2,1)S(1)}, bf16[384,192]{1,0:T(8,128)(2,1)S(1)}, bf16[3,256,256]{2,1,0:T(8,128)(2,1)S(1)}) custom-call(f32[3,4,64,64]{3,2,1,0:T(8,128)} %drive_ref, f32[2,64,128]{2,1,0:T(8,128)} %constant.38.clone.maps_x_ref, ...), custom_call_target="tpu_custom_call" | custom-call | tf_op jit(solution)/shard_map/pallas_call | solution.py:123
  16.3 0.0 copy-start.3
  16.3 0.7 %copy-done.3 = bf16[3,128,256]{2,1,0:T(8,128)(2,1)} copy-done((bf16[3,128,256]{2,1,0:T(8,128)(2,1)}, bf16[3,128,256]{2,1,0:T(8,128)(2,1)S(1)}, u32[]{:S(2)}) %copy-start.3) | copy-done | bytes 196632
  17.0 0.8 %collective-permute-done.3.other_ref.second_ref = f32[80,256]{1,0:T(8,128)S(1)} collective-permute-done((f32[80,256]{1,0:T(8,128)S(1)}, f32[80,256]{1,0:T(8,128)S(1)}, u32[]{:S(2)}, u32[]{:S(2)}) %collective-permute-start.3) | collective-permute-done | bytes 81952 | tf_op jit(solution)/shard_map/ppermute | solution.py:636
  17.7 0.0 copy-start.10
  17.7 1.6 %collective-permute-start.4 = (f32[80,256]{1,0:T(8,128)S(1)}, f32[80,256]{1,0:T(8,128)S(1)}, u32[]{:S(2)}, u32[]{:S(2)}) collective-permute-start(f32[80,256]{1,0:T(8,128)S(1)} %shard_map.215.refs_0_), channel_id=1, source_target_pairs={{0,16},{8,24},{16,0},{24,8},{1,17},{9,25},{17,1},{25,9},{2,18},{10... | collective-permute-start | bytes 245768 | tf_op jit(solution)/shard_map/ppermute | solution.py:636
  19.3 0.0 collective-permute-start.5
  19.3 0.0 copy-done.10
  19.3 0.0 copy-start.1
  19.3 0.0 copy-start.2
  19.3 0.0 copy-start.5
  19.3 0.0 copy-start.7
  19.3 0.0 copy-start.9
  19.3 1.0 %shard_map.216.stepped_ref = f32[4,64,128]{2,1,0:T(8,128)S(1)} custom-call(f32[1,4,64,128]{3,2,1,0:T(8,128)S(1)} %copy-done, f32[80,256]{1,0:T(8,128)S(1)} %collective-permute-done.y_ref.columns_ref, f32[8,256]{1,0:T(8,128)S(1)} %get-tuple-element.34.first_ref, f32[80,256]{1,0:T(8,128)S(1)} %collective-permute-done.3.other_ref.second_ref, ...), custom_call_target="tpu_custom_call" | custom-call | tf_op jit(solution)/shard_map/pallas_call | solution.py:123
  20.3 0.0 copy-start.4
  20.3 0.0 copy-start.6
  20.3 0.0 copy-start.8
  20.3 1.9 %collective-permute-done.4.refs_1_ = f32[80,256]{1,0:T(8,128)S(1)} collective-permute-done((f32[80,256]{1,0:T(8,128)S(1)}, f32[80,256]{1,0:T(8,128)S(1)}, u32[]{:S(2)}, u32[]{:S(2)}) %collective-permute-start.4) | collective-permute-done | bytes 81952 | tf_op jit(solution)/shard_map/ppermute | solution.py:636
  22.2 0.0 collective-permute-start.6
  22.2 0.0 collective-permute-done.5.refs_2_
  22.2 0.0 copy-done.1
  22.3 0.0 copy-done.2
  22.3 0.0 copy-done.5
  22.3 0.0 copy-done.7
  22.3 0.0 copy-done.9
  22.3 0.6 %shard_map.217.early_ref = f32[3,3,64,256]{3,2,1,0:T(8,128)S(1)} custom-call(f32[80,256]{1,0:T(8,128)S(1)} %shard_map.215.refs_0_, f32[80,256]{1,0:T(8,128)S(1)} %collective-permute-done.4.refs_1_, f32[80,256]{1,0:T(8,128)S(1)} %collective-permute-done.5.refs_2_, bf16[32,384]{1,0:T(8,128)(2,1)S(1)} %copy-done.7, bf16[256,384]{1,0:T(8,128)(2,1)S(1)} %copy-done.1, ...), custom_call_target="tpu_custom_call" | custom-call | tf_op jit(solution)/shard_map/pallas_call | solution.py:123
  22.9 0.6 %collective-permute-done.6.refs_3_ = f32[80,256]{1,0:T(8,128)S(1)} collective-permute-done((f32[80,256]{1,0:T(8,128)S(1)}, f32[80,256]{1,0:T(8,128)S(1)}, u32[]{:S(2)}, u32[]{:S(2)}) %collective-permute-start.6) | collective-permute-done | bytes 81952 | tf_op jit(solution)/shard_map/ppermute | solution.py:636
  23.5 0.0 copy-done.4
  23.5 0.0 copy-done.6
  23.5 0.0 copy-done.8
  23.5 3.2 %shard_map.218 = (f32[1,4,64,128]{3,2,1,0:T(8,128)}, f32[1,4,64,64]{3,2,1,0:T(8,128)}) custom-call(f32[4,64,128]{2,1,0:T(8,128)S(1)} %shard_map.216.stepped_ref, f32[3,64,256]{2,1,0:T(8,128)S(1)} %get-tuple-element.36.drive_ref, bf16[3,64,192]{2,1,0:T(8,128)(2,1)S(1)} %get-tuple-element.37.row_ref, bf16[3,128,256]{2,1,0:T(8,128)(2,1)S(1)} %copy-done.4, ...), custom_call_target="tpu_custom_call" | custom-call | tf_op jit(solution)/shard_map/pallas_call | solution.py:123
  (1 shorter events, 0.0 us)
Async XLA Ops:
  0.6 10.6 %copy-start = (f32[1,4,64,128]{3,2,1,0:T(8,128)S(1)}, f32[1,4,64,128]{3,2,1,0:T(8,128)}, u32[]{:S(2)}) copy-start(f32[1,4,64,128]{3,2,1,0:T(8,128)} %state_ref.3) | copy-start | bytes 393220
  2.2 6.7 %collective-permute-start.2 = (f32[80,256]{1,0:T(8,128)S(1)}, f32[80,256]{1,0:T(8,128)S(1)}, u32[]{:S(2)}, u32[]{:S(2)}) collective-permute-start(f32[80,256]{1,0:T(8,128)S(1)} %get-tuple-element.22.own_ref), channel_id=1, source_target_pairs={{0,5},{1,4},{2,7},{3,6},{4,1},{5,0},{6,3},{7,2},{8,13},{9,12},{10,... | collective-permute-start | bytes 245768 | tf_op jit(solution)/shard_map/ppermute | solution.py:636
  6.3 4.4 %collective-permute-start = (f32[80,256]{1,0:T(8,128)S(1)}, f32[80,256]{1,0:T(8,128)S(1)}, u32[]{:S(2)}, u32[]{:S(2)}) collective-permute-start(f32[80,256]{1,0:T(8,128)S(1)} %get-tuple-element.22.own_ref), channel_id=1, source_target_pairs={{0,4},{4,0},{1,5},{5,1},{2,6},{6,2},{3,7},{7,3},{8,12},{12,8},{9,1... | collective-permute-start | bytes 245768 | tf_op jit(solution)/shard_map/ppermute | solution.py:636
  6.8 4.4 %collective-permute-start.1 = (f32[80,256]{1,0:T(8,128)S(1)}, f32[80,256]{1,0:T(8,128)S(1)}, u32[]{:S(2)}, u32[]{:S(2)}) collective-permute-start(f32[80,256]{1,0:T(8,128)S(1)} %get-tuple-element.23), channel_id=1, source_target_pairs={{0,1},{1,0},{2,3},{3,2},{4,5},{5,4},{6,7},{7,6},{8,9},{9,8},{10,11... | collective-permute-start | bytes 245768 | tf_op jit(solution)/shard_map/ppermute | solution.py:636
  11.5 6.3 %collective-permute-start.3 = (f32[80,256]{1,0:T(8,128)S(1)}, f32[80,256]{1,0:T(8,128)S(1)}, u32[]{:S(2)}, u32[]{:S(2)}) collective-permute-start(f32[80,256]{1,0:T(8,128)S(1)} %get-tuple-element.25.own_ref), channel_id=1, source_target_pairs={{0,3},{1,2},{2,1},{3,0},{4,7},{5,6},{6,5},{7,4},{8,11},{9,10},{10,... | collective-permute-start | bytes 245768 | tf_op jit(solution)/shard_map/ppermute | solution.py:636
  16.3 0.7 %copy-start.3 = (bf16[3,128,256]{2,1,0:T(8,128)(2,1)}, bf16[3,128,256]{2,1,0:T(8,128)(2,1)S(1)}, u32[]{:S(2)}) copy-start(bf16[3,128,256]{2,1,0:T(8,128)(2,1)S(1)} %get-tuple-element.38.col_ref) | copy-start | bytes 589828
  17.7 1.6 %copy-start.10 = (bf16[32,128]{1,0:T(8,128)(2,1)S(1)}, bf16[32,128]{1,0:T(8,128)(2,1)}, u32[]{:S(2)}) copy-start(bf16[32,128]{1,0:T(8,128)(2,1)} %constant.42.clone.place_ref) | copy-start | bytes 24580
  17.7 4.5 %collective-permute-start.4 = (f32[80,256]{1,0:T(8,128)S(1)}, f32[80,256]{1,0:T(8,128)S(1)}, u32[]{:S(2)}, u32[]{:S(2)}) collective-permute-start(f32[80,256]{1,0:T(8,128)S(1)} %shard_map.215.refs_0_), channel_id=1, source_target_pairs={{0,16},{8,24},{16,0},{24,8},{1,17},{9,25},{17,1},{25,9},{2,18},{10... | collective-permute-start | bytes 245768 | tf_op jit(solution)/shard_map/ppermute | solution.py:636
  19.3 3.0 %collective-permute-start.5 = (f32[80,256]{1,0:T(8,128)S(1)}, f32[80,256]{1,0:T(8,128)S(1)}, u32[]{:S(2)}, u32[]{:S(2)}) collective-permute-start(f32[80,256]{1,0:T(8,128)S(1)} %shard_map.215.refs_0_), channel_id=1, source_target_pairs={{0,8},{8,0},{16,24},{24,16},{1,9},{9,1},{17,25},{25,17},{2,10},{10... | collective-permute-start | bytes 245768 | tf_op jit(solution)/shard_map/ppermute | solution.py:636
  19.3 3.0 %copy-start.1 = (bf16[256,384]{1,0:T(8,128)(2,1)S(1)}, bf16[256,384]{1,0:T(8,128)(2,1)}, u32[]{:S(2)}) copy-start(bf16[256,384]{1,0:T(8,128)(2,1)} %constant.44.clone.refs_4_.refs_5_) | copy-start | bytes 589828
  19.3 3.0 %copy-start.2 = (f32[64,256]{1,0:T(8,128)S(1)}, f32[64,256]{1,0:T(8,128)}, u32[]{:S(2)}) copy-start(f32[64,256]{1,0:T(8,128)} %constant.46.clone.refs_6_.refs_7_) | copy-start | bytes 196612
  19.3 3.0 %copy-start.5 = (bf16[192,96]{1,0:T(8,128)(2,1)S(1)}, bf16[192,96]{1,0:T(8,128)(2,1)}, u32[]{:S(2)}) copy-start(bf16[192,96]{1,0:T(8,128)(2,1)} %constant.45.clone.refs_5_.refs_6_) | copy-start | bytes 110596
  19.3 3.0 %copy-start.7 = (bf16[32,384]{1,0:T(8,128)(2,1)S(1)}, bf16[32,384]{1,0:T(8,128)(2,1)}, u32[]{:S(2)}) copy-start(bf16[32,384]{1,0:T(8,128)(2,1)} %constant.43.clone.refs_3_.refs_4_) | copy-start | bytes 73732
  19.3 3.0 %copy-start.9 = (f32[8,256]{1,0:T(8,128)S(1)}, f32[8,256]{1,0:T(8,128)}, u32[]{:S(2)}) copy-start(f32[8,256]{1,0:T(8,128)} %constant.47.clone.refs_7_.refs_8_) | copy-start | bytes 24580
  20.3 3.2 %copy-start.4 = (bf16[3,128,256]{2,1,0:T(8,128)(2,1)S(1)}, bf16[3,128,256]{2,1,0:T(8,128)(2,1)}, u32[]{:S(2)}) copy-start(bf16[3,128,256]{2,1,0:T(8,128)(2,1)} %copy-done.3) | copy-start | bytes 589828
  20.3 3.2 %copy-start.6 = (bf16[2,128,256]{2,1,0:T(8,128)(2,1)S(1)}, bf16[2,128,256]{2,1,0:T(8,128)(2,1)}, u32[]{:S(2)}) copy-start(bf16[2,128,256]{2,1,0:T(8,128)(2,1)} %constant.55.sideways_ref) | copy-start | bytes 393220
  20.3 3.2 %copy-start.8 = (bf16[128,192]{1,0:T(8,128)(2,1)S(1)}, bf16[128,192]{1,0:T(8,128)(2,1)}, u32[]{:S(2)}) copy-start(bf16[128,192]{1,0:T(8,128)(2,1)} %constant.48.clone.again_ref) | copy-start | bytes 147460
  22.2 1.3 %collective-permute-start.6 = (f32[80,256]{1,0:T(8,128)S(1)}, f32[80,256]{1,0:T(8,128)S(1)}, u32[]{:S(2)}, u32[]{:S(2)}) collective-permute-start(f32[80,256]{1,0:T(8,128)S(1)} %collective-permute-done.4.refs_1_), channel_id=1, source_target_pairs={{0,8},{8,0},{16,24},{24,16},{1,9},{9,1},{17,25},{25,17},{2,10},{10... | collective-permute-start | bytes 245768 | tf_op jit(solution)/shard_map/ppermute | solution.py:636
